TPU v7x, 8 devices: a whole 2x2x1 slice. The times are simulated.
8 devices in a mesh: dp: 1 (over z), tp: 8 (over y, x, core).
Axes of the slice: x: 2, y: 2, z: 1, core: 2. Of those that a mesh axis runs over, the one named last changes fastest.
Arguments:
- hidden: bfloat16 [4096, 4096], P(('dp', 'tp'))
- w_head: bfloat16 [4096, 32768], P(None, 'tp')
- labels: int32 [4096], P(('dp', 'tp'))
Outputs:
- output 1: float32 [1], P('dp')
- output 2: bfloat16 [4096, 4096], P(('dp', 'tp'))
- output 3: bfloat16 [4096, 32768], P('dp', 'tp')
All inputs are finite; a program needn't handle non-finite values.
Results may differ from a plain program's by a relative error of at most 0.001.
Values are sent between devices in bfloat16 or wider.
A program may use at most 1 GiB of HBM per device.

v0:
```python
import jax
import jax.numpy as jnp
from jax import lax
from jax.sharding import PartitionSpec as P


def solution(mesh):
    group_size = mesh.shape["tp"]

    def local_step(hid_loc, w_loc, lab_loc):
        inv_tokens = 1.0 / (hid_loc.shape[0] * group_size)
        vocab_loc = w_loc.shape[1]
        hid_all = lax.all_gather(hid_loc, "tp", axis=0, tiled=True)
        lab_all = lax.all_gather(lab_loc, "tp", axis=0, tiled=True)
        logits = jnp.dot(hid_all, w_loc, preferred_element_type=jnp.float32)
        glob_max = lax.pmax(jnp.max(logits, axis=1), "tp")
        shifted = jnp.exp(logits - glob_max[:, None])
        local_ids = lab_all - lax.axis_index("tp") * vocab_loc
        is_label = jnp.arange(vocab_loc, dtype=jnp.int32) == local_ids[:, None]
        local_stats = jnp.stack([jnp.sum(shifted, axis=1), jnp.sum(jnp.where(is_label, logits, 0.0), axis=1)])
        stat_sums = lax.psum(local_stats, "tp")
        row_sum = stat_sums[0]
        token_loss = glob_max + jnp.log(row_sum) - stat_sums[1]
        mean_loss = (jnp.sum(token_loss) * inv_tokens).reshape(1)
        prob_rows = shifted / row_sum[:, None]
        grad_out = (jnp.where(is_label, prob_rows - 1.0, prob_rows) * inv_tokens).astype(jnp.bfloat16)
        d_head = lax.dot_general(hid_all, grad_out, (((0,), (0,)), ((), ())), preferred_element_type=jnp.float32)
        dx_part = lax.dot_general(grad_out, w_loc, (((1,), (1,)), ((), ())), preferred_element_type=jnp.float32)
        d_hidden = lax.psum_scatter(dx_part, "tp", scatter_dimension=0, tiled=True)
        return mean_loss, d_hidden.astype(jnp.bfloat16), d_head.astype(jnp.bfloat16)

    return jax.shard_map(
        local_step,
        mesh=mesh,
        in_specs=(P(("dp", "tp"), None), P(None, "tp"), P(("dp", "tp"))),
        out_specs=(P("dp"), P(("dp", "tp"), None), P("dp", "tp")),
        check_vma=False,
    )
```

profile of v0, /device:TPU:0, one launch (start us, length us, event | category | flops | bytes accessed | tf_op | source)
XLA Modules:
  0.0 964.8 jit_solution(2059479417738748587)
XLA Ops:
  7.2 0.0 all-gather.3.cloned.1.call-start
  7.2 0.7 all-gather.3.cloned.1.call-update
  7.9 0.0 reduce-scatter.2.cloned.1.call-start
  7.9 13.6 %all-gather = s32[8,1,512]{2,1,0:T(1,128)S(1)} all-gather(s32[1,1,512]{2,1,0:T(1,128)} %bitcast.25), channel_id=1, replica_groups=mesh['dp'=1,'tp'=8] {'tp'}, dimensions={0}, use_global_device_ids=true | all-gather | bytes 18432 | tf_op jit(solution)/shard_map/all_gather | solution.py:14
  21.5 0.6 broadcast_subtract_fusion
  22.1 145.7 %all-gather.3.cloned.1.call-done = bf16[4096,4096]{1,0:T(8,128)(2,1)} async-done(((bf16[512,4096]{1,0:T(8,128)(2,1)}), bf16[4096,4096]{1,0:T(8,128)(2,1)}) %all-gather.3.cloned.1.call-update) | async-done | bytes 33554448 | tf_op jit(solution)/shard_map/all_gather | solution.py:13
  167.9 0.0 copy-start.2
  167.9 154.6 %fusion.4 = (f32[4096]{0:T(1024)S(1)}, f32[4096,4096]{0,1:T(8,128)}) fusion(bf16[4096,4096]{1,0:T(8,128)(2,1)} %all-gather.3.cloned.1.call-done, bf16[4096,4096]{1,0:T(8,128)(2,1)} %param.4), kind=kOutput, calls=%fused_computation.12 | convolution fusion | flops 137455730688 | bytes 134234112 | tf_op jit(solution)/shard_map/dot_general | solution.py:15
  322.5 22.3 %pmax.7 = f32[4096]{0:T(1024)S(1)} all-reduce(f32[4096]{0:T(1024)S(1)} %get-tuple-element.13), channel_id=1, replica_groups=mesh['dp'=1,'tp'=8] {'tp'}, use_global_device_ids=true, to_apply=%region_1.0 | all-reduce | flops 4096 | bytes 32768 | tf_op jit(solution)/shard_map/pmax | solution.py:16
  344.8 0.0 copy-start
  344.8 0.0 copy-done.2
  344.8 21.7 %fusion.2 = (f32[4096]{0:T(1024)S(1)}, f32[4096]{0:T(1024)S(1)}) fusion(f32[4096,4096]{0,1:T(8,128)} %get-tuple-element.14, f32[4096]{0:T(1024)S(1)} %pmax.7, s32[4096]{0:T(1024)S(1)} %bitcast.17), kind=kLoop, calls=%fused_computation.6 | loop fusion | flops 83877888 | bytes 67174400 | tf_op jit(solution)/shard_map/reduce_sum | solution.py:20
  366.6 24.3 %psum.7 = f32[2,4096]{1,0:T(2,128)S(1)} all-reduce(f32[2,4096]{1,0:T(2,128)S(1)} %pad_maximum_fusion), channel_id=1, replica_groups=mesh['dp'=1,'tp'=8] {'tp'}, use_global_device_ids=true, to_apply=%region_4.5 | all-reduce | flops 8192 | bytes 65536 | tf_op jit(solution)/shard_map/psum | solution.py:21
  390.9 0.6 fusion.3
  391.5 0.0 copy-start.3
  391.5 0.0 copy-done
  391.5 33.8 %fusion.1 = bf16[4096,4096]{0,1:T(8,128)(2,1)} fusion(f32[4096,4096]{0,1:T(8,128)} %get-tuple-element.14, f32[4096]{0:T(1024)S(1)} %bitcast.19, s32[4096]{0:T(1024)S(1)} %bitcast.18, f32[4096]{0:T(1024)S(1)} %pmax.7), kind=kLoop, calls=%fused_computation.2 | loop fusion | flops 117440512 | bytes 100712448 | tf_op jit(solution)/shard_map/convert_element_type | solution.py:26
  425.4 0.0 copy-done.3
  425.4 149.7 %fusion.5 = f32[4096,4096]{1,0:T(8,128)} fusion(bf16[4096,4096]{0,1:T(8,128)(2,1)} %fusion.1, bf16[4096,4096]{1,0:T(8,128)(2,1)} %param.4), kind=kOutput, calls=%fused_computation.13 | convolution fusion | flops 137438953472 | bytes 134217728 | tf_op jit(solution)/shard_map/dot_general | solution.py:28
  575.1 0.0 reduce-scatter.2.cloned.1.call-update
  575.1 150.5 %convert_bitcast_fusion = bf16[4096,4096]{0,1:T(8,128)(2,1)} fusion(bf16[4096,4096]{0,1:T(8,128)(2,1)} %fusion.1, bf16[4096,4096]{1,0:T(8,128)(2,1)} %all-gather.3.cloned.1.call-done), kind=kOutput, calls=%fused_computation.7 | convolution fusion | flops 137455730688 | bytes 100663296 | tf_op jit(solution)/shard_map/dot_general | solution.py:27
  725.6 0.0 copy-start.1
  725.6 0.0 copy-start.4
  725.6 0.0 copy-start.5
  725.6 44.1 %copy.7 = bf16[4096,4096]{1,0:T(8,128)(2,1)} copy(bf16[4096,4096]{0,1:T(8,128)(2,1)} %convert_bitcast_fusion) | data formatting | bytes 67108864
  769.7 0.0 copy-done.1
  769.7 0.0 copy-done.4
  769.7 0.0 copy-done.5
  769.8 0.6 subtract_reduce_fusion
  771.0 179.8 %reduce-scatter.2.cloned.1.call-done = f32[512,4096]{1,0:T(8,128)} async-done(((f32[4096,4096]{1,0:T(8,128)}), f32[512,4096]{1,0:T(8,128)}) %reduce-scatter.2.cloned.1.call-update) | async-done | bytes 8388624 | tf_op jit(solution)/shard_map/reduce_scatter | solution.py:29
  950.8 6.0 convert_element_type.13
  (1 shorter events, 0.0 us)
Async XLA Ops:
  7.2 160.7 %all-gather.3.cloned.1.call-start = ((), (), s32[]{:S(2)}) async-start(), calls=%async_computation.1 | async-start | bytes 37748736 | tf_op jit(solution)/shard_map/all_gather | solution.py:13
  7.9 942.9 %reduce-scatter.2.cloned.1.call-start = ((), (), s32[]{:S(2)}) async-start(), calls=%async_computation.2 | async-start | bytes 75497472 | tf_op jit(solution)/shard_map/reduce_scatter | solution.py:29
  167.9 176.9 %copy-start.2 = (s32[1,8,512]{2,1,0:T(8,128)S(1)}, s32[1,8,512]{2,1,0:T(8,128)}, u32[]{:S(2)}) copy-start(s32[1,8,512]{2,1,0:T(8,128)} %broadcast_subtract_fusion) | copy-start | bytes 49156
  344.8 46.8 %copy-start = (f32[4096]{0:T(1024)}, f32[4096]{0:T(1024)S(1)}, u32[]{:S(2)}) copy-start(f32[4096]{0:T(1024)S(1)} %pmax.7) | copy-start | bytes 49156
  391.5 33.8 %copy-start.3 = (f32[1,4096]{1,0:T(1,128)}, f32[1,4096]{1,0:T(1,128)S(1)}, u32[]{:S(2)}) copy-start(f32[1,4096]{1,0:T(1,128)S(1)} %get-tuple-element.11) | copy-start | bytes 49156
  725.6 44.1 %copy-start.1 = (f32[4096]{0:T(1024)S(1)}, f32[4096]{0:T(1024)}, u32[]{:S(2)}) copy-start(f32[4096]{0:T(1024)} %copy-done) | copy-start | bytes 49156
  725.6 44.1 %copy-start.4 = (f32[1,4096]{1,0:T(1,128)S(1)}, f32[1,4096]{1,0:T(1,128)}, u32[]{:S(2)}) copy-start(f32[1,4096]{1,0:T(1,128)} %copy-done.3) | copy-start | bytes 49156
  725.6 44.1 %copy-start.5 = (f32[1,4096]{1,0:T(1,128)S(1)}, f32[1,4096]{1,0:T(1,128)}, u32[]{:S(2)}) copy-start(f32[1,4096]{1,0:T(1,128)} %get-tuple-element.12) | copy-start | bytes 49156
Sparse Core Ops, SparseCore 0:
  9.8 158.0 all-gather.2
  575.2 375.5 reduce-scatter.1
where the time goes:
time: 966 us; the launch traced here: 965 us
  matrix products  455 us (47%)
  waiting for transfers between devices  326 us (34%)
  other arithmetic  62.8 us (7%)
  blocking collectives  60.2 us (6%)
  local copies, waits for them, and re-layouts  44.8 us (5%)
  between operations  15.9 us (2%)
    reduce_scatter x1, waiting for transfers between devices, local_step(): d_hidden = lax.psum_scatter(dx_part, 'tp', scatter_dimension=0, tiled=True)  180 us
    dot_general x1, matrix products, local_step(): logits = jnp.dot(hid_all, w_loc, preferred_element_type=jnp.float32)  155 us
    dot_general x1, matrix products, local_step(): lax.dot_general(hid_all, grad_out, (((0,), (0,)), ((), ())), preferred_el...  151 us
    dot_general x1, matrix products, local_step(): lax.dot_general(grad_out, w_loc, (((1,), (1,)), ((), ())), preferred_elem...  150 us
    all_gather x1, waiting for transfers between devices, local_step(): hid_all = lax.all_gather(hid_loc, 'tp', axis=0, tiled=True)  146 us
    unnamed x13, local copies, waits for them, and re-layouts  44.2 us
    convert_element_type x1, other arithmetic, local_step(): (jnp.where(is_label, prob_rows - 1.0, prob_rows) * inv_tokens).astype(jnp...  33.8 us
    psum x1, blocking collectives, local_step(): stat_sums = lax.psum(local_stats, 'tp')  24.3 us
  transfers between devices with their start and end apart: 2, of which 2 were waited for; matrix products, arithmetic and copies ran while one was open for 20% of the time, Pallas kernels for 0%

commit v1 on v0

v1 whole, which is shorter than its diff:
```python
import functools

import jax
import jax.numpy as jnp
from jax import lax
from jax.experimental import pallas as pl
from jax.experimental.pallas import tpu as pltpu
from jax.sharding import PartitionSpec as P

F32, BF16, I32 = jnp.float32, jnp.bfloat16, jnp.int32
MESH = pl.DeviceIdType.MESH
ANY = pl.ANY

TOK = 4096
HID = 4096
VOC = 4096
BLK = 256
HALF = 2048
NBLK = TOK // BLK
LANE = 128
PIECE = 512
INV = 1.0 / TOK


def _copy(src, dst, sem):
    return pltpu.make_async_copy(src, dst, sem)


def _send(src, dst, send_sem, recv_sem, dev):
    return pltpu.make_async_remote_copy(
        src_ref=src, dst_ref=dst, send_sem=send_sem, recv_sem=recv_sem, device_id={"tp": dev}, device_id_type=MESH
    )


def _product(lhs, rhs, put, jobs, transposed):
    pl.when(lax.axis_index("tp") < 8)(functools.partial(_pieces, lhs, rhs, put, jobs, transposed))


def _pieces(lhs, rhs, put, jobs, transposed):
    dims = (((1,), (1,)), ((), ())) if transposed else (((1,), (0,)), ((), ()))
    pieces = HALF // PIECE
    deep = 8
    for nt in range(pieces):
        acc = None
        for kt in range(deep):
            part = lax.dot_general(lhs(kt), rhs(nt, kt), dims, preferred_element_type=F32)
            acc = part if acc is None else acc + part
            for job in jobs[nt * deep + kt]:
                job()
        put(nt, acc)


def _wide(v, times=HALF // LANE):
    return jnp.concatenate([v] * times, axis=1)


def _fold(v):
    width = v.shape[1] // 2
    while width >= LANE:
        v = v[:, :width] + v[:, width:]
        width //= 2
    return v


def _column(row):
    return jnp.transpose(jnp.broadcast_to(row, (LANE, LANE)))


def _head_kernel(
    x_hbm, lab_hbm, w_hbm,
    xall, gall, s_n1b, s_self, y2, r1a, loss_out,
    zst, s_d, s_n1a, s_n2, r1n2,
    wv, xg, ga, gb, zb, pbuf, rbuf, sbuf, ab, bb, cb, lab_v, la, lb, st_new, st_all, ml, mk, sl, tl, comb,
    w_sem, lab_sem, labtx_sem, rx, tx, xl_sem, xs_sem, zo_sem, st_sem, sttx_sem,
    zi_sem, rr, ps, ss_sem, s1tx, r1s, r1as, ab_sem, cb_sem, g_sem,
):
    me = lax.axis_index("tp")
    chip = me // 2
    c = me % 2
    x = chip % 2
    y = chip // 2
    oc = 1 - c
    partner = me + 1 - 2 * c
    dx, dy = 2 - 4 * x, 4 - 8 * y
    n1 = me + oc * dx + c * dy
    n2 = me + c * dx + oc * dy
    n1kind = 1 + c

    def chip_of(kind):
        return chip + (kind % 2) * (1 - 2 * x) + (kind // 2) * (2 - 4 * y)

    def order1(i):
        mid, end = (i // 4 + 1) // 2 % 2, i // 12
        return mid * (1 + i % 2) + 3 * end, mid * ((i - 4) // 2) + (1 - mid) * (i % 4)

    def order2(i):
        mid, end = (i // 4 + 1) // 2 % 2, i // 12
        return mid * (1 + i % 2) + 3 * (1 - mid) * (1 - end), mid * ((i - 4) // 2) + (1 - mid) * (i % 4)

    def block_id(kind, q):
        return chip_of(kind) * 4 + q

    def xrows(kind, q, part):
        return xall.at[pl.ds(pl.multiple_of(block_id(kind, q) * BLK + part * LANE, LANE), LANE)]

    def xblock(kind, q):
        return xall.at[pl.ds(pl.multiple_of(block_id(kind, q) * BLK, BLK), BLK)]

    def own(q):
        return x_hbm.at[pl.ds(pl.multiple_of(q * LANE, LANE), LANE)]

    def rxs(kind, q, part):
        return rx.at[kind * 8 + q * 2 + part]

    def wcopy(h):
        return _copy(w_hbm.at[:, pl.ds(h * HALF, HALF)], wv.at[:, pl.ds(h * HALF, HALF)], w_sem.at[h])

    wcopy(0).start()
    wcopy(1).start()

    barrier = pltpu.get_barrier_semaphore()
    for d in range(1, 8):
        pl.semaphore_signal(barrier, inc=1, device_id={"tp": (me + d) % 8}, device_id_type=MESH)
    pl.semaphore_wait(barrier, 7)

    for q in range(4):
        _send(own(q), xrows(0, q, c), tx, rxs(0, q, c), partner).start()
        _send(own(q), xrows_at(xall, me, q), tx, rxs(n1kind, q, c), n1).start()
        _send(own(q), xrows_at(xall, me, q), tx, rxs(3 - n1kind, q, c), n2).start()
    for d in range(1, 8):
        _send(lab_hbm, lab_v.at[me], labtx_sem, lab_sem, (me + d) % 8).start()
    _copy(lab_hbm, lab_v.at[me], lab_sem).start()

    def load_x(b):
        kind, q = order1(b)
        slot = b % 2

        @pl.when(kind == 0)
        def _():
            _copy(own(q), xg.at[slot, pl.ds(pl.multiple_of(c * LANE, LANE), LANE)], xl_sem.at[slot]).start()
            _copy(xrows(0, q, oc), xg.at[slot, pl.ds(pl.multiple_of(oc * LANE, LANE), LANE)], xl_sem.at[slot]).start()

        @pl.when(kind != 0)
        def _():
            _copy(xblock(kind, q), xg.at[slot], xl_sem.at[slot]).start()

    def wait_rows(kind, q, part):
        _copy(xrows(kind, q, part), xrows(kind, q, part), rxs(kind, q, part)).wait()

    def zcopy(b, h):
        kind, q = order1(b)
        return _copy(zb.at[h], zst.at[block_id(kind, q), h], zo_sem.at[h])

    def own_store(b):
        slot = b % 2
        return _copy(xg.at[slot, pl.ds(pl.multiple_of(c * LANE, LANE), LANE)], xrows(0, b % 4, c), xs_sem.at[slot])

    def label_column(blk, part):
        return _column(lab_v[2 * (blk // 4) + part, pl.ds(blk % 4, 1), :])

    def lane_stats(col, h, r):
        rows = pl.ds(r, 8)
        z = zb[h, rows, :]
        m = ml[h, rows, :]
        hit = _wide(col[rows, :] - (me * VOC + h * HALF)) == lax.broadcasted_iota(I32, (8, HALF), 1)
        s = _fold(jnp.exp(z - _wide(m)))
        t = _fold(jnp.where(hit, z, 0.0))
        if h == 1:
            m0 = mk[0, rows, :]
            mm = jnp.maximum(m0, m)
            s = sl[0, rows, :] * jnp.exp(m0 - mm) + s * jnp.exp(m - mm)
            t = tl[0, rows, :] + t
            m = mm
        mk[h, rows, :] = m
        sl[h, rows, :] = s
        tl[h, rows, :] = t

    def label_columns(blk, col, part):
        col[pl.ds(part * LANE, LANE), :] = label_column(blk, part)

    def row_stats(part):
        rows = pl.ds(part * LANE, LANE)
        m = jnp.transpose(mk[1, rows, :])
        top = jnp.max(m, axis=0, keepdims=True)
        st_new[part : part + 1, :] = top
        st_new[2 + part : 3 + part, :] = jnp.sum(jnp.transpose(sl[1, rows, :]) * jnp.exp(m - top), axis=0, keepdims=True)
        st_new[4 + part : 5 + part, :] = jnp.sum(jnp.transpose(tl[1, rows, :]), axis=0, keepdims=True)

    def send_stats(blk):
        for d in range(1, 8):
            _send(st_new, st_all.at[blk, me], sttx_sem, st_sem.at[blk], (me + d) % 8).start()
        st_all[blk, me] = st_new[...]

    def stats_sent():
        _copy(st_all.at[0, pl.ds(0, 7)], st_all.at[0, pl.ds(0, 7)], sttx_sem).wait()

    def logits(b, h, jobs):
        slot = b % 2
        def put(nt, z):
            zb[h, :, nt * PIECE : (nt + 1) * PIECE] = z
            m = z[:, :LANE]
            for j in range(1, 4):
                m = jnp.maximum(m, z[:, j * LANE : (j + 1) * LANE])
            if nt:
                m = jnp.maximum(m, ml[h])
            ml[h] = m

        _product(
            lambda kt: xg[slot, :, kt * PIECE : (kt + 1) * PIECE],
            lambda nt, kt: wv[kt * PIECE : (kt + 1) * PIECE, h * HALF + nt * PIECE : h * HALF + (nt + 1) * PIECE],
            put,
            jobs,
            False,
        )

    _copy(own(0), xg.at[0, pl.ds(pl.multiple_of(c * LANE, LANE), LANE)], xl_sem.at[0]).start()
    wait_rows(0, 0, oc)
    _copy(xrows(0, 0, oc), xg.at[0, pl.ds(pl.multiple_of(oc * LANE, LANE), LANE)], xl_sem.at[0]).start()
    _copy(lab_v, lab_v, lab_sem).wait()
    wcopy(0).wait()

    def phase1(i, carry):
        slot = i % 2
        kind, q = order1(i)
        kprev, qprev = order1((i + NBLK - 2) % NBLK)
        kn, qn = order1((i + 1) % NBLK)

        _copy(xg.at[slot], xg.at[slot], xl_sem.at[slot]).wait()

        @pl.when(i < 4)
        def _():
            own_store(i).start()

        @pl.when(i > 0)
        def _():
            zcopy(i - 1, 1).start()
            zcopy(i - 1, 0).wait()

        @pl.when(i > 1)
        def _():
            send_stats(block_id(kprev, qprev))

        @pl.when((i >= 3) & (i < NBLK - 1))
        def _():
            wait_rows(kn, qn, c)
            _send(xrows(kn, qn, c), xrows(kn, qn, c), tx, rxs(kn, qn, c), partner).start()

            @pl.when(kn == n1kind)
            def _():
                _send(xrows(kn, qn, c), xrows(kn, qn, c), tx, rxs(3, qn, c), n2).start()

        jobs = [[] for _ in range(32)]
        for r in range(32):
            jobs[r].append(functools.partial(lane_stats, la, 1, r * 8))
        for part in range(2):
            jobs[4 + 4 * part].append(functools.partial(label_columns, block_id(kind, q), lb, part))
        logits(i, 0, jobs)

        zcopy(i, 0).start()

        @pl.when(i == 0)
        def _():
            wcopy(1).wait()

        @pl.when(i > 0)
        def _():
            zcopy(i - 1, 1).wait()

        @pl.when(i > 1)
        def _():
            stats_sent()

        @pl.when(i < NBLK - 1)
        def _():
            wait_rows(kn, qn, oc)

            @pl.when((i >= 1) & (i < 5))
            def _():
                own_store(i - 1).wait()

            load_x(i + 1)

        la[...] = lb[...]
        jobs = [[] for _ in range(32)]
        for r in range(32):
            jobs[r].append(functools.partial(lane_stats, lb, 0, r * 8))
        for part in range(2):
            jobs[8 + 8 * part].append(functools.partial(row_stats, part))
        logits(i, 1, jobs)
        return carry

    lax.fori_loop(0, NBLK, phase1, 0)
    last = NBLK - 1
    klast, qlast = order1(jnp.int32(last))
    zcopy(last, 1).start()
    zcopy(last, 0).wait()
    kprev, qprev = order1(jnp.int32(last - 1))
    send_stats(block_id(kprev, qprev))
    stats_sent()
    for r in range(32):
        lane_stats(la, 1, r * 8)
    for part in range(2):
        row_stats(part)
    zcopy(last, 1).wait()
    send_stats(block_id(klast, qlast))

    def zload(k, n):
        kind, q = order2(k)
        return _copy(zst.at[block_id(kind, q), n], zb.at[n], zi_sem.at[n])

    zload(0, 0).start()
    zload(0, 1).start()

    def combine(b, acc):
        _copy(st_all.at[b, pl.ds(0, 7)], st_all.at[b, pl.ds(0, 7)], st_sem.at[b]).wait()
        top = st_all[b, 0, 0:2, :]
        for d in range(1, 8):
            top = jnp.maximum(top, st_all[b, d, 0:2, :])
        s = jnp.zeros((2, LANE), F32)
        t = jnp.zeros((2, LANE), F32)
        for d in range(8):
            s = s + st_all[b, d, 2:4, :] * jnp.exp(st_all[b, d, 0:2, :] - top)
            t = t + st_all[b, d, 4:6, :]
        comb[b, 0:2, :] = top
        comb[b, 2:4, :] = INV / s
        return acc + (top + jnp.log(s) - t)

    token_loss = lax.fori_loop(0, NBLK, combine, jnp.zeros((2, LANE), F32))
    loss_out[...] = jnp.full((8, LANE), jnp.sum(token_loss) * INV, F32)

    gbufs = (ga, gb)

    def columns(k, par, part):
        kind, q = order2(k)
        blk = block_id(kind, q)
        rows = pl.ds(part * LANE, LANE)
        (la if par == 0 else lb)[rows, :] = label_column(blk, part)
        ml[par, rows, :] = _column(comb[blk, part : part + 1, :])
        sl[par, rows, :] = _column(comb[blk, 2 + part : 3 + part, :])

    def gradient(n, par, r, j):
        rows = pl.ds(r, 16)
        col = (la if par == 0 else lb)[rows, :] - (me * VOC + n * HALF + j)
        p = jnp.exp(zb[n, rows, j : j + 1024] - _wide(ml[par, rows, :], 8)) * _wide(sl[par, rows, :], 8)
        g = jnp.where(_wide(col, 8) == lax.broadcasted_iota(I32, (16, 1024), 1), p - INV, p)
        gbufs[par][rows, n * HALF + j : n * HALF + j + 1024] = g.astype(BF16)

    def gstore(k, par):
        kind, q = order2(k)
        return _copy(gbufs[par], gall.at[pl.ds(pl.multiple_of(block_id(kind, q) * BLK, BLK), BLK)], g_sem.at[par])

    def tile(ref, q, n):
        return ref.at[pl.ds(pl.multiple_of(q * LANE, LANE), LANE), pl.ds(pl.multiple_of(n * HALF, HALF), HALF)]

    def spair(k, n):
        return _send(
            pbuf.at[n, pl.ds(pl.multiple_of(oc * LANE, LANE), LANE)], rbuf.at[k % 2, n], ps.at[n], rr.at[(k % 2) * 2 + n], partner
        )

    def sstore_start(k, n):
        kind, q = order2(k)
        sem = ss_sem.at[n]

        @pl.when(kind == 3)
        def _():
            _copy(sbuf.at[n], tile(s_d, q, n), sem).start()

        @pl.when((kind == n1kind) & (q < 2))
        def _():
            _copy(sbuf.at[n], tile(s_n1a, q % 2, n), sem).start()

        @pl.when((kind == n1kind) & (q >= 2))
        def _():
            _copy(sbuf.at[n], tile(s_n1b, q % 2, n), sem).start()

        @pl.when(kind == 3 - n1kind)
        def _():
            _copy(sbuf.at[n], tile(s_n2, q, n), sem).start()

        @pl.when(kind == 0)
        def _():
            _copy(sbuf.at[n], tile(s_self, q, n), sem).start()

    def sstore_done(k, n):
        kind, q = order2(k)
        _copy(sbuf.at[n], tile(s_d, 0, n), ss_sem.at[n]).wait()

        @pl.when(kind == 3)
        def _():
            _send(tile(s_d, q, n), tile(r1n2, q, n), s1tx, r1s.at[q * 2 + n], n1).start()

        @pl.when((kind == n1kind) & (q < 2))
        def _():
            _send(tile(s_n1a, q % 2, n), tile(r1a, q % 2, n), s1tx, r1as.at[(q % 2) * 2 + n], n1).start()

    def stage2_load(q, n):
        _copy(tile(r1n2, q, n), tile(r1n2, q, n), r1s.at[q * 2 + n]).wait()
        _copy(tile(s_n2, q, n), ab.at[n], ab_sem.at[n * 2]).start()
        _copy(tile(r1n2, q, n), bb.at[n], ab_sem.at[n * 2 + 1]).start()

    def pair_sum(k, n, r):
        sbuf[n, pl.ds(r, 16), :] = pbuf[n, pl.ds(pl.multiple_of(c * LANE + r, 16), 16), :] + rbuf[k % 2, n, pl.ds(r, 16), :]

    def stage2_sum(n, r):
        cb[pl.ds(r, 16), :] = ab[n, pl.ds(r, 16), :] + bb[n, pl.ds(r, 16), :]

    def rwait(k, n):
        _copy(rbuf.at[k % 2, n], rbuf.at[k % 2, n], rr.at[(k % 2) * 2 + n]).wait()

    for part in range(2):
        columns(jnp.int32(0), 0, part)
        columns(jnp.int32(1), 1, part)
    for n in range(2):
        zload(0, n).wait()
        for r in range(0, BLK, 16):
            gradient(n, 0, r, 0)
            gradient(n, 0, r, 1024)
    gstore(0, 0).start()
    zload(1, 0).start()
    zload(1, 1).start()

    def sub(k, cur):
        nxt = 1 - cur

        @pl.when(k >= 1)
        def _():
            gstore(k - 1, nxt).wait()

        def trip(n):
            @pl.when(k < NBLK - 1)
            def _():
                zload(k + 1, n).wait()

            @pl.when(k >= 1)
            def _():
                rwait(k - 1, n)
                spair(k - 1, n).wait_send()

            @pl.when(k >= 12)
            def _():
                _copy(tile(s_n2, 0, n), ab.at[n], ab_sem.at[n * 2]).wait()
                _copy(tile(r1n2, 0, n), bb.at[n], ab_sem.at[n * 2 + 1]).wait()

            @pl.when(k >= 13 - n)
            def _():
                _copy(cb, tile(y2, 0, n), cb_sem).wait()

            jobs = [[] for _ in range(32)]
            for r in range(8):
                jobs[r // 2].append(functools.partial(pair_sum, k - 1, n, r * 16))
                jobs[20 + r].append(functools.partial(stage2_sum, n, r * 16))
            for r in range(32):
                jobs[4 + r * 7 // 8].append(functools.partial(gradient, n, nxt, r // 2 * 16, r % 2 * 1024))
            for part in range(2):
                jobs[8 + 8 * part].append(functools.partial(columns, (k + 2) % NBLK, cur, part))

            def put(nt, acc):
                pbuf[n, :, nt * PIECE : (nt + 1) * PIECE] = acc

            _product(
                lambda kt: gbufs[cur][:, kt * PIECE : (kt + 1) * PIECE],
                lambda nt, kt: wv[pl.ds(pl.multiple_of(n * HALF + nt * PIECE, PIECE), PIECE), kt * PIECE : (kt + 1) * PIECE],
                put,
                jobs,
                True,
            )

            spair(k, n).start()

            @pl.when(k < NBLK - 2)
            def _():
                zload(k + 2, n).start()

            @pl.when(k >= 2 - n)
            def _():
                sstore_done(k - 2 + n, 1 - n)

            @pl.when(k >= 1)
            def _():
                sstore_start(k - 1, n)

            @pl.when(k >= 12)
            def _():
                _copy(cb, tile(y2, k - 12, n), cb_sem).start()

            @pl.when((k >= 11) & (k < NBLK - 1))
            def _():
                stage2_load(k - 11, n)

        trip(0)
        trip(1)

        @pl.when(k < NBLK - 1)
        def _():
            gstore(k + 1, nxt).start()

    def pair(p, carry):
        sub(2 * p, 0)
        sub(2 * p + 1, 1)
        return carry

    lax.fori_loop(0, NBLK // 2, pair, 0)

    kl = jnp.int32(NBLK - 1)
    for n in range(2):
        rwait(kl, n)
        spair(kl, n).wait_send()
        if n == 0:
            sstore_done(kl - 1, 1)
        for r in range(8):
            pair_sum(kl, n, r * 16)
        sstore_start(kl, n)
    for n in range(2):
        sstore_done(kl, n)
    gstore(kl, 1).wait()
    _copy(cb, tile(y2, 0, 0), cb_sem).wait()

    for i in range(4):
        _copy(tile(r1a, i // 2, i % 2), tile(r1a, i // 2, i % 2), r1as.at[i]).wait()
    _copy(s_d, s_d, s1tx).wait()
    _copy(s_n1a, s_n1a, s1tx).wait()
    _copy(xall.at[pl.ds(0, 28 * LANE)], xall.at[pl.ds(0, 28 * LANE)], tx).wait()
    for d in range(7):
        _copy(lab_v.at[d], lab_v.at[d], labtx_sem).wait()
    stats_sent()


def xrows_at(xall, dev, q):
    return xall.at[pl.ds(pl.multiple_of((dev // 2) * 1024 + q * BLK + (dev % 2) * LANE, LANE), LANE)]


def _head(hid, lab, w):
    hbm = pl.BlockSpec(memory_space=ANY)
    sd = jax.ShapeDtypeStruct
    dma = pltpu.SemaphoreType.DMA
    vmem = pltpu.VMEM
    quarter = (LANE, HALF)
    return pl.pallas_call(
        _head_kernel,
        out_shape=(
            sd((TOK, HID), BF16),
            sd((TOK, VOC), BF16),
            sd((256, HID), F32),
            sd((PIECE, HID), F32),
            sd((PIECE, HID), F32),
            sd((256, HID), F32),
            sd((8, LANE), F32),
            sd((NBLK, 2, BLK, HALF), F32),
            sd((PIECE, HID), F32),
            sd((256, HID), F32),
            sd((PIECE, HID), F32),
            sd((PIECE, HID), F32),
        ),
        in_specs=[hbm] * 3,
        out_specs=(hbm,) * 6 + (pl.BlockSpec(memory_space=vmem),) + (hbm,) * 5,
        scratch_shapes=[
            vmem((HID, VOC), BF16),
            vmem((2, BLK, HID), BF16),
            vmem((BLK, VOC), BF16),
            vmem((BLK, VOC), BF16),
            vmem((2, BLK, HALF), F32),
            vmem((2, BLK, HALF), F32),
            vmem((2, 2) + quarter, F32),
            vmem((2,) + quarter, F32),
            vmem((2,) + quarter, F32),
            vmem((2,) + quarter, F32),
            vmem(quarter, F32),
            vmem((8, 4, LANE), I32),
            vmem((BLK, LANE), I32),
            vmem((BLK, LANE), I32),
            vmem((8, LANE), F32),
            vmem((NBLK, 8, 8, LANE), F32),
            vmem((2, BLK, LANE), F32),
            vmem((2, BLK, LANE), F32),
            vmem((2, BLK, LANE), F32),
            vmem((2, BLK, LANE), F32),
            vmem((NBLK, 8, LANE), F32),
            dma((2,)),
            dma(()),
            dma(()),
            dma((32,)),
            dma(()),
            dma((2,)),
            dma((2,)),
            dma((2,)),
            dma((NBLK,)),
            dma(()),
            dma((2,)),
            dma((4,)),
            dma((2,)),
            dma((2,)),
            dma(()),
            dma((8,)),
            dma((4,)),
            dma((4,)),
            dma(()),
            dma((2,)),
        ],
        compiler_params=pltpu.CompilerParams(collective_id=0, has_side_effects=True, vmem_limit_bytes=67_043_328),
        cost_estimate=pl.CostEstimate(flops=4 * TOK * HID * VOC, bytes_accessed=400 * 2**20, transcendentals=2 * TOK * VOC),
        name="head",
    )(hid, lab, w)


def _dhead_kernel(x_ref, g_ref, o_ref):
    o_ref[...] = lax.dot_general(x_ref[...], g_ref[...], (((0,), (0,)), ((), ())), preferred_element_type=F32).astype(BF16)


def _dhead(xall, gall):
    bm, bn = PIECE, 1024
    return pl.pallas_call(
        _dhead_kernel,
        grid=(VOC // bn, HID // bm),
        in_specs=[pl.BlockSpec((TOK, bm), lambda j, i: (0, i)), pl.BlockSpec((TOK, bn), lambda j, i: (0, j))],
        out_specs=pl.BlockSpec((bm, bn), lambda j, i: (i, j)),
        out_shape=jax.ShapeDtypeStruct((HID, VOC), BF16),
        compiler_params=pltpu.CompilerParams(vmem_limit_bytes=60 * 2**20, dimension_semantics=("arbitrary", "arbitrary")),
        cost_estimate=pl.CostEstimate(flops=2 * TOK * HID * VOC, bytes_accessed=200 * 2**20, transcendentals=0),
        name="dhead",
    )(xall, gall)


def solution(mesh):
    def device(y, x, core):
        return (y % 2) * 4 + (x % 2) * 2 + core

    first, second = [], []
    for yy in range(2):
        for xx in range(2):
            along_x = [(device(yy, xx, k), device(yy, xx + 1, k)) for k in range(2)]
            along_y = [(device(yy, xx, k), device(yy + 1, xx, k)) for k in range(2)]
            first += [along_x[0], along_y[1]]
            second += [along_y[0], along_x[1]]

    def local_step(hid, w, lab):
        xall, gall, s_n1b, s_self, y2, r1a, loss = _head(hid, lab.reshape(4, LANE), w)[:7]
        r1b = lax.ppermute(s_n1b, "tp", first)
        r2 = lax.ppermute(y2, "tp", second)
        d_head = _dhead(xall, gall)
        d_hidden = (s_self + jnp.concatenate([r1a, r1b], axis=0) + r2).astype(BF16)
        return loss[0, :1], d_hidden, d_head

    return jax.shard_map(
        local_step,
        mesh=mesh,
        in_specs=(P(("dp", "tp"), None), P(None, "tp"), P(("dp", "tp"))),
        out_specs=(P("dp"), P(("dp", "tp"), None), P("dp", "tp")),
        check_vma=False,
    )
```

time: 966 us -> 587 us (0.61)
  Pallas kernels: 0 us -> 572 us
  matrix products: 455 us -> 0 us
  waiting for transfers between devices: 326 us -> 0.01 us
  blocking collectives: 60.2 us -> 0 us
  other arithmetic: 62.8 us -> 11.4 us
  local copies, waits for them, and re-layouts: 44.8 us -> 1.2 us
  between operations: 15.9 us -> 0.64 us
    pallas_call x0 -> x2, Pallas kernels: none -> 572 us  [the longest x1 420 us: _head(): pl.pallas_call(_head_kernel, out_shape=(sd((TOK, HID), BF16), sd((TOK, VO...]
    dot_general x3 -> x0, matrix products: 455 us -> none  [the longest x1 155 us: local_step(): logits = jnp.dot(hid_all, w_loc, preferred_element_type=jnp.float32)]
    reduce_scatter x1 -> x0, waiting for transfers between devices: 180 us -> none  [local_step(): d_hidden = lax.psum_scatter(dx_part, 'tp', scatter_dimension=0, tiled=True)]
    all_gather x1 -> x0, waiting for transfers between devices: 146 us -> none  [local_step(): hid_all = lax.all_gather(hid_loc, 'tp', axis=0, tiled=True)]
    unnamed x13 -> x0, local copies, waits for them, and re-layouts: 44.2 us -> none
    convert_element_type x2 -> x1, other arithmetic: 39.8 us -> 11.4 us  [local_step(): d_hidden = (s_self + jnp.concatenate([r1a, r1b], axis=0) + r2).astype(BF16)]
    psum x1 -> x0, blocking collectives: 24.3 us -> none  [local_step(): stat_sums = lax.psum(local_stats, 'tp')]
    reduce_sum x2 -> x0, other arithmetic: 22.4 us -> none  [the longest x1 21.7 us: local_step(): jnp.sum(shifted, axis=1)]
  transfers between devices with their start and end apart: 2 -> 2, of which waited for: 2 -> 0; matrix products, arithmetic and copies ran while one was open for 20% -> 0% of each run, Pallas kernels for 0% -> 26%
where the time goes in v1:
time: 587 us; the launch traced here: 586 us
  Pallas kernels  572 us (97%)
  other arithmetic  11.4 us (2%)
    pallas_call x1, Pallas kernels, _head(): pl.pallas_call(_head_kernel, out_shape=(sd((TOK, HID), BF16), sd((TOK, VO...  420 us
    pallas_call x1, Pallas kernels, _dhead(): pl.pallas_call(_dhead_kernel, grid=(VOC // bn, HID // bm), in_specs=[pl.B...  152 us
  transfers between devices with their start and end apart: 2, of which 0 were waited for; matrix products, arithmetic and copies ran while one was open for 0% of the time, Pallas kernels for 26%

profile of v1, /device:TPU:0, one launch (start us, length us, event | category | flops | bytes accessed | tf_op | source)
XLA Modules:
  0.0 586.4 jit_solution(6590745634159589254)
XLA Ops:
  0.6 419.8 %head.1 = (bf16[4096,4096]{1,0:T(8,128)(2,1)}, bf16[4096,4096]{1,0:T(8,128)(2,1)}, f32[256,4096]{1,0:T(8,128)}, f32[512,4096]{1,0:T(8,128)}, f32[512,4096]{1,0:T...) custom-call(bf16[512,4096]{1,0:T(8,128)(2,1)} %x_hbm.1, ...), custom_call_target="tpu_custom_call" | custom-call | flops 274877906944 | bytes 419430400 | tf_op jit(solution)/shard_map/head/pallas_call | solution.py:538
  420.5 0.6 collective-permute-start
  421.1 0.4 collective-permute-start.1
  421.5 152.3 %dhead.1 = bf16[4096,4096]{1,0:T(8,128)(2,1)} custom-call(bf16[4096,4096]{1,0:T(8,128)(2,1)} %get-tuple-element.15.x_ref, bf16[4096,4096]{1,0:T(8,128)(2,1)} %get-tuple-element.16.g_ref), custom_call_target="tpu_custom_call" | custom-call | flops 137438953472 | bytes 209715200 | tf_op jit(solution)/shard_map/dhead/pallas_call | solution.py:611
  573.8 1.2 slice.3
  575.0 0.0 collective-permute-done
  575.0 0.0 collective-permute-done.1
  575.0 11.4 %fusion.1 = bf16[512,4096]{1,0:T(8,128)(2,1)} fusion(f32[512,4096]{1,0:T(8,128)} %collective-permute-done.1, f32[512,4096]{1,0:T(8,128)} %get-tuple-element.11, f32[256,4096]{1,0:T(8,128)} %collective-permute-done, f32[256,4096]{1,0:T(8,128)} %get-tuple-element.12), kind=kLoop, calls=%fused_computation.2 | loop fusion | flops 8388608 | bytes 29360128 | tf_op jit(solution)/shard_map/convert_element_type | solution.py:640
Async XLA Ops:
  420.5 154.5 %collective-permute-start = (f32[256,4096]{1,0:T(8,128)}, f32[256,4096]{1,0:T(8,128)}, u32[]{:S(2)}, u32[]{:S(2)}) collective-permute-start(f32[256,4096]{1,0:T(8,128)} %get-tuple-element.13), channel_id=1, source_target_pairs={{0,2},{1,5},{2,0},{3,7},{4,6},{5,1},{6,4},{7,3}} | collective-permute-start | bytes 12582920 | tf_op jit(solution)/shard_map/ppermute | solution.py:637
  421.1 153.9 %collective-permute-start.1 = (f32[512,4096]{1,0:T(8,128)}, f32[512,4096]{1,0:T(8,128)}, u32[]{:S(2)}, u32[]{:S(2)}) collective-permute-start(f32[512,4096]{1,0:T(8,128)} %get-tuple-element.14), channel_id=1, source_target_pairs={{0,4},{1,3},{2,6},{3,1},{4,0},{5,7},{6,2},{7,5}} | collective-permute-start | bytes 25165832 | tf_op jit(solution)/shard_map/ppermute | solution.py:638

commit v2 on v1

--- a/solution.py
+++ b/solution.py
@@ -18,6 +18,12 @@
 HALF = 2048
 NBLK = TOK // BLK
 LANE = 128
+MIB = 1 << 20
+TWO = (2,)
+PAIR = (0, 1)
+TILE = (8, LANE)
+SUB = 16
+FOUR = range(4)
 PIECE = 512
 INV = 1.0 / TOK
 
@@ -70,7 +76,7 @@
     x_hbm, lab_hbm, w_hbm,
     xall, gall, s_n1b, s_self, y2, r1a, loss_out,
     zst, s_d, s_n1a, s_n2, r1n2,
-    wv, xg, ga, gb, zb, pbuf, rbuf, sbuf, ab, bb, cb, lab_v, la, lb, st_new, st_all, ml, mk, sl, tl, comb,
+    wv, xg, ga, gb, zb, pbuf, rbuf, sbuf, ab, bb, cb, lab_v, la, lb, st_new, st_loc, st_all, ml, mk, sl, tl, comb, c_lab, c_top, c_scale, loss_acc,
     w_sem, lab_sem, labtx_sem, rx, tx, xl_sem, xs_sem, zo_sem, st_sem, sttx_sem,
     zi_sem, rr, ps, ss_sem, s1tx, r1s, r1as, ab_sem, cb_sem, g_sem,
 ):
@@ -112,24 +118,27 @@
     def rxs(kind, q, part):
         return rx.at[kind * 8 + q * 2 + part]
 
-    def wcopy(h):
-        return _copy(w_hbm.at[:, pl.ds(h * HALF, HALF)], wv.at[:, pl.ds(h * HALF, HALF)], w_sem.at[h])
-
-    wcopy(0).start()
-    wcopy(1).start()
+    def wcopy(j):
+        cols = pl.ds(j * PIECE, PIECE)
+        return _copy(w_hbm.at[:, cols], wv.at[:, cols], w_sem.at[j])
+
+    _copy(own(0), xg.at[0, pl.ds(pl.multiple_of(c * LANE, LANE), LANE)], xl_sem.at[0]).start()
+    for j in FOUR:
+        wcopy(j).start()
 
     barrier = pltpu.get_barrier_semaphore()
     for d in range(1, 8):
         pl.semaphore_signal(barrier, inc=1, device_id={"tp": (me + d) % 8}, device_id_type=MESH)
     pl.semaphore_wait(barrier, 7)
 
-    for q in range(4):
-        _send(own(q), xrows(0, q, c), tx, rxs(0, q, c), partner).start()
-        _send(own(q), xrows_at(xall, me, q), tx, rxs(n1kind, q, c), n1).start()
-        _send(own(q), xrows_at(xall, me, q), tx, rxs(3 - n1kind, q, c), n2).start()
     for d in range(1, 8):
         _send(lab_hbm, lab_v.at[me], labtx_sem, lab_sem, (me + d) % 8).start()
     _copy(lab_hbm, lab_v.at[me], lab_sem).start()
+    for q in FOUR:
+        _send(own(q), xrows(0, q, c), tx, rxs(0, q, c), partner).start()
+    for q in FOUR:
+        _send(own(q), xrows_at(xall, me, q), tx, rxs(n1kind, q, c), n1).start()
+        _send(own(q), xrows_at(xall, me, q), tx, rxs(3 - n1kind, q, c), n2).start()
 
     def load_x(b):
         kind, q = order1(b)
@@ -146,6 +155,14 @@
 
     def wait_rows(kind, q, part):
         _copy(xrows(kind, q, part), xrows(kind, q, part), rxs(kind, q, part)).wait()
+
+    def take_rows(kind, q):
+        wait_rows(kind, q, c)
+        _send(xrows(kind, q, c), xrows(kind, q, c), tx, rxs(kind, q, c), partner).start()
+
+    def part_load(b, part):
+        kind, q = order1(b)
+        return _copy(xrows(kind, q, part), xg.at[b % 2, pl.ds(pl.multiple_of(part * LANE, LANE), LANE)], xl_sem.at[b % 2])
 
     def zcopy(b, h):
         kind, q = order1(b)
@@ -188,11 +205,56 @@
 
     def send_stats(blk):
         for d in range(1, 8):
-            _send(st_new, st_all.at[blk, me], sttx_sem, st_sem.at[blk], (me + d) % 8).start()
+            _send(st_loc.at[blk], st_all.at[blk, me], sttx_sem, st_sem.at[blk], (me + d) % 8).start()
+
+    def keep_stats(blk):
+        st_loc[blk] = st_new[...]
         st_all[blk, me] = st_new[...]
 
-    def stats_sent():
-        _copy(st_all.at[0, pl.ds(0, 7)], st_all.at[0, pl.ds(0, 7)], sttx_sem).wait()
+    def combine(blk):
+        top = st_all[blk, 0, 0:2, :]
+        for d in range(1, 8):
+            top = jnp.maximum(top, st_all[blk, d, 0:2, :])
+        s = jnp.zeros((2, LANE), F32)
+        t = jnp.zeros((2, LANE), F32)
+        for d in range(8):
+            s = s + st_all[blk, d, 2:4, :] * jnp.exp(st_all[blk, d, 0:2, :] - top)
+            t = t + st_all[blk, d, 4:6, :]
+        comb[0:2, :] = top
+        comb[2:4, :] = INV / s
+        return top + jnp.log(s) - t
+
+    def stats_arrived(blk):
+        _copy(st_all.at[blk, pl.ds(0, 7)], st_all.at[blk, pl.ds(0, 7)], st_sem.at[blk]).wait()
+
+    def columns(blk, par, part):
+        rows = pl.ds(part * LANE, LANE)
+        c_lab[par, rows, :] = label_column(blk, part)
+        c_top[par, rows, :] = _column(comb[part : part + 1, :])
+        c_scale[par, rows, :] = _column(comb[2 + part : 3 + part, :])
+
+    def gradient(src, n, par, r, j):
+        rows = pl.ds(pl.multiple_of(r, SUB), SUB)
+        col = c_lab[par, rows, :] - (me * VOC + n * HALF + j)
+        p = jnp.exp(src[n, rows, j : j + 1024] - _wide(c_top[par, rows, :], 8)) * _wide(c_scale[par, rows, :], 8)
+        g = jnp.where(_wide(col, 8) == lax.broadcasted_iota(I32, (SUB, 1024), 1), p - INV, p)
+        gbufs[par][rows, n * HALF + j : n * HALF + j + 1024] = g.astype(BF16)
+
+    def gradient_jobs(src, n, par):
+        return [functools.partial(gradient, src, n, par, r, j) for r in range(0, BLK, SUB) for j in (0, 1024)]
+
+    gbufs = (ga, gb)
+
+    def gstore(k, par):
+        kind, q = order2(k)
+        return _copy(gbufs[par], gall.at[pl.ds(pl.multiple_of(block_id(kind, q) * BLK, BLK), BLK)], g_sem.at[par])
+
+    def zload(k, dst, n):
+        kind, q = order2(k)
+        return _copy(zst.at[block_id(kind, q), n], dst.at[n], zi_sem.at[n])
+
+    first_kind, first_q = order2(me * 0)
+    first_blk = block_id(first_kind, first_q)
 
     def logits(b, h, jobs):
         slot = b % 2
@@ -213,11 +275,13 @@
             False,
         )
 
-    _copy(own(0), xg.at[0, pl.ds(pl.multiple_of(c * LANE, LANE), LANE)], xl_sem.at[0]).start()
     wait_rows(0, 0, oc)
     _copy(xrows(0, 0, oc), xg.at[0, pl.ds(pl.multiple_of(oc * LANE, LANE), LANE)], xl_sem.at[0]).start()
     _copy(lab_v, lab_v, lab_sem).wait()
-    wcopy(0).wait()
+    for j in FOUR:
+        wcopy(j).wait()
+    for j in range(4, 8):
+        wcopy(j).start()
 
     def phase1(i, carry):
         slot = i % 2
@@ -225,6 +289,11 @@
         kprev, qprev = order1((i + NBLK - 2) % NBLK)
         kn, qn = order1((i + 1) % NBLK)
 
+        @pl.when(i == NBLK - 1)
+        def _():
+            wait_rows(kind, q, oc)
+            part_load(i, oc).start()
+
         _copy(xg.at[slot], xg.at[slot], xl_sem.at[slot]).wait()
 
         @pl.when(i < 4)
@@ -238,12 +307,34 @@
 
         @pl.when(i > 1)
         def _():
-            send_stats(block_id(kprev, qprev))
-
-        @pl.when((i >= 3) & (i < NBLK - 1))
-        def _():
-            wait_rows(kn, qn, c)
-            _send(xrows(kn, qn, c), xrows(kn, qn, c), tx, rxs(kn, qn, c), partner).start()
+            keep_stats(block_id(kprev, qprev))
+
+        @pl.when(i == NBLK - 2)
+        def _():
+            zload(0, pbuf, 0).start()
+            zload(0, pbuf, 1).start()
+
+        @pl.when(i == NBLK - 1)
+        def _():
+            stats_arrived(first_blk)
+            loss_acc[...] = combine(first_blk)
+            for part in PAIR:
+                columns(first_blk, 0, part)
+            for n in PAIR:
+                zload(0, pbuf, n).wait()
+
+                def some(r, carry, n=n):
+                    for j in FOUR:
+                        gradient(pbuf, n, 0, r * 32 + j // 2 * SUB, j % 2 * 1024)
+                    return carry
+
+                lax.fori_loop(0, 8, some, 0)
+
+            gstore(0, 0).start()
+
+        @pl.when((i >= 3) & (i < NBLK - 2))
+        def _():
+            take_rows(kn, qn)
 
             @pl.when(kn == n1kind)
             def _():
@@ -252,7 +343,7 @@
         jobs = [[] for _ in range(32)]
         for r in range(32):
             jobs[r].append(functools.partial(lane_stats, la, 1, r * 8))
-        for part in range(2):
+        for part in PAIR:
             jobs[4 + 4 * part].append(functools.partial(label_columns, block_id(kind, q), lb, part))
         logits(i, 0, jobs)
 
@@ -260,7 +351,8 @@
 
         @pl.when(i == 0)
         def _():
-            wcopy(1).wait()
+            for j in range(4, 8):
+                wcopy(j).wait()
 
         @pl.when(i > 0)
         def _():
@@ -268,9 +360,14 @@
 
         @pl.when(i > 1)
         def _():
-            stats_sent()
-
-        @pl.when(i < NBLK - 1)
+            send_stats(block_id(kprev, qprev))
+
+        @pl.when(i == NBLK - 2)
+        def _():
+            take_rows(kn, qn)
+            part_load(i + 1, c).start()
+
+        @pl.when(i < NBLK - 2)
         def _():
             wait_rows(kn, qn, oc)
 
@@ -284,7 +381,7 @@
         jobs = [[] for _ in range(32)]
         for r in range(32):
             jobs[r].append(functools.partial(lane_stats, lb, 0, r * 8))
-        for part in range(2):
+        for part in PAIR:
             jobs[8 + 8 * part].append(functools.partial(row_stats, part))
         logits(i, 1, jobs)
         return carry
@@ -292,62 +389,27 @@
     lax.fori_loop(0, NBLK, phase1, 0)
     last = NBLK - 1
     klast, qlast = order1(jnp.int32(last))
+    kprev, qprev = order1(jnp.int32(last - 1))
+    bprev, blast = block_id(kprev, qprev), block_id(klast, qlast)
     zcopy(last, 1).start()
     zcopy(last, 0).wait()
-    kprev, qprev = order1(jnp.int32(last - 1))
-    send_stats(block_id(kprev, qprev))
-    stats_sent()
+    zload(1, zb, 0).start()
+    keep_stats(bprev)
     for r in range(32):
         lane_stats(la, 1, r * 8)
-    for part in range(2):
+    send_stats(bprev)
+    for part in PAIR:
         row_stats(part)
+    keep_stats(blast)
     zcopy(last, 1).wait()
-    send_stats(block_id(klast, qlast))
-
-    def zload(k, n):
-        kind, q = order2(k)
-        return _copy(zst.at[block_id(kind, q), n], zb.at[n], zi_sem.at[n])
-
-    zload(0, 0).start()
-    zload(0, 1).start()
-
-    def combine(b, acc):
-        _copy(st_all.at[b, pl.ds(0, 7)], st_all.at[b, pl.ds(0, 7)], st_sem.at[b]).wait()
-        top = st_all[b, 0, 0:2, :]
-        for d in range(1, 8):
-            top = jnp.maximum(top, st_all[b, d, 0:2, :])
-        s = jnp.zeros((2, LANE), F32)
-        t = jnp.zeros((2, LANE), F32)
-        for d in range(8):
-            s = s + st_all[b, d, 2:4, :] * jnp.exp(st_all[b, d, 0:2, :] - top)
-            t = t + st_all[b, d, 4:6, :]
-        comb[b, 0:2, :] = top
-        comb[b, 2:4, :] = INV / s
-        return acc + (top + jnp.log(s) - t)
-
-    token_loss = lax.fori_loop(0, NBLK, combine, jnp.zeros((2, LANE), F32))
-    loss_out[...] = jnp.full((8, LANE), jnp.sum(token_loss) * INV, F32)
-
-    gbufs = (ga, gb)
-
-    def columns(k, par, part):
-        kind, q = order2(k)
-        blk = block_id(kind, q)
-        rows = pl.ds(part * LANE, LANE)
-        (la if par == 0 else lb)[rows, :] = label_column(blk, part)
-        ml[par, rows, :] = _column(comb[blk, part : part + 1, :])
-        sl[par, rows, :] = _column(comb[blk, 2 + part : 3 + part, :])
-
-    def gradient(n, par, r, j):
-        rows = pl.ds(r, 16)
-        col = (la if par == 0 else lb)[rows, :] - (me * VOC + n * HALF + j)
-        p = jnp.exp(zb[n, rows, j : j + 1024] - _wide(ml[par, rows, :], 8)) * _wide(sl[par, rows, :], 8)
-        g = jnp.where(_wide(col, 8) == lax.broadcasted_iota(I32, (16, 1024), 1), p - INV, p)
-        gbufs[par][rows, n * HALF + j : n * HALF + j + 1024] = g.astype(BF16)
-
-    def gstore(k, par):
-        kind, q = order2(k)
-        return _copy(gbufs[par], gall.at[pl.ds(pl.multiple_of(block_id(kind, q) * BLK, BLK), BLK)], g_sem.at[par])
+    zload(1, zb, 1).start()
+    send_stats(blast)
+    second_kind, second_q = order2(jnp.int32(1))
+    second_blk = block_id(second_kind, second_q)
+    stats_arrived(second_blk)
+    loss_acc[...] += combine(second_blk)
+    for part in PAIR:
+        columns(second_blk, 1, part)
 
     def tile(ref, q, n):
         return ref.at[pl.ds(pl.multiple_of(q * LANE, LANE), LANE), pl.ds(pl.multiple_of(n * HALF, HALF), HALF)]
@@ -399,60 +461,60 @@
         _copy(tile(r1n2, q, n), bb.at[n], ab_sem.at[n * 2 + 1]).start()
 
     def pair_sum(k, n, r):
-        sbuf[n, pl.ds(r, 16), :] = pbuf[n, pl.ds(pl.multiple_of(c * LANE + r, 16), 16), :] + rbuf[k % 2, n, pl.ds(r, 16), :]
+        sbuf[n, pl.ds(r, SUB), :] = pbuf[n, pl.ds(pl.multiple_of(c * LANE + r, SUB), SUB), :] + rbuf[k % 2, n, pl.ds(r, SUB), :]
 
     def stage2_sum(n, r):
-        cb[pl.ds(r, 16), :] = ab[n, pl.ds(r, 16), :] + bb[n, pl.ds(r, 16), :]
+        cb[n, pl.ds(r, SUB), :] = ab[n, pl.ds(r, SUB), :] + bb[n, pl.ds(r, SUB), :]
 
     def rwait(k, n):
         _copy(rbuf.at[k % 2, n], rbuf.at[k % 2, n], rr.at[(k % 2) * 2 + n]).wait()
 
-    for part in range(2):
-        columns(jnp.int32(0), 0, part)
-        columns(jnp.int32(1), 1, part)
-    for n in range(2):
-        zload(0, n).wait()
-        for r in range(0, BLK, 16):
-            gradient(n, 0, r, 0)
-            gradient(n, 0, r, 1024)
-    gstore(0, 0).start()
-    zload(1, 0).start()
-    zload(1, 1).start()
+    def loss_part(k, blk):
+        loss_acc[...] += jnp.where(k < NBLK - 2, combine(blk), 0.0)
 
     def sub(k, cur):
         nxt = 1 - cur
-
-        @pl.when(k >= 1)
-        def _():
-            gstore(k - 1, nxt).wait()
+        kind2, q2 = order2((k + 2) % NBLK)
+        blk2 = block_id(kind2, q2)
 
         def trip(n):
             @pl.when(k < NBLK - 1)
             def _():
-                zload(k + 1, n).wait()
+                zload(k + 1, zb, n).wait()
 
             @pl.when(k >= 1)
             def _():
                 rwait(k - 1, n)
                 spair(k - 1, n).wait_send()
+                if n == 0:
+                    gstore(k - 1, nxt).wait()
+
+            if n == 0:
+
+                @pl.when(k < NBLK - 2)
+                def _():
+                    stats_arrived(blk2)
 
             @pl.when(k >= 12)
             def _():
                 _copy(tile(s_n2, 0, n), ab.at[n], ab_sem.at[n * 2]).wait()
                 _copy(tile(r1n2, 0, n), bb.at[n], ab_sem.at[n * 2 + 1]).wait()
 
-            @pl.when(k >= 13 - n)
-            def _():
-                _copy(cb, tile(y2, 0, n), cb_sem).wait()
+            @pl.when(k >= 13)
+            def _():
+                _copy(cb.at[n], tile(y2, 0, n), cb_sem.at[n]).wait()
 
             jobs = [[] for _ in range(32)]
             for r in range(8):
-                jobs[r // 2].append(functools.partial(pair_sum, k - 1, n, r * 16))
-                jobs[20 + r].append(functools.partial(stage2_sum, n, r * 16))
-            for r in range(32):
-                jobs[4 + r * 7 // 8].append(functools.partial(gradient, n, nxt, r // 2 * 16, r % 2 * 1024))
-            for part in range(2):
-                jobs[8 + 8 * part].append(functools.partial(columns, (k + 2) % NBLK, cur, part))
+                jobs[r // 2].append(functools.partial(pair_sum, k - 1, n, r * SUB))
+                jobs[20 + r].append(functools.partial(stage2_sum, n, r * SUB))
+            for r, job in enumerate(gradient_jobs(zb, n, nxt)):
+                jobs[4 + r * 7 // 8].append(job)
+            if n == 0:
+                jobs[8].append(lambda: loss_part(k, blk2))
+            else:
+                for part in PAIR:
+                    jobs[8 + 8 * part].append(functools.partial(columns, blk2, cur, part))
 
             def put(nt, acc):
                 pbuf[n, :, nt * PIECE : (nt + 1) * PIECE] = acc
@@ -469,7 +531,7 @@
 
             @pl.when(k < NBLK - 2)
             def _():
-                zload(k + 2, n).start()
+                zload(k + 2, zb, n).start()
 
             @pl.when(k >= 2 - n)
             def _():
@@ -481,11 +543,12 @@
 
             @pl.when(k >= 12)
             def _():
-                _copy(cb, tile(y2, k - 12, n), cb_sem).start()
+                _copy(cb.at[n], tile(y2, k - 12, n), cb_sem.at[n]).start()
 
             @pl.when((k >= 11) & (k < NBLK - 1))
             def _():
                 stage2_load(k - 11, n)
+
 
         trip(0)
         trip(1)
@@ -502,27 +565,30 @@
     lax.fori_loop(0, NBLK // 2, pair, 0)
 
     kl = jnp.int32(NBLK - 1)
-    for n in range(2):
+    for n in PAIR:
         rwait(kl, n)
         spair(kl, n).wait_send()
         if n == 0:
             sstore_done(kl - 1, 1)
         for r in range(8):
-            pair_sum(kl, n, r * 16)
+            pair_sum(kl, n, r * SUB)
         sstore_start(kl, n)
-    for n in range(2):
+    for n in PAIR:
         sstore_done(kl, n)
     gstore(kl, 1).wait()
-    _copy(cb, tile(y2, 0, 0), cb_sem).wait()
-
-    for i in range(4):
+    for n in PAIR:
+        _copy(cb.at[n], tile(y2, 0, n), cb_sem.at[n]).wait()
+
+    loss_out[...] = jnp.full(TILE, jnp.sum(loss_acc[...]) * INV, F32)
+
+    for i in FOUR:
         _copy(tile(r1a, i // 2, i % 2), tile(r1a, i // 2, i % 2), r1as.at[i]).wait()
     _copy(s_d, s_d, s1tx).wait()
     _copy(s_n1a, s_n1a, s1tx).wait()
     _copy(xall.at[pl.ds(0, 28 * LANE)], xall.at[pl.ds(0, 28 * LANE)], tx).wait()
     for d in range(7):
         _copy(lab_v.at[d], lab_v.at[d], labtx_sem).wait()
-    stats_sent()
+        _copy(st_loc, st_loc, sttx_sem).wait()
 
 
 def xrows_at(xall, dev, q):
@@ -544,7 +610,7 @@
             sd((PIECE, HID), F32),
             sd((PIECE, HID), F32),
             sd((256, HID), F32),
-            sd((8, LANE), F32),
+            sd(TILE, F32),
             sd((NBLK, 2, BLK, HALF), F32),
             sd((PIECE, HID), F32),
             sd((256, HID), F32),
@@ -561,63 +627,174 @@
             vmem((2, BLK, HALF), F32),
             vmem((2, BLK, HALF), F32),
             vmem((2, 2) + quarter, F32),
-            vmem((2,) + quarter, F32),
-            vmem((2,) + quarter, F32),
-            vmem((2,) + quarter, F32),
-            vmem(quarter, F32),
+            vmem(TWO + quarter, F32),
+            vmem(TWO + quarter, F32),
+            vmem(TWO + quarter, F32),
+            vmem(TWO + quarter, F32),
             vmem((8, 4, LANE), I32),
             vmem((BLK, LANE), I32),
             vmem((BLK, LANE), I32),
-            vmem((8, LANE), F32),
-            vmem((NBLK, 8, 8, LANE), F32),
+            vmem(TILE, F32),
+            vmem((NBLK,) + TILE, F32),
+            vmem((NBLK, 8) + TILE, F32),
             vmem((2, BLK, LANE), F32),
             vmem((2, BLK, LANE), F32),
             vmem((2, BLK, LANE), F32),
             vmem((2, BLK, LANE), F32),
-            vmem((NBLK, 8, LANE), F32),
-            dma((2,)),
+            vmem(TILE, F32),
+            vmem((2, BLK, LANE), I32),
+            vmem((2, BLK, LANE), F32),
+            vmem((2, BLK, LANE), F32),
+            vmem((2, LANE), F32),
+            dma((8,)),
             dma(()),
             dma(()),
             dma((32,)),
             dma(()),
-            dma((2,)),
-            dma((2,)),
-            dma((2,)),
+            dma(TWO),
+            dma(TWO),
+            dma(TWO),
             dma((NBLK,)),
             dma(()),
-            dma((2,)),
+            dma(TWO),
             dma((4,)),
-            dma((2,)),
-            dma((2,)),
+            dma(TWO),
+            dma(TWO),
             dma(()),
             dma((8,)),
             dma((4,)),
             dma((4,)),
-            dma(()),
-            dma((2,)),
+            dma(TWO),
+            dma(TWO),
         ],
         compiler_params=pltpu.CompilerParams(collective_id=0, has_side_effects=True, vmem_limit_bytes=67_043_328),
-        cost_estimate=pl.CostEstimate(flops=4 * TOK * HID * VOC, bytes_accessed=400 * 2**20, transcendentals=2 * TOK * VOC),
+        cost_estimate=pl.CostEstimate(flops=4 * TOK * HID * VOC, bytes_accessed=400 * MIB, transcendentals=2 * TOK * VOC),
         name="head",
     )(hid, lab, w)
 
 
-def _dhead_kernel(x_ref, g_ref, o_ref):
-    o_ref[...] = lax.dot_general(x_ref[...], g_ref[...], (((0,), (0,)), ((), ())), preferred_element_type=F32).astype(BF16)
+def _dhead_kernel(x_hbm, g_hbm, o_hbm, gv, xb, ob, x_sem, g_sem, o_sem):
+    rows = HID // PIECE
+
+    def xload(b):
+        return _copy(x_hbm.at[:, pl.ds(pl.multiple_of(b * PIECE, PIECE), PIECE)], xb.at[b % 2], x_sem.at[b % 2])
+
+    def gload(j):
+        cols = pl.ds(pl.multiple_of(j * PIECE, PIECE), PIECE)
+        return _copy(g_hbm.at[:, cols], gv.at[:, cols], g_sem.at[j])
+
+    def ostore(b, n):
+        dst = o_hbm.at[pl.ds(pl.multiple_of(b * PIECE, PIECE), PIECE), pl.ds(pl.multiple_of(n * HALF, HALF), HALF)]
+        return _copy(ob.at[n], dst, o_sem.at[n])
+
+    def dot(lhs, rhs):
+        return lax.dot_general(lhs, rhs, (((0,), (0,)), ((), ())), preferred_element_type=F32).astype(BF16)
+
+    xload(0).start()
+    gload(0).start()
+    gload(1).start()
+    xload(0).wait()
+
+    def first(j, carry):
+        gload(j).wait()
+
+        @pl.when(j < 6)
+        def _():
+            gload(j + 2).start()
+
+        @pl.when(j == 6)
+        def _():
+            xload(1).start()
+
+        cols = pl.ds(pl.multiple_of(j % 4 * PIECE, PIECE), PIECE)
+        ob[j // 4, :, cols] = dot(xb[0], gv[:, pl.ds(pl.multiple_of(j * PIECE, PIECE), PIECE)])
+        return carry
+
+    lax.fori_loop(0, 8, first, 0)
+    ostore(0, 0).start()
+    ostore(0, 1).start()
+
+    def block(b, carry):
+        xload(b).wait()
+
+        @pl.when(b < rows - 1)
+        def _():
+            xload(b + 1).start()
+
+        def half(n, carry):
+            ostore(b - 1, n).wait()
+
+            @pl.when(b < rows)
+            def _():
+                ob[n] = dot(xb[b % 2], gv[:, pl.ds(pl.multiple_of(n * HALF, HALF), HALF)])
+
+            ostore(b, n).start()
+            return carry
+
+        return lax.fori_loop(0, 2, half, carry)
+
+    lax.fori_loop(1, rows, block, 0)
+    ostore(rows - 1, 0).wait()
+    ostore(rows - 1, 1).wait()
 
 
 def _dhead(xall, gall):
-    bm, bn = PIECE, 1024
+    hbm = pl.BlockSpec(memory_space=ANY)
+    dma = pltpu.SemaphoreType.DMA
     return pl.pallas_call(
         _dhead_kernel,
-        grid=(VOC // bn, HID // bm),
-        in_specs=[pl.BlockSpec((TOK, bm), lambda j, i: (0, i)), pl.BlockSpec((TOK, bn), lambda j, i: (0, j))],
-        out_specs=pl.BlockSpec((bm, bn), lambda j, i: (i, j)),
+        in_specs=[hbm, hbm],
+        out_specs=hbm,
         out_shape=jax.ShapeDtypeStruct((HID, VOC), BF16),
-        compiler_params=pltpu.CompilerParams(vmem_limit_bytes=60 * 2**20, dimension_semantics=("arbitrary", "arbitrary")),
-        cost_estimate=pl.CostEstimate(flops=2 * TOK * HID * VOC, bytes_accessed=200 * 2**20, transcendentals=0),
+        scratch_shapes=[
+            pltpu.VMEM((TOK, VOC), BF16),
+            pltpu.VMEM((2, TOK, PIECE), BF16),
+            pltpu.VMEM((2, PIECE, HALF), BF16),
+            dma(TWO),
+            dma((8,)),
+            dma(TWO),
+        ],
+        compiler_params=pltpu.CompilerParams(vmem_limit_bytes=60 * MIB),
+        cost_estimate=pl.CostEstimate(flops=2 * TOK * HID * VOC, bytes_accessed=200 * MIB, transcendentals=0),
         name="dhead",
     )(xall, gall)
+
+
+def _final_kernel(s_ref, a_ref, b_ref, r_ref, l_ref, o_ref, loss_ref):
+    i = pl.program_id(0)
+    half = pl.num_programs(0) // 2
+
+    @pl.when(i < half)
+    def _():
+        o_ref[...] = (s_ref[...] + a_ref[...] + r_ref[...]).astype(BF16)
+
+    @pl.when(i >= half)
+    def _():
+        o_ref[...] = (s_ref[...] + b_ref[...] + r_ref[...]).astype(BF16)
+
+    loss_ref[0] = l_ref[0, 0]
+
+
+def _final(s_self, r1a, r1b, r2, loss):
+    steps = 8
+    rows = PIECE // steps
+    spec = functools.partial(pl.BlockSpec, (rows, HID))
+    return pl.pallas_call(
+        _final_kernel,
+        grid=(steps,),
+        in_specs=[
+            spec(lambda i: (i, 0)),
+            spec(lambda i: (jnp.minimum(i, steps // 2 - 1), 0)),
+            spec(lambda i: (jnp.maximum(i - steps // 2, 0), 0)),
+            spec(lambda i: (i, 0)),
+            pl.BlockSpec(TILE, lambda i: (0, 0)),
+        ],
+        out_specs=(spec(lambda i: (i, 0)), pl.BlockSpec(memory_space=pltpu.SMEM)),
+        out_shape=(jax.ShapeDtypeStruct((PIECE, HID), BF16), jax.ShapeDtypeStruct((1,), F32)),
+        compiler_params=pltpu.CompilerParams(vmem_limit_bytes=62 * MIB),
+        cost_estimate=pl.CostEstimate(flops=3 * PIECE * HID, bytes_accessed=28 * MIB, transcendentals=0),
+        name="final",
+    )(s_self, r1a, r1b, r2, loss)
 
 
 def solution(mesh):
@@ -625,10 +802,10 @@
         return (y % 2) * 4 + (x % 2) * 2 + core
 
     first, second = [], []
-    for yy in range(2):
-        for xx in range(2):
-            along_x = [(device(yy, xx, k), device(yy, xx + 1, k)) for k in range(2)]
-            along_y = [(device(yy, xx, k), device(yy + 1, xx, k)) for k in range(2)]
+    for yy in PAIR:
+        for xx in PAIR:
+            along_x = [(device(yy, xx, k), device(yy, xx + 1, k)) for k in PAIR]
+            along_y = [(device(yy, xx, k), device(yy + 1, xx, k)) for k in PAIR]
             first += [along_x[0], along_y[1]]
             second += [along_y[0], along_x[1]]
 
@@ -637,8 +814,8 @@
         r1b = lax.ppermute(s_n1b, "tp", first)
         r2 = lax.ppermute(y2, "tp", second)
         d_head = _dhead(xall, gall)
-        d_hidden = (s_self + jnp.concatenate([r1a, r1b], axis=0) + r2).astype(BF16)
-        return loss[0, :1], d_hidden, d_head
+        d_hidden, mean_loss = _final(s_self, r1a, r1b, r2, loss)
+        return mean_loss, d_hidden, d_head
 
     return jax.shard_map(
         local_step,

time: 587 us -> 487 us (0.83)
  Pallas kernels: 572 us -> 485 us
  other arithmetic: 11.4 us -> 0 us
    pallas_call x1, Pallas kernels: 420 us -> 325 us  [_head(): pl.pallas_call(_head_kernel, out_shape=(sd((TOK, HID), BF16), sd((TOK, VO...]
    convert_element_type x1 -> x0, other arithmetic: 11.4 us -> none  [local_step(): d_hidden = (s_self + jnp.concatenate([r1a, r1b], axis=0) + r2).astype(BF16)]
    pallas_call x1 -> x2, Pallas kernels: 152 us -> 161 us  [the longest x1 149 us: _dhead(): pl.pallas_call(_dhead_kernel, in_specs=[hbm, hbm], out_specs=hbm, out_sha...]
  transfers between devices with their start and end apart: 2 -> 2, of which waited for: 0 -> 0; matrix products, arithmetic and copies ran while one was open for 0% -> 0% of each run, Pallas kernels for 26% -> 31%
where the time goes in v2:
time: 487 us
  Pallas kernels  485 us (100%)
    pallas_call x1, Pallas kernels, _head(): pl.pallas_call(_head_kernel, out_shape=(sd((TOK, HID), BF16), sd((TOK, VO...  325 us
    pallas_call x1, Pallas kernels, _dhead(): pl.pallas_call(_dhead_kernel, in_specs=[hbm, hbm], out_specs=hbm, out_sha...  149 us
    pallas_call x1, Pallas kernels, _final(): pl.pallas_call(_final_kernel, grid=(steps,), in_specs=[spec(lambda i: (i,...  11.7 us
  transfers between devices with their start and end apart: 2, of which 0 were waited for; matrix products, arithmetic and copies ran while one was open for 0% of the time, Pallas kernels for 31%

profile of v2, /device:TPU:0, one launch (start us, length us, event | category | flops | bytes accessed | tf_op | source)
XLA Modules:
  0.0 487.2 jit_solution(11858592418955528326)
XLA Ops:
  0.6 324.7 %head.1 = (bf16[4096,4096]{1,0:T(8,128)(2,1)}, bf16[4096,4096]{1,0:T(8,128)(2,1)}, f32[256,4096]{1,0:T(8,128)}, f32[512,4096]{1,0:T(8,128)}, f32[512,4096]{1,0:T...) custom-call(bf16[512,4096]{1,0:T(8,128)(2,1)} %x_hbm.1, ...), custom_call_target="tpu_custom_call" | custom-call | flops 274877906944 | bytes 419430400 | tf_op jit(solution)/shard_map/head/pallas_call | solution.py:604
  325.4 0.6 collective-permute-start
  326.0 0.5 collective-permute-start.1
  326.5 148.8 %dhead.1 = bf16[4096,4096]{1,0:T(8,128)(2,1)} custom-call(bf16[4096,4096]{1,0:T(8,128)(2,1)} %get-tuple-element.19.x_hbm, bf16[4096,4096]{1,0:T(8,128)(2,1)} %get-tuple-element.20.g_hbm), custom_call_target="tpu_custom_call" | custom-call | flops 137438953472 | bytes 209715200 | tf_op jit(solution)/shard_map/dhead/pallas_call | solution.py:744
  475.4 0.0 collective-permute-done.b_ref
  475.4 0.0 collective-permute-done.1.r_ref
  475.4 11.7 %final.1 = (bf16[512,4096]{1,0:T(8,128)(2,1)}, f32[1]{0:T(128)}) custom-call(f32[512,4096]{1,0:T(8,128)} %get-tuple-element.12.s_ref, f32[256,4096]{1,0:T(8,128)} %get-tuple-element.13.a_ref, f32[256,4096]{1,0:T(8,128)} %collective-permute-done.b_ref, f32[512,4096]{1,0:T(8,128)} %collective-permute-done.1.r_ref, f32[8,128]{1,0:T(8,128)} %get-tuple-element.16.l_ref), custom_call_target="tpu_custom_call" | custom-call | flops 6291456 | bytes 29360128 | tf_op jit(solution)/shard_map/final/pallas_call | solution.py:782
Async XLA Ops:
  325.4 150.0 %collective-permute-start = (f32[256,4096]{1,0:T(8,128)}, f32[256,4096]{1,0:T(8,128)}, u32[]{:S(2)}, u32[]{:S(2)}) collective-permute-start(f32[256,4096]{1,0:T(8,128)} %get-tuple-element.14), channel_id=1, source_target_pairs={{0,2},{1,5},{2,0},{3,7},{4,6},{5,1},{6,4},{7,3}} | collective-permute-start | bytes 12582920 | tf_op jit(solution)/shard_map/ppermute | solution.py:814
  326.0 149.4 %collective-permute-start.1 = (f32[512,4096]{1,0:T(8,128)}, f32[512,4096]{1,0:T(8,128)}, u32[]{:S(2)}, u32[]{:S(2)}) collective-permute-start(f32[512,4096]{1,0:T(8,128)} %get-tuple-element.15), channel_id=1, source_target_pairs={{0,4},{1,3},{2,6},{3,1},{4,0},{5,7},{6,2},{7,5}} | collective-permute-start | bytes 25165832 | tf_op jit(solution)/shard_map/ppermute | solution.py:815

commit v3 on v2

--- a/solution.py
+++ b/solution.py
@@ -24,6 +24,7 @@
 TILE = (8, LANE)
 SUB = 16
 FOUR = range(4)
+LATE = 9
 PIECE = 512
 INV = 1.0 / TOK
 
@@ -160,6 +161,10 @@
         wait_rows(kind, q, c)
         _send(xrows(kind, q, c), xrows(kind, q, c), tx, rxs(kind, q, c), partner).start()
 
+        @pl.when(kind == n1kind)
+        def _():
+            _send(xrows(kind, q, c), xrows(kind, q, c), tx, rxs(3, q, c), n2).start()
+
     def part_load(b, part):
         kind, q = order1(b)
         return _copy(xrows(kind, q, part), xg.at[b % 2, pl.ds(pl.multiple_of(part * LANE, LANE), LANE)], xl_sem.at[b % 2])
@@ -289,7 +294,7 @@
         kprev, qprev = order1((i + NBLK - 2) % NBLK)
         kn, qn = order1((i + 1) % NBLK)
 
-        @pl.when(i == NBLK - 1)
+        @pl.when((i == LATE + 1) | (i == NBLK - 1))
         def _():
             wait_rows(kind, q, oc)
             part_load(i, oc).start()
@@ -332,13 +337,9 @@
 
             gstore(0, 0).start()
 
-        @pl.when((i >= 3) & (i < NBLK - 2))
+        @pl.when((i >= 3) & (i != LATE) & (i < NBLK - 2))
         def _():
             take_rows(kn, qn)
-
-            @pl.when(kn == n1kind)
-            def _():
-                _send(xrows(kn, qn, c), xrows(kn, qn, c), tx, rxs(3, qn, c), n2).start()
 
         jobs = [[] for _ in range(32)]
         for r in range(32):
@@ -362,12 +363,12 @@
         def _():
             send_stats(block_id(kprev, qprev))
 
-        @pl.when(i == NBLK - 2)
+        @pl.when((i == LATE) | (i == NBLK - 2))
         def _():
             take_rows(kn, qn)
             part_load(i + 1, c).start()
 
-        @pl.when(i < NBLK - 2)
+        @pl.when((i != LATE) & (i < NBLK - 2))
         def _():
             wait_rows(kn, qn, oc)
 
@@ -760,37 +761,44 @@
     )(xall, gall)
 
 
-def _final_kernel(s_ref, a_ref, b_ref, r_ref, l_ref, o_ref, loss_ref):
-    i = pl.program_id(0)
-    half = pl.num_programs(0) // 2
-
-    @pl.when(i < half)
-    def _():
-        o_ref[...] = (s_ref[...] + a_ref[...] + r_ref[...]).astype(BF16)
-
-    @pl.when(i >= half)
-    def _():
-        o_ref[...] = (s_ref[...] + b_ref[...] + r_ref[...]).astype(BF16)
-
+def _final_kernel(s_hbm, a_hbm, b_hbm, r_hbm, l_ref, o_hbm, loss_ref, terms, ov, in_sem, o_sem):
+    rows = PIECE // SUB
+
+    def chunk(ref, i):
+        return ref.at[pl.ds(pl.multiple_of(i * rows, rows), rows)]
+
+    for i in range(SUB):
+        half = (a_hbm, b_hbm)[i * 2 // SUB]
+        for t, src in enumerate((chunk(s_hbm, i), chunk(half, i % (SUB // 2)), chunk(r_hbm, i))):
+            _copy(src, chunk(terms.at[t], i), in_sem.at[t, i]).start()
     loss_ref[0] = l_ref[0, 0]
 
+    def add(i, carry):
+        for t in range(3):
+            _copy(chunk(s_hbm, i), chunk(terms.at[t], i), in_sem.at[t, i]).wait()
+        rs = pl.ds(pl.multiple_of(i * rows, rows), rows)
+        ov[rs, :] = (terms[0, rs, :] + terms[1, rs, :] + terms[2, rs, :]).astype(BF16)
+        _copy(chunk(ov, i), chunk(o_hbm, i), o_sem).start()
+        return carry
+
+    lax.fori_loop(0, SUB, add, 0)
+    _copy(ov, o_hbm, o_sem).wait()
+
 
 def _final(s_self, r1a, r1b, r2, loss):
-    steps = 8
-    rows = PIECE // steps
-    spec = functools.partial(pl.BlockSpec, (rows, HID))
+    hbm = pl.BlockSpec(memory_space=ANY)
+    dma = pltpu.SemaphoreType.DMA
     return pl.pallas_call(
         _final_kernel,
-        grid=(steps,),
-        in_specs=[
-            spec(lambda i: (i, 0)),
-            spec(lambda i: (jnp.minimum(i, steps // 2 - 1), 0)),
-            spec(lambda i: (jnp.maximum(i - steps // 2, 0), 0)),
-            spec(lambda i: (i, 0)),
-            pl.BlockSpec(TILE, lambda i: (0, 0)),
+        in_specs=[hbm] * 4 + [pl.BlockSpec(memory_space=pltpu.VMEM)],
+        out_specs=(hbm, pl.BlockSpec(memory_space=pltpu.SMEM)),
+        out_shape=(jax.ShapeDtypeStruct((PIECE, HID), BF16), jax.ShapeDtypeStruct((1,), F32)),
+        scratch_shapes=[
+            pltpu.VMEM((3, PIECE, HID), F32),
+            pltpu.VMEM((PIECE, HID), BF16),
+            dma((3, SUB)),
+            dma(()),
         ],
-        out_specs=(spec(lambda i: (i, 0)), pl.BlockSpec(memory_space=pltpu.SMEM)),
-        out_shape=(jax.ShapeDtypeStruct((PIECE, HID), BF16), jax.ShapeDtypeStruct((1,), F32)),
         compiler_params=pltpu.CompilerParams(vmem_limit_bytes=62 * MIB),
         cost_estimate=pl.CostEstimate(flops=3 * PIECE * HID, bytes_accessed=28 * MIB, transcendentals=0),
         name="final",

time: 487 us -> 487 us (level)
  no operation moved by 1% of the time
where the time goes in v3:
time: 487 us
  Pallas kernels  484 us (99%)
    pallas_call x1, Pallas kernels, _head(): pl.pallas_call(_head_kernel, out_shape=(sd((TOK, HID), BF16), sd((TOK, VO...  323 us
    pallas_call x1, Pallas kernels, _dhead(): pl.pallas_call(_dhead_kernel, in_specs=[hbm, hbm], out_specs=hbm, out_sha...  149 us
    pallas_call x1, Pallas kernels, _final(): pl.pallas_call(_final_kernel, in_specs=[hbm] * 4 + [pl.BlockSpec(memory_s...  11.9 us
  transfers between devices with their start and end apart: 2, of which 0 were waited for; matrix products, arithmetic and copies ran while one was open for 0% of the time, Pallas kernels for 31%

profile of v3, /device:TPU:0, one launch (start us, length us, event | category | flops | bytes accessed | tf_op | source)
XLA Modules:
  0.0 487.1 jit_solution(15670654968499761224)
XLA Ops:
  0.6 323.4 %head.1 = (bf16[4096,4096]{1,0:T(8,128)(2,1)}, bf16[4096,4096]{1,0:T(8,128)(2,1)}, f32[256,4096]{1,0:T(8,128)}, f32[512,4096]{1,0:T(8,128)}, f32[512,4096]{1,0:T...) custom-call(bf16[512,4096]{1,0:T(8,128)(2,1)} %x_hbm.1, ...), custom_call_target="tpu_custom_call" | custom-call | flops 274877906944 | bytes 419430400 | tf_op jit(solution)/shard_map/head/pallas_call | solution.py:605
  324.1 0.5 collective-permute-start
  324.6 1.6 collective-permute-start.1
  326.2 148.8 %dhead.1 = bf16[4096,4096]{1,0:T(8,128)(2,1)} custom-call(bf16[4096,4096]{1,0:T(8,128)(2,1)} %get-tuple-element.19.x_hbm, bf16[4096,4096]{1,0:T(8,128)(2,1)} %get-tuple-element.20.g_hbm), custom_call_target="tpu_custom_call" | custom-call | flops 137438953472 | bytes 209715200 | tf_op jit(solution)/shard_map/dhead/pallas_call | solution.py:745
  475.0 0.0 collective-permute-done.b_hbm
  475.0 0.0 collective-permute-done.1.r_hbm
  475.0 11.9 %final.1 = (bf16[512,4096]{1,0:T(8,128)(2,1)}, f32[1]{0:T(128)}) custom-call(f32[512,4096]{1,0:T(8,128)} %get-tuple-element.12.s_hbm, f32[256,4096]{1,0:T(8,128)} %get-tuple-element.13.a_hbm, f32[256,4096]{1,0:T(8,128)} %collective-permute-done.b_hbm, f32[512,4096]{1,0:T(8,128)} %collective-permute-done.1.r_hbm, f32[8,128]{1,0:T(8,128)} %get-tuple-element.16.l_ref), custom_call_target="tpu_custom_call" | custom-call | flops 6291456 | bytes 29360128 | tf_op jit(solution)/shard_map/final/pallas_call | solution.py:791
Async XLA Ops:
  324.1 150.9 %collective-permute-start = (f32[256,4096]{1,0:T(8,128)}, f32[256,4096]{1,0:T(8,128)}, u32[]{:S(2)}, u32[]{:S(2)}) collective-permute-start(f32[256,4096]{1,0:T(8,128)} %get-tuple-element.14), channel_id=1, source_target_pairs={{0,2},{1,5},{2,0},{3,7},{4,6},{5,1},{6,4},{7,3}} | collective-permute-start | bytes 12582920 | tf_op jit(solution)/shard_map/ppermute | solution.py:822
  324.6 150.5 %collective-permute-start.1 = (f32[512,4096]{1,0:T(8,128)}, f32[512,4096]{1,0:T(8,128)}, u32[]{:S(2)}, u32[]{:S(2)}) collective-permute-start(f32[512,4096]{1,0:T(8,128)} %get-tuple-element.15), channel_id=1, source_target_pairs={{0,4},{1,3},{2,6},{3,1},{4,0},{5,7},{6,2},{7,5}} | collective-permute-start | bytes 25165832 | tf_op jit(solution)/shard_map/ppermute | solution.py:823

commit v4 on v3

--- a/solution.py
+++ b/solution.py
@@ -29,6 +29,14 @@
 INV = 1.0 / TOK
 
 
+def _div(a, b):
+    return lax.div(jnp.int32(a), jnp.int32(b))
+
+
+def _rem(a, b):
+    return lax.rem(jnp.int32(a), jnp.int32(b))
+
+
 def _copy(src, dst, sem):
     return pltpu.make_async_copy(src, dst, sem)
 
@@ -82,10 +90,10 @@
     zi_sem, rr, ps, ss_sem, s1tx, r1s, r1as, ab_sem, cb_sem, g_sem,
 ):
     me = lax.axis_index("tp")
-    chip = me // 2
-    c = me % 2
-    x = chip % 2
-    y = chip // 2
+    chip = _div(me, 2)
+    c = _rem(me, 2)
+    x = _rem(chip, 2)
+    y = _div(chip, 2)
     oc = 1 - c
     partner = me + 1 - 2 * c
     dx, dy = 2 - 4 * x, 4 - 8 * y
@@ -94,15 +102,19 @@
     n1kind = 1 + c
 
     def chip_of(kind):
-        return chip + (kind % 2) * (1 - 2 * x) + (kind // 2) * (2 - 4 * y)
+        return chip + _rem(kind, 2) * (1 - 2 * x) + _div(kind, 2) * (2 - 4 * y)
+
+    def order(i, first, last):
+        a = _div(i, 4)
+        mid, end = _rem(_div(a + 1, 2), 2), _div(a, 3)
+        kind = mid * (1 + _rem(i, 2)) + first * (1 - mid) * (1 - end) + last * end
+        return kind, mid * _div(i - 4, 2) + (1 - mid) * _rem(i, 4)
 
     def order1(i):
-        mid, end = (i // 4 + 1) // 2 % 2, i // 12
-        return mid * (1 + i % 2) + 3 * end, mid * ((i - 4) // 2) + (1 - mid) * (i % 4)
+        return order(i, 0, 3)
 
     def order2(i):
-        mid, end = (i // 4 + 1) // 2 % 2, i // 12
-        return mid * (1 + i % 2) + 3 * (1 - mid) * (1 - end), mid * ((i - 4) // 2) + (1 - mid) * (i % 4)
+        return order(i, 3, 0)
 
     def block_id(kind, q):
         return chip_of(kind) * 4 + q
@@ -129,11 +141,11 @@
 
     barrier = pltpu.get_barrier_semaphore()
     for d in range(1, 8):
-        pl.semaphore_signal(barrier, inc=1, device_id={"tp": (me + d) % 8}, device_id_type=MESH)
+        pl.semaphore_signal(barrier, inc=1, device_id={"tp": _rem(me + d, 8)}, device_id_type=MESH)
     pl.semaphore_wait(barrier, 7)
 
     for d in range(1, 8):
-        _send(lab_hbm, lab_v.at[me], labtx_sem, lab_sem, (me + d) % 8).start()
+        _send(lab_hbm, lab_v.at[me], labtx_sem, lab_sem, _rem(me + d, 8)).start()
     _copy(lab_hbm, lab_v.at[me], lab_sem).start()
     for q in FOUR:
         _send(own(q), xrows(0, q, c), tx, rxs(0, q, c), partner).start()
@@ -143,7 +155,7 @@
 
     def load_x(b):
         kind, q = order1(b)
-        slot = b % 2
+        slot = _rem(b, 2)
 
         @pl.when(kind == 0)
         def _():
@@ -167,18 +179,18 @@
 
     def part_load(b, part):
         kind, q = order1(b)
-        return _copy(xrows(kind, q, part), xg.at[b % 2, pl.ds(pl.multiple_of(part * LANE, LANE), LANE)], xl_sem.at[b % 2])
+        return _copy(xrows(kind, q, part), xg.at[_rem(b, 2), pl.ds(pl.multiple_of(part * LANE, LANE), LANE)], xl_sem.at[_rem(b, 2)])
 
     def zcopy(b, h):
         kind, q = order1(b)
         return _copy(zb.at[h], zst.at[block_id(kind, q), h], zo_sem.at[h])
 
     def own_store(b):
-        slot = b % 2
-        return _copy(xg.at[slot, pl.ds(pl.multiple_of(c * LANE, LANE), LANE)], xrows(0, b % 4, c), xs_sem.at[slot])
+        slot = _rem(b, 2)
+        return _copy(xg.at[slot, pl.ds(pl.multiple_of(c * LANE, LANE), LANE)], xrows(0, _rem(b, 4), c), xs_sem.at[slot])
 
     def label_column(blk, part):
-        return _column(lab_v[2 * (blk // 4) + part, pl.ds(blk % 4, 1), :])
+        return _column(lab_v[2 * _div(blk, 4) + part, pl.ds(_rem(blk, 4), 1), :])
 
     def lane_stats(col, h, r):
         rows = pl.ds(r, 8)
@@ -210,7 +222,7 @@
 
     def send_stats(blk):
         for d in range(1, 8):
-            _send(st_loc.at[blk], st_all.at[blk, me], sttx_sem, st_sem.at[blk], (me + d) % 8).start()
+            _send(st_loc.at[blk], st_all.at[blk, me], sttx_sem, st_sem.at[blk], _rem(me + d, 8)).start()
 
     def keep_stats(blk):
         st_loc[blk] = st_new[...]
@@ -241,12 +253,12 @@
     def gradient(src, n, par, r, j):
         rows = pl.ds(pl.multiple_of(r, SUB), SUB)
         col = c_lab[par, rows, :] - (me * VOC + n * HALF + j)
-        p = jnp.exp(src[n, rows, j : j + 1024] - _wide(c_top[par, rows, :], 8)) * _wide(c_scale[par, rows, :], 8)
-        g = jnp.where(_wide(col, 8) == lax.broadcasted_iota(I32, (SUB, 1024), 1), p - INV, p)
-        gbufs[par][rows, n * HALF + j : n * HALF + j + 1024] = g.astype(BF16)
+        p = jnp.exp(src[n, rows, j : j + PIECE] - _wide(c_top[par, rows, :], 4)) * _wide(c_scale[par, rows, :], 4)
+        g = jnp.where(_wide(col, 4) == lax.broadcasted_iota(I32, (SUB, PIECE), 1), p - INV, p)
+        gbufs[par][rows, n * HALF + j : n * HALF + j + PIECE] = g.astype(BF16)
 
     def gradient_jobs(src, n, par):
-        return [functools.partial(gradient, src, n, par, r, j) for r in range(0, BLK, SUB) for j in (0, 1024)]
+        return [functools.partial(gradient, src, n, par, r, j) for r in range(0, BLK, SUB) for j in range(0, HALF, PIECE)]
 
     gbufs = (ga, gb)
 
@@ -262,7 +274,7 @@
     first_blk = block_id(first_kind, first_q)
 
     def logits(b, h, jobs):
-        slot = b % 2
+        slot = _rem(b, 2)
         def put(nt, z):
             zb[h, :, nt * PIECE : (nt + 1) * PIECE] = z
             m = z[:, :LANE]
@@ -289,10 +301,10 @@
         wcopy(j).start()
 
     def phase1(i, carry):
-        slot = i % 2
+        slot = _rem(i, 2)
         kind, q = order1(i)
-        kprev, qprev = order1((i + NBLK - 2) % NBLK)
-        kn, qn = order1((i + 1) % NBLK)
+        kprev, qprev = order1(_rem(i + NBLK - 2, NBLK))
+        kn, qn = order1(_rem(i + 1, NBLK))
 
         @pl.when((i == LATE + 1) | (i == NBLK - 1))
         def _():
@@ -329,11 +341,11 @@
                 zload(0, pbuf, n).wait()
 
                 def some(r, carry, n=n):
-                    for j in FOUR:
-                        gradient(pbuf, n, 0, r * 32 + j // 2 * SUB, j % 2 * 1024)
+                    for j in range(0, HALF, PIECE):
+                        gradient(pbuf, n, 0, r * SUB, j)
                     return carry
 
-                lax.fori_loop(0, 8, some, 0)
+                lax.fori_loop(0, SUB, some, 0)
 
             gstore(0, 0).start()
 
@@ -343,7 +355,7 @@
 
         jobs = [[] for _ in range(32)]
         for r in range(32):
-            jobs[r].append(functools.partial(lane_stats, la, 1, r * 8))
+            jobs[min(r + 1, 31)].append(functools.partial(lane_stats, la, 1, r * 8))
         for part in PAIR:
             jobs[4 + 4 * part].append(functools.partial(label_columns, block_id(kind, q), lb, part))
         logits(i, 0, jobs)
@@ -381,7 +393,7 @@
         la[...] = lb[...]
         jobs = [[] for _ in range(32)]
         for r in range(32):
-            jobs[r].append(functools.partial(lane_stats, lb, 0, r * 8))
+            jobs[min(r + 1, 31)].append(functools.partial(lane_stats, lb, 0, r * 8))
         for part in PAIR:
             jobs[8 + 8 * part].append(functools.partial(row_stats, part))
         logits(i, 1, jobs)
@@ -417,7 +429,7 @@
 
     def spair(k, n):
         return _send(
-            pbuf.at[n, pl.ds(pl.multiple_of(oc * LANE, LANE), LANE)], rbuf.at[k % 2, n], ps.at[n], rr.at[(k % 2) * 2 + n], partner
+            pbuf.at[n, pl.ds(pl.multiple_of(oc * LANE, LANE), LANE)], rbuf.at[_rem(k + 2, 2), n], ps.at[n], rr.at[_rem(k + 2, 2) * 2 + n], partner
         )
 
     def sstore_start(k, n):
@@ -430,11 +442,11 @@
 
         @pl.when((kind == n1kind) & (q < 2))
         def _():
-            _copy(sbuf.at[n], tile(s_n1a, q % 2, n), sem).start()
+            _copy(sbuf.at[n], tile(s_n1a, _rem(q, 2), n), sem).start()
 
         @pl.when((kind == n1kind) & (q >= 2))
         def _():
-            _copy(sbuf.at[n], tile(s_n1b, q % 2, n), sem).start()
+            _copy(sbuf.at[n], tile(s_n1b, _rem(q, 2), n), sem).start()
 
         @pl.when(kind == 3 - n1kind)
         def _():
@@ -454,7 +466,7 @@
 
         @pl.when((kind == n1kind) & (q < 2))
         def _():
-            _send(tile(s_n1a, q % 2, n), tile(r1a, q % 2, n), s1tx, r1as.at[(q % 2) * 2 + n], n1).start()
+            _send(tile(s_n1a, _rem(q, 2), n), tile(r1a, _rem(q, 2), n), s1tx, r1as.at[_rem(q, 2) * 2 + n], n1).start()
 
     def stage2_load(q, n):
         _copy(tile(r1n2, q, n), tile(r1n2, q, n), r1s.at[q * 2 + n]).wait()
@@ -462,20 +474,20 @@
         _copy(tile(r1n2, q, n), bb.at[n], ab_sem.at[n * 2 + 1]).start()
 
     def pair_sum(k, n, r):
-        sbuf[n, pl.ds(r, SUB), :] = pbuf[n, pl.ds(pl.multiple_of(c * LANE + r, SUB), SUB), :] + rbuf[k % 2, n, pl.ds(r, SUB), :]
+        sbuf[n, pl.ds(r, SUB), :] = pbuf[n, pl.ds(pl.multiple_of(c * LANE + r, SUB), SUB), :] + rbuf[_rem(k + 2, 2), n, pl.ds(r, SUB), :]
 
     def stage2_sum(n, r):
         cb[n, pl.ds(r, SUB), :] = ab[n, pl.ds(r, SUB), :] + bb[n, pl.ds(r, SUB), :]
 
     def rwait(k, n):
-        _copy(rbuf.at[k % 2, n], rbuf.at[k % 2, n], rr.at[(k % 2) * 2 + n]).wait()
+        _copy(rbuf.at[_rem(k + 2, 2), n], rbuf.at[_rem(k + 2, 2), n], rr.at[_rem(k + 2, 2) * 2 + n]).wait()
 
     def loss_part(k, blk):
         loss_acc[...] += jnp.where(k < NBLK - 2, combine(blk), 0.0)
 
     def sub(k, cur):
         nxt = 1 - cur
-        kind2, q2 = order2((k + 2) % NBLK)
+        kind2, q2 = order2(_rem(k + 2, NBLK))
         blk2 = block_id(kind2, q2)
 
         def trip(n):
@@ -507,10 +519,10 @@
 
             jobs = [[] for _ in range(32)]
             for r in range(8):
-                jobs[r // 2].append(functools.partial(pair_sum, k - 1, n, r * SUB))
-                jobs[20 + r].append(functools.partial(stage2_sum, n, r * SUB))
+                jobs[2 + r * 3 // 5].append(functools.partial(pair_sum, k - 1, n, r * SUB))
+                jobs[10 + r * 5 // 2].append(functools.partial(stage2_sum, n, r * SUB))
             for r, job in enumerate(gradient_jobs(zb, n, nxt)):
-                jobs[4 + r * 7 // 8].append(job)
+                jobs[2 + r * 9 // 20].append(job)
             if n == 0:
                 jobs[8].append(lambda: loss_part(k, blk2))
             else:
@@ -534,13 +546,18 @@
             def _():
                 zload(k + 2, zb, n).start()
 
-            @pl.when(k >= 2 - n)
+            @pl.when(k >= 2)
             def _():
                 sstore_done(k - 2 + n, 1 - n)
 
             @pl.when(k >= 1)
             def _():
                 sstore_start(k - 1, n)
+
+            if n == 0:
+                @pl.when(k == 1)
+                def _():
+                    sstore_done(k - 1, n)
 
             @pl.when(k >= 12)
             def _():

time: 487 us -> 483 us (level)
  no operation moved by 1% of the time
where the time goes in v4:
time: 483 us
  Pallas kernels  480 us (99%)
    pallas_call x1, Pallas kernels, _head(): pl.pallas_call(_head_kernel, out_shape=(sd((TOK, HID), BF16), sd((TOK, VO...  319 us
    pallas_call x1, Pallas kernels, _dhead(): pl.pallas_call(_dhead_kernel, in_specs=[hbm, hbm], out_specs=hbm, out_sha...  149 us
    pallas_call x1, Pallas kernels, _final(): pl.pallas_call(_final_kernel, in_specs=[hbm] * 4 + [pl.BlockSpec(memory_s...  11.9 us
  transfers between devices with their start and end apart: 2, of which 0 were waited for; matrix products, arithmetic and copies ran while one was open for 0% of the time, Pallas kernels for 31%

profile of v4, /device:TPU:0, one launch (start us, length us, event | category | flops | bytes accessed | tf_op | source)
XLA Modules:
  0.0 483.0 jit_solution(4691916483219434129)
XLA Ops:
  0.6 319.4 %head.1 = (bf16[4096,4096]{1,0:T(8,128)(2,1)}, bf16[4096,4096]{1,0:T(8,128)(2,1)}, f32[256,4096]{1,0:T(8,128)}, f32[512,4096]{1,0:T(8,128)}, f32[512,4096]{1,0:T...) custom-call(bf16[512,4096]{1,0:T(8,128)(2,1)} %x_hbm.1, ...), custom_call_target="tpu_custom_call" | custom-call | flops 274877906944 | bytes 419430400 | tf_op jit(solution)/shard_map/head/pallas_call | solution.py:622
  320.0 1.6 collective-permute-start
  321.6 0.5 collective-permute-start.1
  322.1 148.9 %dhead.1 = bf16[4096,4096]{1,0:T(8,128)(2,1)} custom-call(bf16[4096,4096]{1,0:T(8,128)(2,1)} %get-tuple-element.19.x_hbm, bf16[4096,4096]{1,0:T(8,128)(2,1)} %get-tuple-element.20.g_hbm), custom_call_target="tpu_custom_call" | custom-call | flops 137438953472 | bytes 209715200 | tf_op jit(solution)/shard_map/dhead/pallas_call | solution.py:762
  470.9 0.0 collective-permute-done.b_hbm
  470.9 0.0 collective-permute-done.1.r_hbm
  471.0 11.9 %final.1 = (bf16[512,4096]{1,0:T(8,128)(2,1)}, f32[1]{0:T(128)}) custom-call(f32[512,4096]{1,0:T(8,128)} %get-tuple-element.12.s_hbm, f32[256,4096]{1,0:T(8,128)} %get-tuple-element.13.a_hbm, f32[256,4096]{1,0:T(8,128)} %collective-permute-done.b_hbm, f32[512,4096]{1,0:T(8,128)} %collective-permute-done.1.r_hbm, f32[8,128]{1,0:T(8,128)} %get-tuple-element.16.l_ref), custom_call_target="tpu_custom_call" | custom-call | flops 6291456 | bytes 29360128 | tf_op jit(solution)/shard_map/final/pallas_call | solution.py:808
Async XLA Ops:
  320.0 150.9 %collective-permute-start = (f32[256,4096]{1,0:T(8,128)}, f32[256,4096]{1,0:T(8,128)}, u32[]{:S(2)}, u32[]{:S(2)}) collective-permute-start(f32[256,4096]{1,0:T(8,128)} %get-tuple-element.14), channel_id=1, source_target_pairs={{0,2},{1,5},{2,0},{3,7},{4,6},{5,1},{6,4},{7,3}} | collective-permute-start | bytes 12582920 | tf_op jit(solution)/shard_map/ppermute | solution.py:839
  321.6 149.3 %collective-permute-start.1 = (f32[512,4096]{1,0:T(8,128)}, f32[512,4096]{1,0:T(8,128)}, u32[]{:S(2)}, u32[]{:S(2)}) collective-permute-start(f32[512,4096]{1,0:T(8,128)} %get-tuple-element.15), channel_id=1, source_target_pairs={{0,4},{1,3},{2,6},{3,1},{4,0},{5,7},{6,2},{7,5}} | collective-permute-start | bytes 25165832 | tf_op jit(solution)/shard_map/ppermute | solution.py:840

commit v5 on v4

--- a/solution.py
+++ b/solution.py
@@ -24,6 +24,7 @@
 TILE = (8, LANE)
 SUB = 16
 FOUR = range(4)
+CORNER = 6
 LATE = 9
 PIECE = 512
 INV = 1.0 / TOK
@@ -35,6 +36,14 @@
 
 def _rem(a, b):
     return lax.rem(jnp.int32(a), jnp.int32(b))
+
+
+def _odd(a):
+    return _rem(a, 2)
+
+
+def _half(a):
+    return _div(a, 2)
 
 
 def _copy(src, dst, sem):
@@ -90,10 +99,10 @@
     zi_sem, rr, ps, ss_sem, s1tx, r1s, r1as, ab_sem, cb_sem, g_sem,
 ):
     me = lax.axis_index("tp")
-    chip = _div(me, 2)
-    c = _rem(me, 2)
-    x = _rem(chip, 2)
-    y = _div(chip, 2)
+    chip = _half(me)
+    c = _odd(me)
+    x = _odd(chip)
+    y = _half(chip)
     oc = 1 - c
     partner = me + 1 - 2 * c
     dx, dy = 2 - 4 * x, 4 - 8 * y
@@ -102,13 +111,13 @@
     n1kind = 1 + c
 
     def chip_of(kind):
-        return chip + _rem(kind, 2) * (1 - 2 * x) + _div(kind, 2) * (2 - 4 * y)
+        return chip + _odd(kind) * (1 - 2 * x) + _half(kind) * (2 - 4 * y)
 
     def order(i, first, last):
         a = _div(i, 4)
-        mid, end = _rem(_div(a + 1, 2), 2), _div(a, 3)
-        kind = mid * (1 + _rem(i, 2)) + first * (1 - mid) * (1 - end) + last * end
-        return kind, mid * _div(i - 4, 2) + (1 - mid) * _rem(i, 4)
+        mid, end = _rem(_half(a + 1), 2), _div(a, 3)
+        kind = mid * (1 + _odd(i)) + first * (1 - mid) * (1 - end) + last * end
+        return kind, mid * _half(i - 4) + (1 - mid) * _rem(i, 4)
 
     def order1(i):
         return order(i, 0, 3)
@@ -155,7 +164,7 @@
 
     def load_x(b):
         kind, q = order1(b)
-        slot = _rem(b, 2)
+        slot = _odd(b)
 
         @pl.when(kind == 0)
         def _():
@@ -179,14 +188,14 @@
 
     def part_load(b, part):
         kind, q = order1(b)
-        return _copy(xrows(kind, q, part), xg.at[_rem(b, 2), pl.ds(pl.multiple_of(part * LANE, LANE), LANE)], xl_sem.at[_rem(b, 2)])
+        return _copy(xrows(kind, q, part), xg.at[_odd(b), pl.ds(pl.multiple_of(part * LANE, LANE), LANE)], xl_sem.at[_odd(b)])
 
     def zcopy(b, h):
         kind, q = order1(b)
         return _copy(zb.at[h], zst.at[block_id(kind, q), h], zo_sem.at[h])
 
     def own_store(b):
-        slot = _rem(b, 2)
+        slot = _odd(b)
         return _copy(xg.at[slot, pl.ds(pl.multiple_of(c * LANE, LANE), LANE)], xrows(0, _rem(b, 4), c), xs_sem.at[slot])
 
     def label_column(blk, part):
@@ -274,7 +283,7 @@
     first_blk = block_id(first_kind, first_q)
 
     def logits(b, h, jobs):
-        slot = _rem(b, 2)
+        slot = _odd(b)
         def put(nt, z):
             zb[h, :, nt * PIECE : (nt + 1) * PIECE] = z
             m = z[:, :LANE]
@@ -301,7 +310,7 @@
         wcopy(j).start()
 
     def phase1(i, carry):
-        slot = _rem(i, 2)
+        slot = _odd(i)
         kind, q = order1(i)
         kprev, qprev = order1(_rem(i + NBLK - 2, NBLK))
         kn, qn = order1(_rem(i + 1, NBLK))
@@ -429,7 +438,7 @@
 
     def spair(k, n):
         return _send(
-            pbuf.at[n, pl.ds(pl.multiple_of(oc * LANE, LANE), LANE)], rbuf.at[_rem(k + 2, 2), n], ps.at[n], rr.at[_rem(k + 2, 2) * 2 + n], partner
+            pbuf.at[n, pl.ds(pl.multiple_of(oc * LANE, LANE), LANE)], rbuf.at[_odd(k + 2), n], ps.at[n], rr.at[_odd(k + 2) * 2 + n], partner
         )
 
     def sstore_start(k, n):
@@ -442,11 +451,11 @@
 
         @pl.when((kind == n1kind) & (q < 2))
         def _():
-            _copy(sbuf.at[n], tile(s_n1a, _rem(q, 2), n), sem).start()
+            _copy(sbuf.at[n], tile(s_n1a, _odd(q), n), sem).start()
 
         @pl.when((kind == n1kind) & (q >= 2))
         def _():
-            _copy(sbuf.at[n], tile(s_n1b, _rem(q, 2), n), sem).start()
+            _copy(sbuf.at[n], tile(s_n1b, _odd(q), n), sem).start()
 
         @pl.when(kind == 3 - n1kind)
         def _():
@@ -466,7 +475,7 @@
 
         @pl.when((kind == n1kind) & (q < 2))
         def _():
-            _send(tile(s_n1a, _rem(q, 2), n), tile(r1a, _rem(q, 2), n), s1tx, r1as.at[_rem(q, 2) * 2 + n], n1).start()
+            _send(tile(s_n1a, _odd(q), n), tile(r1a, _odd(q), n), s1tx, r1as.at[_odd(q) * 2 + n], n1).start()
 
     def stage2_load(q, n):
         _copy(tile(r1n2, q, n), tile(r1n2, q, n), r1s.at[q * 2 + n]).wait()
@@ -474,13 +483,13 @@
         _copy(tile(r1n2, q, n), bb.at[n], ab_sem.at[n * 2 + 1]).start()
 
     def pair_sum(k, n, r):
-        sbuf[n, pl.ds(r, SUB), :] = pbuf[n, pl.ds(pl.multiple_of(c * LANE + r, SUB), SUB), :] + rbuf[_rem(k + 2, 2), n, pl.ds(r, SUB), :]
+        sbuf[n, pl.ds(r, SUB), :] = pbuf[n, pl.ds(pl.multiple_of(c * LANE + r, SUB), SUB), :] + rbuf[_odd(k + 2), n, pl.ds(r, SUB), :]
 
     def stage2_sum(n, r):
         cb[n, pl.ds(r, SUB), :] = ab[n, pl.ds(r, SUB), :] + bb[n, pl.ds(r, SUB), :]
 
     def rwait(k, n):
-        _copy(rbuf.at[_rem(k + 2, 2), n], rbuf.at[_rem(k + 2, 2), n], rr.at[_rem(k + 2, 2) * 2 + n]).wait()
+        _copy(rbuf.at[_odd(k + 2), n], rbuf.at[_odd(k + 2), n], rr.at[_odd(k + 2) * 2 + n]).wait()
 
     def loss_part(k, blk):
         loss_acc[...] += jnp.where(k < NBLK - 2, combine(blk), 0.0)
@@ -691,69 +700,99 @@
     )(hid, lab, w)
 
 
+def _outer(lhs, rhs):
+    return lax.dot_general(lhs, rhs, (((0,), (0,)), ((), ())), preferred_element_type=F32).astype(BF16)
+
+
+def _cols(j, width=PIECE):
+    return pl.ds(pl.multiple_of(j * width, width), width)
+
+
 def _dhead_kernel(x_hbm, g_hbm, o_hbm, gv, xb, ob, x_sem, g_sem, o_sem):
-    rows = HID // PIECE
+    blocks = HID // PIECE
 
     def xload(b):
-        return _copy(x_hbm.at[:, pl.ds(pl.multiple_of(b * PIECE, PIECE), PIECE)], xb.at[b % 2], x_sem.at[b % 2])
+        return _copy(x_hbm.at[:, _cols(b)], xb.at[_odd(b)], x_sem.at[_odd(b)])
 
     def gload(j):
-        cols = pl.ds(pl.multiple_of(j * PIECE, PIECE), PIECE)
-        return _copy(g_hbm.at[:, cols], gv.at[:, cols], g_sem.at[j])
+        return _copy(g_hbm.at[:, _cols(j)], gv.at[:, _cols(j)], g_sem.at[j])
 
     def ostore(b, n):
-        dst = o_hbm.at[pl.ds(pl.multiple_of(b * PIECE, PIECE), PIECE), pl.ds(pl.multiple_of(n * HALF, HALF), HALF)]
-        return _copy(ob.at[n], dst, o_sem.at[n])
-
-    def dot(lhs, rhs):
-        return lax.dot_general(lhs, rhs, (((0,), (0,)), ((), ())), preferred_element_type=F32).astype(BF16)
+        return _copy(ob.at[n], o_hbm.at[_cols(b), _cols(n, HALF)], o_sem.at[n])
+
+    def short_store(b):
+        return _copy(ob.at[1, :, pl.ds(0, 2 * PIECE)], o_hbm.at[_cols(b), pl.ds(HALF, 2 * PIECE)], o_sem.at[1])
+
+    def stored(b, n):
+        short = (b >= CORNER) & (n == 1)
+        pl.when(short)(lambda: short_store(b).wait())
+        pl.when(jnp.logical_not(short))(lambda: ostore(b, n).wait())
+
+    def piece(b, j):
+        ob[_div(j, 4), :, _cols(_rem(j, 4))] = _outer(xb[_odd(b)], gv[:, _cols(j)])
 
     xload(0).start()
     gload(0).start()
     gload(1).start()
-    xload(0).wait()
-
-    def first(j, carry):
-        gload(j).wait()
-
-        @pl.when(j < 6)
-        def _():
-            gload(j + 2).start()
-
-        @pl.when(j == 6)
-        def _():
-            xload(1).start()
-
-        cols = pl.ds(pl.multiple_of(j % 4 * PIECE, PIECE), PIECE)
-        ob[j // 4, :, cols] = dot(xb[0], gv[:, pl.ds(pl.multiple_of(j * PIECE, PIECE), PIECE)])
-        return carry
-
-    lax.fori_loop(0, 8, first, 0)
-    ostore(0, 0).start()
-    ostore(0, 1).start()
 
     def block(b, carry):
         xload(b).wait()
 
-        @pl.when(b < rows - 1)
+        @pl.when((b > 0) & (b < blocks - 1))
         def _():
             xload(b + 1).start()
 
         def half(n, carry):
-            ostore(b - 1, n).wait()
-
-            @pl.when(b < rows)
-            def _():
-                ob[n] = dot(xb[b % 2], gv[:, pl.ds(pl.multiple_of(n * HALF, HALF), HALF)])
+            stored(b - 1, n)
+
+            @pl.when(b < blocks)
+            def _():
+                ob[n] = _outer(xb[_odd(b)], gv[:, _cols(n, HALF)])
 
             ostore(b, n).start()
             return carry
 
-        return lax.fori_loop(0, 2, half, carry)
-
-    lax.fori_loop(1, rows, block, 0)
-    ostore(rows - 1, 0).wait()
-    ostore(rows - 1, 1).wait()
+        lax.fori_loop(0, jnp.where(b == 0, 0, jnp.where(b < CORNER, 2, 1)), half, 0)
+
+        @pl.when(b >= CORNER)
+        def _():
+            stored(b - 1, 1)
+
+        def small(j, carry):
+            @pl.when(b == 0)
+            def _():
+                gload(j).wait()
+
+                @pl.when(j < 6)
+                def _():
+                    gload(j + 2).start()
+
+                @pl.when(j == 6)
+                def _():
+                    xload(1).start()
+
+            pl.when(b < blocks)(lambda: piece(b, j))
+            return carry
+
+        part = (b == 0) | (b >= CORNER)
+        low = jnp.where(b == 0, 0, 4)
+        lax.fori_loop(low, jnp.where(part, jnp.where(b == 0, 8, 6), low), small, 0)
+
+        @pl.when(b == 0)
+        def _():
+            ostore(0, 0).start()
+            ostore(0, 1).start()
+
+        @pl.when(b >= CORNER)
+        def _():
+            short_store(b).start()
+
+        return carry
+
+    lax.fori_loop(0, blocks, block, 0)
+    last = jnp.int32(blocks - 1)
+    stored(last, 0)
+    stored(last, 1)
 
 
 def _dhead(xall, gall):
@@ -778,48 +817,113 @@
     )(xall, gall)
 
 
-def _final_kernel(s_hbm, a_hbm, b_hbm, r_hbm, l_ref, o_hbm, loss_ref, terms, ov, in_sem, o_sem):
-    rows = PIECE // SUB
+def _tail_kernel(
+    x_hbm, g_hbm, d_hbm, s_hbm, a_hbm, b_hbm, r_hbm, l_ref, do_hbm, o_hbm, loss_ref,
+    gv, xb, ob, terms, ov, x_sem, g_sem, d_sem, in_sem, o_sem,
+):
+    steps = 2 * (HID // PIECE - CORNER)
+    rows = PIECE // steps
+
+    def xload(b):
+        return _copy(x_hbm.at[:, _cols(CORNER + b)], xb.at[_odd(b)], x_sem.at[_odd(b)])
+
+    def gload(j):
+        return _copy(g_hbm.at[:, _cols(6 + j)], gv.at[:, _cols(j)], g_sem.at[j])
+
+    def dstore(m):
+        dst = do_hbm.at[_cols(CORNER + _half(m)), _cols(6 + _odd(m))]
+        return _copy(ob.at[_odd(m)], dst, d_sem.at[_odd(m)])
 
     def chunk(ref, i):
-        return ref.at[pl.ds(pl.multiple_of(i * rows, rows), rows)]
-
-    for i in range(SUB):
-        half = (a_hbm, b_hbm)[i * 2 // SUB]
-        for t, src in enumerate((chunk(s_hbm, i), chunk(half, i % (SUB // 2)), chunk(r_hbm, i))):
+        return ref.at[_cols(i, rows)]
+
+    def load_terms(i):
+        half = (a_hbm, b_hbm)[i * 2 // steps]
+        for t, src in enumerate((chunk(s_hbm, i), chunk(half, i % (steps // 2)), chunk(r_hbm, i))):
             _copy(src, chunk(terms.at[t], i), in_sem.at[t, i]).start()
+
+    xload(0).start()
+    gload(0).start()
+    load_terms(0)
+    gload(1).start()
+    xload(1).start()
+    for i in range(1, steps):
+        load_terms(i)
     loss_ref[0] = l_ref[0, 0]
 
-    def add(i, carry):
+    def add(i):
         for t in range(3):
             _copy(chunk(s_hbm, i), chunk(terms.at[t], i), in_sem.at[t, i]).wait()
-        rs = pl.ds(pl.multiple_of(i * rows, rows), rows)
-        ov[rs, :] = (terms[0, rs, :] + terms[1, rs, :] + terms[2, rs, :]).astype(BF16)
+        for r in range(0, rows, SUB):
+            rs = pl.ds(pl.multiple_of(i * rows + r, SUB), SUB)
+            ov[rs, :] = (terms[0, rs, :] + terms[1, rs, :] + terms[2, rs, :]).astype(BF16)
         _copy(chunk(ov, i), chunk(o_hbm, i), o_sem).start()
+
+    def step(m, carry):
+        b, j = _half(m), _odd(m)
+
+        @pl.when(j == 0)
+        def _():
+            xload(b).wait()
+
+        @pl.when(b == 0)
+        def _():
+            gload(j).wait()
+
+        @pl.when(m > 1)
+        def _():
+            dstore(m - 2).wait()
+
+        @pl.when(m < steps)
+        def _():
+            ob[j] = _outer(xb[_odd(b)], gv[:, _cols(j)])
+
+        dstore(m).start()
+
+        @pl.when((j == 1) & (m < steps - 3))
+        def _():
+            xload(b + 2).start()
+
+        pl.when(m > 0)(lambda: add(m - 1))
         return carry
 
-    lax.fori_loop(0, SUB, add, 0)
+    lax.fori_loop(0, steps, step, 0)
+    add(jnp.int32(steps - 1))
+    dstore(steps - 2).wait()
+    dstore(steps - 1).wait()
     _copy(ov, o_hbm, o_sem).wait()
 
 
-def _final(s_self, r1a, r1b, r2, loss):
+def _tail(xall, gall, d_head, s_self, r1a, r1b, r2, loss):
     hbm = pl.BlockSpec(memory_space=ANY)
     dma = pltpu.SemaphoreType.DMA
+    steps = 2 * (HID // PIECE - CORNER)
     return pl.pallas_call(
-        _final_kernel,
-        in_specs=[hbm] * 4 + [pl.BlockSpec(memory_space=pltpu.VMEM)],
-        out_specs=(hbm, pl.BlockSpec(memory_space=pltpu.SMEM)),
-        out_shape=(jax.ShapeDtypeStruct((PIECE, HID), BF16), jax.ShapeDtypeStruct((1,), F32)),
+        _tail_kernel,
+        in_specs=[hbm] * 7 + [pl.BlockSpec(memory_space=pltpu.VMEM)],
+        out_specs=(hbm, hbm, pl.BlockSpec(memory_space=pltpu.SMEM)),
+        out_shape=(
+            jax.ShapeDtypeStruct((HID, VOC), BF16),
+            jax.ShapeDtypeStruct((PIECE, HID), BF16),
+            jax.ShapeDtypeStruct((1,), F32),
+        ),
+        input_output_aliases={2: 0},
         scratch_shapes=[
+            pltpu.VMEM((TOK, 2 * PIECE), BF16),
+            pltpu.VMEM((2, TOK, PIECE), BF16),
+            pltpu.VMEM((2, PIECE, PIECE), BF16),
             pltpu.VMEM((3, PIECE, HID), F32),
             pltpu.VMEM((PIECE, HID), BF16),
-            dma((3, SUB)),
+            dma(TWO),
+            dma(TWO),
+            dma(TWO),
+            dma((3, steps)),
             dma(()),
         ],
         compiler_params=pltpu.CompilerParams(vmem_limit_bytes=62 * MIB),
-        cost_estimate=pl.CostEstimate(flops=3 * PIECE * HID, bytes_accessed=28 * MIB, transcendentals=0),
-        name="final",
-    )(s_self, r1a, r1b, r2, loss)
+        cost_estimate=pl.CostEstimate(flops=TOK * HID * VOC // 8, bytes_accessed=46 * MIB, transcendentals=0),
+        name="tail",
+    )(xall, gall, d_head, s_self, r1a, r1b, r2, loss)
 
 
 def solution(mesh):
@@ -839,7 +943,7 @@
         r1b = lax.ppermute(s_n1b, "tp", first)
         r2 = lax.ppermute(y2, "tp", second)
         d_head = _dhead(xall, gall)
-        d_hidden, mean_loss = _final(s_self, r1a, r1b, r2, loss)
+        d_head, d_hidden, mean_loss = _tail(xall, gall, d_head, s_self, r1a, r1b, r2, loss)
         return mean_loss, d_hidden, d_head
 
     return jax.shard_map(

time: 483 us -> 485 us (level)
    pallas_call x1, Pallas kernels: 11.9 us -> 22.4 us  [_tail(): pl.pallas_call(_tail_kernel, in_specs=[hbm] * 7 + [pl.BlockSpec(memory_sp...]
    pallas_call x1, Pallas kernels: 149 us -> 140 us  [_dhead(): pl.pallas_call(_dhead_kernel, in_specs=[hbm, hbm], out_specs=hbm, out_sha...]
  transfers between devices with their start and end apart: 2 -> 2, of which waited for: 0 -> 0; matrix products, arithmetic and copies ran while one was open for 0% -> 0% of each run, Pallas kernels for 31% -> 29%
where the time goes in v5:
time: 485 us
  Pallas kernels  482 us (99%)
    pallas_call x1, Pallas kernels, _head(): pl.pallas_call(_head_kernel, out_shape=(sd((TOK, HID), BF16), sd((TOK, VO...  319 us
    pallas_call x1, Pallas kernels, _dhead(): pl.pallas_call(_dhead_kernel, in_specs=[hbm, hbm], out_specs=hbm, out_sha...  140 us
    pallas_call x1, Pallas kernels, _tail(): pl.pallas_call(_tail_kernel, in_specs=[hbm] * 7 + [pl.BlockSpec(memory_sp...  22.4 us
  transfers between devices with their start and end apart: 2, of which 0 were waited for; matrix products, arithmetic and copies ran while one was open for 0% of the time, Pallas kernels for 29%

profile of v5, /device:TPU:0, one launch (start us, length us, event | category | flops | bytes accessed | tf_op | source)
XLA Modules:
  0.0 485.1 jit_solution(1124432285893660031)
XLA Ops:
  0.6 319.4 %head.1 = (bf16[4096,4096]{1,0:T(8,128)(2,1)}, bf16[4096,4096]{1,0:T(8,128)(2,1)}, f32[256,4096]{1,0:T(8,128)}, f32[512,4096]{1,0:T(8,128)}, f32[512,4096]{1,0:T...) custom-call(bf16[512,4096]{1,0:T(8,128)(2,1)} %x_hbm.1, ...), custom_call_target="tpu_custom_call" | custom-call | flops 274877906944 | bytes 419430400 | tf_op jit(solution)/shard_map/head/pallas_call | solution.py:631
  320.0 1.6 collective-permute-start
  321.6 0.5 collective-permute-start.1
  322.1 140.4 %dhead.1.d_hbm = bf16[4096,4096]{1,0:T(8,128)(2,1)} custom-call(bf16[4096,4096]{1,0:T(8,128)(2,1)} %get-tuple-element.13.x_hbm, bf16[4096,4096]{1,0:T(8,128)(2,1)} %get-tuple-element.14.g_hbm), custom_call_target="tpu_custom_call" | custom-call | flops 137438953472 | bytes 209715200 | tf_op jit(solution)/shard_map/dhead/pallas_call | solution.py:801
  462.5 0.0 collective-permute-done.b_hbm
  462.5 0.0 collective-permute-done.1.r_hbm
  462.5 22.4 %tail.1 = (bf16[4096,4096]{1,0:T(8,128)(2,1)}, bf16[512,4096]{1,0:T(8,128)(2,1)}, f32[1]{0:T(128)}) custom-call(bf16[4096,4096]{1,0:T(8,128)(2,1)} %get-tuple-element.13.x_hbm, bf16[4096,4096]{1,0:T(8,128)(2,1)} %get-tuple-element.14.g_hbm, bf16[4096,4096]{1,0:T(8,128)(2,1)} %dhead.1.d_hbm, ...), custom_call_target="tpu_custom_call", output_to_operand_aliasing={{0}: (2, {})} | custom-call | flops 8589934592 | bytes 48234496 | tf_op jit(solution)/shard_map/tail/pallas_call | solution.py:901
Async XLA Ops:
  320.0 142.5 %collective-permute-start = (f32[256,4096]{1,0:T(8,128)}, f32[256,4096]{1,0:T(8,128)}, u32[]{:S(2)}, u32[]{:S(2)}) collective-permute-start(f32[256,4096]{1,0:T(8,128)} %get-tuple-element.17), channel_id=1, source_target_pairs={{0,2},{1,5},{2,0},{3,7},{4,6},{5,1},{6,4},{7,3}} | collective-permute-start | bytes 12582920 | tf_op jit(solution)/shard_map/ppermute | solution.py:943
  321.6 140.9 %collective-permute-start.1 = (f32[512,4096]{1,0:T(8,128)}, f32[512,4096]{1,0:T(8,128)}, u32[]{:S(2)}, u32[]{:S(2)}) collective-permute-start(f32[512,4096]{1,0:T(8,128)} %get-tuple-element.18), channel_id=1, source_target_pairs={{0,4},{1,3},{2,6},{3,1},{4,0},{5,7},{6,2},{7,5}} | collective-permute-start | bytes 25165832 | tf_op jit(solution)/shard_map/ppermute | solution.py:944

commit v6 on v5

--- a/solution.py
+++ b/solution.py
@@ -733,7 +733,6 @@
 
     xload(0).start()
     gload(0).start()
-    gload(1).start()
 
     def block(b, carry):
         xload(b).wait()
@@ -762,6 +761,10 @@
             @pl.when(b == 0)
             def _():
                 gload(j).wait()
+
+                @pl.when(j == 0)
+                def _():
+                    gload(1).start()
 
                 @pl.when(j < 6)
                 def _():
@@ -838,17 +841,14 @@
         return ref.at[_cols(i, rows)]
 
     def load_terms(i):
-        half = (a_hbm, b_hbm)[i * 2 // steps]
-        for t, src in enumerate((chunk(s_hbm, i), chunk(half, i % (steps // 2)), chunk(r_hbm, i))):
-            _copy(src, chunk(terms.at[t], i), in_sem.at[t, i]).start()
+        _copy(chunk(s_hbm, i), chunk(terms.at[0], i), in_sem.at[0, i]).start()
+        _copy(chunk(r_hbm, i), chunk(terms.at[2], i), in_sem.at[2, i]).start()
+        row = _rem(i, steps // 2)
+        pl.when(i < steps // 2)(lambda: _copy(chunk(a_hbm, row), chunk(terms.at[1], i), in_sem.at[1, i]).start())
+        pl.when(i >= steps // 2)(lambda: _copy(chunk(b_hbm, row), chunk(terms.at[1], i), in_sem.at[1, i]).start())
 
     xload(0).start()
     gload(0).start()
-    load_terms(0)
-    gload(1).start()
-    xload(1).start()
-    for i in range(1, steps):
-        load_terms(i)
     loss_ref[0] = l_ref[0, 0]
 
     def add(i):
@@ -869,6 +869,16 @@
         @pl.when(b == 0)
         def _():
             gload(j).wait()
+
+        @pl.when(m == 0)
+        def _():
+            gload(1).start()
+
+        @pl.when(m == 1)
+        def _():
+            xload(1).start()
+
+        load_terms(m)
 
         @pl.when(m > 1)
         def _():

time: 485 us -> 484 us (level)
  no operation moved by 1% of the time
where the time goes in v6:
time: 484 us
  Pallas kernels  481 us (99%)
    pallas_call x1, Pallas kernels, _head(): pl.pallas_call(_head_kernel, out_shape=(sd((TOK, HID), BF16), sd((TOK, VO...  319 us
    pallas_call x1, Pallas kernels, _dhead(): pl.pallas_call(_dhead_kernel, in_specs=[hbm, hbm], out_specs=hbm, out_sha...  140 us
    pallas_call x1, Pallas kernels, _tail(): pl.pallas_call(_tail_kernel, in_specs=[hbm] * 7 + [pl.BlockSpec(memory_sp...  20.9 us
  transfers between devices with their start and end apart: 2, of which 0 were waited for; matrix products, arithmetic and copies ran while one was open for 0% of the time, Pallas kernels for 29%

profile of v6, /device:TPU:0, one launch (start us, length us, event | category | flops | bytes accessed | tf_op | source)
XLA Modules:
  0.0 483.6 jit_solution(2675427971342076830)
XLA Ops:
  0.6 319.4 %head.1 = (bf16[4096,4096]{1,0:T(8,128)(2,1)}, bf16[4096,4096]{1,0:T(8,128)(2,1)}, f32[256,4096]{1,0:T(8,128)}, f32[512,4096]{1,0:T(8,128)}, f32[512,4096]{1,0:T...) custom-call(bf16[512,4096]{1,0:T(8,128)(2,1)} %x_hbm.1, ...), custom_call_target="tpu_custom_call" | custom-call | flops 274877906944 | bytes 419430400 | tf_op jit(solution)/shard_map/head/pallas_call | solution.py:631
  320.0 1.6 collective-permute-start
  321.6 0.5 collective-permute-start.1
  322.1 140.4 %dhead.1.d_hbm = bf16[4096,4096]{1,0:T(8,128)(2,1)} custom-call(bf16[4096,4096]{1,0:T(8,128)(2,1)} %get-tuple-element.13.x_hbm, bf16[4096,4096]{1,0:T(8,128)(2,1)} %get-tuple-element.14.g_hbm), custom_call_target="tpu_custom_call" | custom-call | flops 137438953472 | bytes 209715200 | tf_op jit(solution)/shard_map/dhead/pallas_call | solution.py:804
  462.5 0.0 collective-permute-done.b_hbm
  462.5 0.0 collective-permute-done.1.r_hbm
  462.5 20.9 %tail.1 = (bf16[4096,4096]{1,0:T(8,128)(2,1)}, bf16[512,4096]{1,0:T(8,128)(2,1)}, f32[1]{0:T(128)}) custom-call(bf16[4096,4096]{1,0:T(8,128)(2,1)} %get-tuple-element.13.x_hbm, bf16[4096,4096]{1,0:T(8,128)(2,1)} %get-tuple-element.14.g_hbm, bf16[4096,4096]{1,0:T(8,128)(2,1)} %dhead.1.d_hbm, ...), custom_call_target="tpu_custom_call", output_to_operand_aliasing={{0}: (2, {})} | custom-call | flops 8589934592 | bytes 48234496 | tf_op jit(solution)/shard_map/tail/pallas_call | solution.py:911
Async XLA Ops:
  320.0 142.5 %collective-permute-start = (f32[256,4096]{1,0:T(8,128)}, f32[256,4096]{1,0:T(8,128)}, u32[]{:S(2)}, u32[]{:S(2)}) collective-permute-start(f32[256,4096]{1,0:T(8,128)} %get-tuple-element.17), channel_id=1, source_target_pairs={{0,2},{1,5},{2,0},{3,7},{4,6},{5,1},{6,4},{7,3}} | collective-permute-start | bytes 12582920 | tf_op jit(solution)/shard_map/ppermute | solution.py:953
  321.6 140.9 %collective-permute-start.1 = (f32[512,4096]{1,0:T(8,128)}, f32[512,4096]{1,0:T(8,128)}, u32[]{:S(2)}, u32[]{:S(2)}) collective-permute-start(f32[512,4096]{1,0:T(8,128)} %get-tuple-element.18), channel_id=1, source_target_pairs={{0,4},{1,3},{2,6},{3,1},{4,0},{5,7},{6,2},{7,5}} | collective-permute-start | bytes 25165832 | tf_op jit(solution)/shard_map/ppermute | solution.py:954

commit v7 on v4

--- a/solution.py
+++ b/solution.py
@@ -710,8 +710,8 @@
 
     xload(0).start()
     gload(0).start()
+    xload(0).wait()
     gload(1).start()
-    xload(0).wait()
 
     def first(j, carry):
         gload(j).wait()
@@ -726,10 +726,14 @@
 
         cols = pl.ds(pl.multiple_of(j % 4 * PIECE, PIECE), PIECE)
         ob[j // 4, :, cols] = dot(xb[0], gv[:, pl.ds(pl.multiple_of(j * PIECE, PIECE), PIECE)])
+
+        @pl.when(j == 3)
+        def _():
+            ostore(0, 0).start()
+
         return carry
 
     lax.fori_loop(0, 8, first, 0)
-    ostore(0, 0).start()
     ostore(0, 1).start()
 
     def block(b, carry):
@@ -780,19 +784,29 @@
 
 def _final_kernel(s_hbm, a_hbm, b_hbm, r_hbm, l_ref, o_hbm, loss_ref, terms, ov, in_sem, o_sem):
     rows = PIECE // SUB
+    ahead = 6
 
     def chunk(ref, i):
         return ref.at[pl.ds(pl.multiple_of(i * rows, rows), rows)]
 
-    for i in range(SUB):
-        half = (a_hbm, b_hbm)[i * 2 // SUB]
-        for t, src in enumerate((chunk(s_hbm, i), chunk(half, i % (SUB // 2)), chunk(r_hbm, i))):
-            _copy(src, chunk(terms.at[t], i), in_sem.at[t, i]).start()
+    def load(i):
+        row = _rem(i, SUB // 2)
+        _copy(chunk(s_hbm, i), chunk(terms.at[0], i), in_sem.at[0, i]).start()
+        pl.when(i < SUB // 2)(lambda: _copy(chunk(a_hbm, row), chunk(terms.at[1], i), in_sem.at[1, i]).start())
+        pl.when(i >= SUB // 2)(lambda: _copy(chunk(b_hbm, row), chunk(terms.at[1], i), in_sem.at[1, i]).start())
+        _copy(chunk(r_hbm, i), chunk(terms.at[2], i), in_sem.at[2, i]).start()
+
+    def first(i, carry):
+        load(i)
+        return carry
+
+    lax.fori_loop(0, ahead, first, 0)
     loss_ref[0] = l_ref[0, 0]
 
     def add(i, carry):
         for t in range(3):
             _copy(chunk(s_hbm, i), chunk(terms.at[t], i), in_sem.at[t, i]).wait()
+        pl.when(i < SUB - ahead)(lambda: load(i + ahead))
         rs = pl.ds(pl.multiple_of(i * rows, rows), rows)
         ov[rs, :] = (terms[0, rs, :] + terms[1, rs, :] + terms[2, rs, :]).astype(BF16)
         _copy(chunk(ov, i), chunk(o_hbm, i), o_sem).start()

time: 483 us -> 482 us (level)
  no operation moved by 1% of the time
where the time goes in v7:
time: 482 us
  Pallas kernels  479 us (99%)
    pallas_call x1, Pallas kernels, _head(): pl.pallas_call(_head_kernel, out_shape=(sd((TOK, HID), BF16), sd((TOK, VO...  319 us
    pallas_call x1, Pallas kernels, _dhead(): pl.pallas_call(_dhead_kernel, in_specs=[hbm, hbm], out_specs=hbm, out_sha...  148 us
    pallas_call x1, Pallas kernels, _final(): pl.pallas_call(_final_kernel, in_specs=[hbm] * 4 + [pl.BlockSpec(memory_s...  11.9 us
  transfers between devices with their start and end apart: 2, of which 0 were waited for; matrix products, arithmetic and copies ran while one was open for 0% of the time, Pallas kernels for 31%

profile of v7, /device:TPU:0, one launch (start us, length us, event | category | flops | bytes accessed | tf_op | source)
XLA Modules:
  0.0 481.8 jit_solution(11886670916436345046)
XLA Ops:
  0.6 319.4 %head.1 = (bf16[4096,4096]{1,0:T(8,128)(2,1)}, bf16[4096,4096]{1,0:T(8,128)(2,1)}, f32[256,4096]{1,0:T(8,128)}, f32[512,4096]{1,0:T(8,128)}, f32[512,4096]{1,0:T...) custom-call(bf16[512,4096]{1,0:T(8,128)(2,1)} %x_hbm.1, ...), custom_call_target="tpu_custom_call" | custom-call | flops 274877906944 | bytes 419430400 | tf_op jit(solution)/shard_map/head/pallas_call | solution.py:622
  320.0 1.6 collective-permute-start
  321.6 0.5 collective-permute-start.1
  322.1 147.5 %dhead.1 = bf16[4096,4096]{1,0:T(8,128)(2,1)} custom-call(bf16[4096,4096]{1,0:T(8,128)(2,1)} %get-tuple-element.19.x_hbm, bf16[4096,4096]{1,0:T(8,128)(2,1)} %get-tuple-element.20.g_hbm), custom_call_target="tpu_custom_call" | custom-call | flops 137438953472 | bytes 209715200 | tf_op jit(solution)/shard_map/dhead/pallas_call | solution.py:766
  469.6 0.0 collective-permute-done.b_hbm
  469.6 0.0 collective-permute-done.1.r_hbm
  469.7 11.9 %final.1 = (bf16[512,4096]{1,0:T(8,128)(2,1)}, f32[1]{0:T(128)}) custom-call(f32[512,4096]{1,0:T(8,128)} %get-tuple-element.12.s_hbm, f32[256,4096]{1,0:T(8,128)} %get-tuple-element.13.a_hbm, f32[256,4096]{1,0:T(8,128)} %collective-permute-done.b_hbm, f32[512,4096]{1,0:T(8,128)} %collective-permute-done.1.r_hbm, f32[8,128]{1,0:T(8,128)} %get-tuple-element.16.l_ref), custom_call_target="tpu_custom_call" | custom-call | flops 6291456 | bytes 29360128 | tf_op jit(solution)/shard_map/final/pallas_call | solution.py:822
Async XLA Ops:
  320.0 149.6 %collective-permute-start = (f32[256,4096]{1,0:T(8,128)}, f32[256,4096]{1,0:T(8,128)}, u32[]{:S(2)}, u32[]{:S(2)}) collective-permute-start(f32[256,4096]{1,0:T(8,128)} %get-tuple-element.14), channel_id=1, source_target_pairs={{0,2},{1,5},{2,0},{3,7},{4,6},{5,1},{6,4},{7,3}} | collective-permute-start | bytes 12582920 | tf_op jit(solution)/shard_map/ppermute | solution.py:853
  321.6 148.0 %collective-permute-start.1 = (f32[512,4096]{1,0:T(8,128)}, f32[512,4096]{1,0:T(8,128)}, u32[]{:S(2)}, u32[]{:S(2)}) collective-permute-start(f32[512,4096]{1,0:T(8,128)} %get-tuple-element.15), channel_id=1, source_target_pairs={{0,4},{1,3},{2,6},{3,1},{4,0},{5,7},{6,2},{7,5}} | collective-permute-start | bytes 25165832 | tf_op jit(solution)/shard_map/ppermute | solution.py:854

commit v8 on v7

--- a/solution.py
+++ b/solution.py
@@ -24,6 +24,8 @@
 TILE = (8, LANE)
 SUB = 16
 FOUR = range(4)
+OTHERS = range(1, 8)
+SEVEN = pl.ds(0, 7)
 LATE = 9
 PIECE = 512
 INV = 1.0 / TOK
@@ -35,6 +37,10 @@
 
 def _rem(a, b):
     return lax.rem(jnp.int32(a), jnp.int32(b))
+
+
+def _loop(count, body):
+    lax.fori_loop(0, count, body, 0)
 
 
 def _copy(src, dst, sem):
@@ -140,11 +146,11 @@
         wcopy(j).start()
 
     barrier = pltpu.get_barrier_semaphore()
-    for d in range(1, 8):
+    for d in OTHERS:
         pl.semaphore_signal(barrier, inc=1, device_id={"tp": _rem(me + d, 8)}, device_id_type=MESH)
     pl.semaphore_wait(barrier, 7)
 
-    for d in range(1, 8):
+    for d in OTHERS:
         _send(lab_hbm, lab_v.at[me], labtx_sem, lab_sem, _rem(me + d, 8)).start()
     _copy(lab_hbm, lab_v.at[me], lab_sem).start()
     for q in FOUR:
@@ -220,29 +226,45 @@
         st_new[2 + part : 3 + part, :] = jnp.sum(jnp.transpose(sl[1, rows, :]) * jnp.exp(m - top), axis=0, keepdims=True)
         st_new[4 + part : 5 + part, :] = jnp.sum(jnp.transpose(tl[1, rows, :]), axis=0, keepdims=True)
 
-    def send_stats(blk):
-        for d in range(1, 8):
-            _send(st_loc.at[blk], st_all.at[blk, me], sttx_sem, st_sem.at[blk], _rem(me + d, 8)).start()
-
-    def keep_stats(blk):
-        st_loc[blk] = st_new[...]
-        st_all[blk, me] = st_new[...]
-
-    def combine(blk):
-        top = st_all[blk, 0, 0:2, :]
-        for d in range(1, 8):
-            top = jnp.maximum(top, st_all[blk, d, 0:2, :])
+    def entry(kind, q):
+        diagonal = _div(kind, 3)
+        return diagonal * (NBLK + q) + (1 - diagonal) * block_id(kind, q)
+
+    def send_stats(kind, q):
+        def start(dev):
+            _send(st_loc.at[block_id(kind, q)], st_all.at[NBLK + q, me], sttx_sem, st_sem.at[q], dev).start()
+
+        for core in PAIR:
+            dev = 2 * chip_of(3 - kind) + core
+            pl.when(dev != me)(functools.partial(start, dev))
+
+    def send_late():
+        for d in OTHERS:
+            _send(st_loc, st_all.at[pl.ds(0, NBLK), me], sttx_sem, st_sem.at[4], _rem(me + d, 8)).start()
+
+    def keep_stats(kind, q):
+        st_loc[block_id(kind, q)] = st_new[...]
+        st_all[block_id(kind, q), me] = st_new[...]
+        st_all[entry(kind, q), me] = st_new[...]
+
+    def combine(place):
+        top = st_all[place, 0, 0:2, :]
+        for d in OTHERS:
+            top = jnp.maximum(top, st_all[place, d, 0:2, :])
         s = jnp.zeros((2, LANE), F32)
         t = jnp.zeros((2, LANE), F32)
         for d in range(8):
-            s = s + st_all[blk, d, 2:4, :] * jnp.exp(st_all[blk, d, 0:2, :] - top)
-            t = t + st_all[blk, d, 4:6, :]
+            s = s + st_all[place, d, 2:4, :] * jnp.exp(st_all[place, d, 0:2, :] - top)
+            t = t + st_all[place, d, 4:6, :]
         comb[0:2, :] = top
         comb[2:4, :] = INV / s
         return top + jnp.log(s) - t
 
-    def stats_arrived(blk):
-        _copy(st_all.at[blk, pl.ds(0, 7)], st_all.at[blk, pl.ds(0, 7)], st_sem.at[blk]).wait()
+    def stats_arrived(q):
+        _copy(st_all.at[0, SEVEN], st_all.at[0, SEVEN], st_sem.at[q]).wait()
+
+    def late_arrived():
+        _copy(st_all.at[pl.ds(0, 14)], st_all.at[pl.ds(0, 14)], st_sem.at[4]).wait()
 
     def columns(blk, par, part):
         rows = pl.ds(part * LANE, LANE)
@@ -311,12 +333,6 @@
             wait_rows(kind, q, oc)
             part_load(i, oc).start()
 
-        _copy(xg.at[slot], xg.at[slot], xl_sem.at[slot]).wait()
-
-        @pl.when(i < 4)
-        def _():
-            own_store(i).start()
-
         @pl.when(i > 0)
         def _():
             zcopy(i - 1, 1).start()
@@ -324,7 +340,7 @@
 
         @pl.when(i > 1)
         def _():
-            keep_stats(block_id(kprev, qprev))
+            keep_stats(kprev, qprev)
 
         @pl.when(i == NBLK - 2)
         def _():
@@ -333,8 +349,8 @@
 
         @pl.when(i == NBLK - 1)
         def _():
-            stats_arrived(first_blk)
-            loss_acc[...] = combine(first_blk)
+            stats_arrived(0)
+            loss_acc[...] = combine(entry(first_kind, first_q))
             for part in PAIR:
                 columns(first_blk, 0, part)
             for n in PAIR:
@@ -345,13 +361,19 @@
                         gradient(pbuf, n, 0, r * SUB, j)
                     return carry
 
-                lax.fori_loop(0, SUB, some, 0)
+                _loop(SUB, some)
 
             gstore(0, 0).start()
 
         @pl.when((i >= 3) & (i != LATE) & (i < NBLK - 2))
         def _():
             take_rows(kn, qn)
+
+        _copy(xg.at[slot], xg.at[slot], xl_sem.at[slot]).wait()
+
+        @pl.when(i < 4)
+        def _():
+            own_store(i).start()
 
         jobs = [[] for _ in range(32)]
         for r in range(32):
@@ -373,7 +395,7 @@
 
         @pl.when(i > 1)
         def _():
-            send_stats(block_id(kprev, qprev))
+            send_stats(kprev, qprev)
 
         @pl.when((i == LATE) | (i == NBLK - 2))
         def _():
@@ -399,28 +421,27 @@
         logits(i, 1, jobs)
         return carry
 
-    lax.fori_loop(0, NBLK, phase1, 0)
+    _loop(NBLK, phase1)
     last = NBLK - 1
     klast, qlast = order1(jnp.int32(last))
     kprev, qprev = order1(jnp.int32(last - 1))
-    bprev, blast = block_id(kprev, qprev), block_id(klast, qlast)
     zcopy(last, 1).start()
     zcopy(last, 0).wait()
     zload(1, zb, 0).start()
-    keep_stats(bprev)
+    keep_stats(kprev, qprev)
     for r in range(32):
         lane_stats(la, 1, r * 8)
-    send_stats(bprev)
+    send_stats(kprev, qprev)
     for part in PAIR:
         row_stats(part)
-    keep_stats(blast)
+    keep_stats(klast, qlast)
     zcopy(last, 1).wait()
     zload(1, zb, 1).start()
-    send_stats(blast)
+    send_stats(klast, qlast)
     second_kind, second_q = order2(jnp.int32(1))
     second_blk = block_id(second_kind, second_q)
-    stats_arrived(second_blk)
-    loss_acc[...] += combine(second_blk)
+    stats_arrived(1)
+    loss_acc[...] += combine(entry(second_kind, second_q))
     for part in PAIR:
         columns(second_blk, 1, part)
 
@@ -482,8 +503,8 @@
     def rwait(k, n):
         _copy(rbuf.at[_rem(k + 2, 2), n], rbuf.at[_rem(k + 2, 2), n], rr.at[_rem(k + 2, 2) * 2 + n]).wait()
 
-    def loss_part(k, blk):
-        loss_acc[...] += jnp.where(k < NBLK - 2, combine(blk), 0.0)
+    def loss_part(k, place):
+        loss_acc[...] += jnp.where(k < NBLK - 2, combine(place), 0.0)
 
     def sub(k, cur):
         nxt = 1 - cur
@@ -504,9 +525,13 @@
 
             if n == 0:
 
-                @pl.when(k < NBLK - 2)
+                @pl.when(k < 2)
                 def _():
-                    stats_arrived(blk2)
+                    stats_arrived(k + 2)
+
+                @pl.when(k == 2)
+                def _():
+                    late_arrived()
 
             @pl.when(k >= 12)
             def _():
@@ -524,7 +549,7 @@
             for r, job in enumerate(gradient_jobs(zb, n, nxt)):
                 jobs[2 + r * 9 // 20].append(job)
             if n == 0:
-                jobs[8].append(lambda: loss_part(k, blk2))
+                jobs[8].append(lambda: loss_part(k, entry(kind2, q2)))
             else:
                 for part in PAIR:
                     jobs[8 + 8 * part].append(functools.partial(columns, blk2, cur, part))
@@ -542,6 +567,9 @@
 
             spair(k, n).start()
 
+            if cur == n == 0:
+                pl.when(k == 0)(send_late)
+
             @pl.when(k < NBLK - 2)
             def _():
                 zload(k + 2, zb, n).start()
@@ -580,7 +608,7 @@
         sub(2 * p + 1, 1)
         return carry
 
-    lax.fori_loop(0, NBLK // 2, pair, 0)
+    _loop(NBLK // 2, pair)
 
     kl = jnp.int32(NBLK - 1)
     for n in PAIR:
@@ -607,6 +635,8 @@
     for d in range(7):
         _copy(lab_v.at[d], lab_v.at[d], labtx_sem).wait()
         _copy(st_loc, st_loc, sttx_sem).wait()
+    for d in FOUR:
+        _copy(st_all.at[d, SEVEN], st_all.at[d, SEVEN], sttx_sem).wait()
 
 
 def xrows_at(xall, dev, q):
@@ -654,7 +684,7 @@
             vmem((BLK, LANE), I32),
             vmem(TILE, F32),
             vmem((NBLK,) + TILE, F32),
-            vmem((NBLK, 8) + TILE, F32),
+            vmem((NBLK + 4, 8) + TILE, F32),
             vmem((2, BLK, LANE), F32),
             vmem((2, BLK, LANE), F32),
             vmem((2, BLK, LANE), F32),
@@ -672,7 +702,7 @@
             dma(TWO),
             dma(TWO),
             dma(TWO),
-            dma((NBLK,)),
+            dma((5,)),
             dma(()),
             dma(TWO),
             dma((4,)),
@@ -733,7 +763,7 @@
 
         return carry
 
-    lax.fori_loop(0, 8, first, 0)
+    _loop(8, first)
     ostore(0, 1).start()
 
     def block(b, carry):
@@ -800,7 +830,7 @@
         load(i)
         return carry
 
-    lax.fori_loop(0, ahead, first, 0)
+    _loop(ahead, first)
     loss_ref[0] = l_ref[0, 0]
 
     def add(i, carry):
@@ -812,7 +842,7 @@
         _copy(chunk(ov, i), chunk(o_hbm, i), o_sem).start()
         return carry
 
-    lax.fori_loop(0, SUB, add, 0)
+    _loop(SUB, add)
     _copy(ov, o_hbm, o_sem).wait()
 
 

time: 482 us -> 481 us (level)
  no operation moved by 1% of the time
where the time goes in v8:
time: 481 us
  Pallas kernels  477 us (99%)
    pallas_call x1, Pallas kernels, _head(): pl.pallas_call(_head_kernel, out_shape=(sd((TOK, HID), BF16), sd((TOK, VO...  318 us
    pallas_call x1, Pallas kernels, _dhead(): pl.pallas_call(_dhead_kernel, in_specs=[hbm, hbm], out_specs=hbm, out_sha...  148 us
    pallas_call x1, Pallas kernels, _final(): pl.pallas_call(_final_kernel, in_specs=[hbm] * 4 + [pl.BlockSpec(memory_s...  11.9 us
  transfers between devices with their start and end apart: 2, of which 0 were waited for; matrix products, arithmetic and copies ran while one was open for 0% of the time, Pallas kernels for 31%

profile of v8, /device:TPU:0, one launch (start us, length us, event | category | flops | bytes accessed | tf_op | source)
XLA Modules:
  0.0 481.1 jit_solution(9148754644822486236)
XLA Ops:
  0.6 317.8 %head.1 = (bf16[4096,4096]{1,0:T(8,128)(2,1)}, bf16[4096,4096]{1,0:T(8,128)(2,1)}, f32[256,4096]{1,0:T(8,128)}, f32[512,4096]{1,0:T(8,128)}, f32[512,4096]{1,0:T...) custom-call(bf16[512,4096]{1,0:T(8,128)(2,1)} %x_hbm.1, ...), custom_call_target="tpu_custom_call" | custom-call | flops 274877906944 | bytes 419430400 | tf_op jit(solution)/shard_map/head/pallas_call | solution.py:652
  318.4 1.7 collective-permute-start
  320.1 1.3 collective-permute-start.1
  321.4 147.5 %dhead.1 = bf16[4096,4096]{1,0:T(8,128)(2,1)} custom-call(bf16[4096,4096]{1,0:T(8,128)(2,1)} %get-tuple-element.19.x_hbm, bf16[4096,4096]{1,0:T(8,128)(2,1)} %get-tuple-element.20.g_hbm), custom_call_target="tpu_custom_call" | custom-call | flops 137438953472 | bytes 209715200 | tf_op jit(solution)/shard_map/dhead/pallas_call | solution.py:796
  468.9 0.0 collective-permute-done.b_hbm
  469.0 0.0 collective-permute-done.1.r_hbm
  469.0 11.9 %final.1 = (bf16[512,4096]{1,0:T(8,128)(2,1)}, f32[1]{0:T(128)}) custom-call(f32[512,4096]{1,0:T(8,128)} %get-tuple-element.12.s_hbm, f32[256,4096]{1,0:T(8,128)} %get-tuple-element.13.a_hbm, f32[256,4096]{1,0:T(8,128)} %collective-permute-done.b_hbm, f32[512,4096]{1,0:T(8,128)} %collective-permute-done.1.r_hbm, f32[8,128]{1,0:T(8,128)} %get-tuple-element.16.l_ref), custom_call_target="tpu_custom_call" | custom-call | flops 6291456 | bytes 29360128 | tf_op jit(solution)/shard_map/final/pallas_call | solution.py:852
Async XLA Ops:
  318.4 150.5 %collective-permute-start = (f32[256,4096]{1,0:T(8,128)}, f32[256,4096]{1,0:T(8,128)}, u32[]{:S(2)}, u32[]{:S(2)}) collective-permute-start(f32[256,4096]{1,0:T(8,128)} %get-tuple-element.14), channel_id=1, source_target_pairs={{0,2},{1,5},{2,0},{3,7},{4,6},{5,1},{6,4},{7,3}} | collective-permute-start | bytes 12582920 | tf_op jit(solution)/shard_map/ppermute | solution.py:883
  320.1 148.8 %collective-permute-start.1 = (f32[512,4096]{1,0:T(8,128)}, f32[512,4096]{1,0:T(8,128)}, u32[]{:S(2)}, u32[]{:S(2)}) collective-permute-start(f32[512,4096]{1,0:T(8,128)} %get-tuple-element.15), channel_id=1, source_target_pairs={{0,4},{1,3},{2,6},{3,1},{4,0},{5,7},{6,2},{7,5}} | collective-permute-start | bytes 25165832 | tf_op jit(solution)/shard_map/ppermute | solution.py:884

commit v9 on v8

--- a/solution.py
+++ b/solution.py
@@ -39,6 +39,10 @@
     return lax.rem(jnp.int32(a), jnp.int32(b))
 
 
+def _odd(a):
+    return _rem(a, 2)
+
+
 def _loop(count, body):
     lax.fori_loop(0, count, body, 0)
 
@@ -97,8 +101,8 @@
 ):
     me = lax.axis_index("tp")
     chip = _div(me, 2)
-    c = _rem(me, 2)
-    x = _rem(chip, 2)
+    c = _odd(me)
+    x = _odd(chip)
     y = _div(chip, 2)
     oc = 1 - c
     partner = me + 1 - 2 * c
@@ -108,12 +112,12 @@
     n1kind = 1 + c
 
     def chip_of(kind):
-        return chip + _rem(kind, 2) * (1 - 2 * x) + _div(kind, 2) * (2 - 4 * y)
+        return chip + _odd(kind) * (1 - 2 * x) + _div(kind, 2) * (2 - 4 * y)
 
     def order(i, first, last):
         a = _div(i, 4)
         mid, end = _rem(_div(a + 1, 2), 2), _div(a, 3)
-        kind = mid * (1 + _rem(i, 2)) + first * (1 - mid) * (1 - end) + last * end
+        kind = mid * (1 + _odd(i)) + first * (1 - mid) * (1 - end) + last * end
         return kind, mid * _div(i - 4, 2) + (1 - mid) * _rem(i, 4)
 
     def order1(i):
@@ -161,7 +165,7 @@
 
     def load_x(b):
         kind, q = order1(b)
-        slot = _rem(b, 2)
+        slot = _odd(b)
 
         @pl.when(kind == 0)
         def _():
@@ -185,14 +189,14 @@
 
     def part_load(b, part):
         kind, q = order1(b)
-        return _copy(xrows(kind, q, part), xg.at[_rem(b, 2), pl.ds(pl.multiple_of(part * LANE, LANE), LANE)], xl_sem.at[_rem(b, 2)])
+        return _copy(xrows(kind, q, part), xg.at[_odd(b), pl.ds(pl.multiple_of(part * LANE, LANE), LANE)], xl_sem.at[_odd(b)])
 
     def zcopy(b, h):
         kind, q = order1(b)
         return _copy(zb.at[h], zst.at[block_id(kind, q), h], zo_sem.at[h])
 
     def own_store(b):
-        slot = _rem(b, 2)
+        slot = _odd(b)
         return _copy(xg.at[slot, pl.ds(pl.multiple_of(c * LANE, LANE), LANE)], xrows(0, _rem(b, 4), c), xs_sem.at[slot])
 
     def label_column(blk, part):
@@ -296,7 +300,7 @@
     first_blk = block_id(first_kind, first_q)
 
     def logits(b, h, jobs):
-        slot = _rem(b, 2)
+        slot = _odd(b)
         def put(nt, z):
             zb[h, :, nt * PIECE : (nt + 1) * PIECE] = z
             m = z[:, :LANE]
@@ -323,7 +327,7 @@
         wcopy(j).start()
 
     def phase1(i, carry):
-        slot = _rem(i, 2)
+        slot = _odd(i)
         kind, q = order1(i)
         kprev, qprev = order1(_rem(i + NBLK - 2, NBLK))
         kn, qn = order1(_rem(i + 1, NBLK))
@@ -450,7 +454,7 @@
 
     def spair(k, n):
         return _send(
-            pbuf.at[n, pl.ds(pl.multiple_of(oc * LANE, LANE), LANE)], rbuf.at[_rem(k + 2, 2), n], ps.at[n], rr.at[_rem(k + 2, 2) * 2 + n], partner
+            pbuf.at[n, pl.ds(pl.multiple_of(oc * LANE, LANE), LANE)], rbuf.at[_odd(k + 2), n], ps.at[n], rr.at[_odd(k + 2) * 2 + n], partner
         )
 
     def sstore_start(k, n):
@@ -463,11 +467,11 @@
 
         @pl.when((kind == n1kind) & (q < 2))
         def _():
-            _copy(sbuf.at[n], tile(s_n1a, _rem(q, 2), n), sem).start()
+            _copy(sbuf.at[n], tile(s_n1a, _odd(q), n), sem).start()
 
         @pl.when((kind == n1kind) & (q >= 2))
         def _():
-            _copy(sbuf.at[n], tile(s_n1b, _rem(q, 2), n), sem).start()
+            _copy(sbuf.at[n], tile(s_n1b, _odd(q), n), sem).start()
 
         @pl.when(kind == 3 - n1kind)
         def _():
@@ -487,7 +491,7 @@
 
         @pl.when((kind == n1kind) & (q < 2))
         def _():
-            _send(tile(s_n1a, _rem(q, 2), n), tile(r1a, _rem(q, 2), n), s1tx, r1as.at[_rem(q, 2) * 2 + n], n1).start()
+            _send(tile(s_n1a, _odd(q), n), tile(r1a, _odd(q), n), s1tx, r1as.at[_odd(q) * 2 + n], n1).start()
 
     def stage2_load(q, n):
         _copy(tile(r1n2, q, n), tile(r1n2, q, n), r1s.at[q * 2 + n]).wait()
@@ -495,13 +499,13 @@
         _copy(tile(r1n2, q, n), bb.at[n], ab_sem.at[n * 2 + 1]).start()
 
     def pair_sum(k, n, r):
-        sbuf[n, pl.ds(r, SUB), :] = pbuf[n, pl.ds(pl.multiple_of(c * LANE + r, SUB), SUB), :] + rbuf[_rem(k + 2, 2), n, pl.ds(r, SUB), :]
+        sbuf[n, pl.ds(r, SUB), :] = pbuf[n, pl.ds(pl.multiple_of(c * LANE + r, SUB), SUB), :] + rbuf[_odd(k + 2), n, pl.ds(r, SUB), :]
 
     def stage2_sum(n, r):
         cb[n, pl.ds(r, SUB), :] = ab[n, pl.ds(r, SUB), :] + bb[n, pl.ds(r, SUB), :]
 
     def rwait(k, n):
-        _copy(rbuf.at[_rem(k + 2, 2), n], rbuf.at[_rem(k + 2, 2), n], rr.at[_rem(k + 2, 2) * 2 + n]).wait()
+        _copy(rbuf.at[_odd(k + 2), n], rbuf.at[_odd(k + 2), n], rr.at[_odd(k + 2) * 2 + n]).wait()
 
     def loss_part(k, place):
         loss_acc[...] += jnp.where(k < NBLK - 2, combine(place), 0.0)
@@ -721,22 +725,35 @@
     )(hid, lab, w)
 
 
-def _dhead_kernel(x_hbm, g_hbm, o_hbm, gv, xb, ob, x_sem, g_sem, o_sem):
-    rows = HID // PIECE
+def _cols(j, width=PIECE):
+    return pl.ds(pl.multiple_of(j * width, width), width)
+
+
+def _dhead_kernel(
+    x_hbm, g_hbm, s_hbm, a_hbm, o_hbm, t_hbm, gv, xb, ob, sv, av, x_sem, g_sem, o_sem, s_sem, a_sem, t_sem
+):
+    blocks = HID // PIECE
+    rows = BLK // 4
 
     def xload(b):
-        return _copy(x_hbm.at[:, pl.ds(pl.multiple_of(b * PIECE, PIECE), PIECE)], xb.at[b % 2], x_sem.at[b % 2])
+        return _copy(x_hbm.at[:, _cols(b)], xb.at[_odd(b)], x_sem.at[_odd(b)])
 
     def gload(j):
-        cols = pl.ds(pl.multiple_of(j * PIECE, PIECE), PIECE)
-        return _copy(g_hbm.at[:, cols], gv.at[:, cols], g_sem.at[j])
+        return _copy(g_hbm.at[:, _cols(j)], gv.at[:, _cols(j)], g_sem.at[j])
 
     def ostore(b, n):
-        dst = o_hbm.at[pl.ds(pl.multiple_of(b * PIECE, PIECE), PIECE), pl.ds(pl.multiple_of(n * HALF, HALF), HALF)]
-        return _copy(ob.at[n], dst, o_sem.at[n])
+        return _copy(ob.at[n], o_hbm.at[_cols(b), _cols(n, HALF)], o_sem.at[n])
 
     def dot(lhs, rhs):
         return lax.dot_general(lhs, rhs, (((0,), (0,)), ((), ())), preferred_element_type=F32).astype(BF16)
+
+    def terms(p):
+        slot = _odd(p)
+        src = _cols(p, rows)
+        return _copy(s_hbm.at[src], sv.at[slot], s_sem.at[slot]), _copy(a_hbm.at[src], av.at[slot], a_sem.at[slot])
+
+    def tstore(p):
+        return _copy(sv.at[_odd(p)], t_hbm.at[_cols(p, rows)], t_sem.at[_odd(p)])
 
     xload(0).start()
     gload(0).start()
@@ -746,107 +763,144 @@
     def first(j, carry):
         gload(j).wait()
 
-        @pl.when(j < 6)
-        def _():
-            gload(j + 2).start()
-
-        @pl.when(j == 6)
-        def _():
-            xload(1).start()
-
-        cols = pl.ds(pl.multiple_of(j % 4 * PIECE, PIECE), PIECE)
-        ob[j // 4, :, cols] = dot(xb[0], gv[:, pl.ds(pl.multiple_of(j * PIECE, PIECE), PIECE)])
-
-        @pl.when(j == 3)
-        def _():
-            ostore(0, 0).start()
-
+        @pl.when(j == 0)
+        def _():
+            gload(2).start()
+
+        @pl.when(j > 0)
+        def _():
+            gload(2 * j + 1).start()
+
+        @pl.when((j > 0) & (j < 3))
+        def _():
+            gload(2 * j + 2).start()
+
+        ob[0, :, _cols(j)] = dot(xb[0], gv[:, _cols(j)])
         return carry
 
-    _loop(8, first)
-    ostore(0, 1).start()
+    _loop(4, first)
+    ostore(0, 0).start()
+    xload(1).start()
+    for j in range(4, 8):
+        gload(j).wait()
 
     def block(b, carry):
-        xload(b).wait()
-
-        @pl.when(b < rows - 1)
+        @pl.when(b > 0)
+        def _():
+            xload(b).wait()
+
+        @pl.when((b > 0) & (b < blocks - 1))
         def _():
             xload(b + 1).start()
 
+        @pl.when((b > 1) & (b < 6))
+        def _():
+            for copy in terms(b - 2):
+                copy.wait()
+            sv[_odd(b)] = sv[_odd(b)] + av[_odd(b)]
+            tstore(b - 2).start()
+
+        @pl.when((b > 0) & (b < 5))
+        def _():
+            pl.when(b > 2)(lambda: tstore(b - 3).wait())
+            for copy in terms(b - 1):
+                copy.start()
+
         def half(n, carry):
-            ostore(b - 1, n).wait()
-
-            @pl.when(b < rows)
-            def _():
-                ob[n] = dot(xb[b % 2], gv[:, pl.ds(pl.multiple_of(n * HALF, HALF), HALF)])
+            pl.when(b > 0)(lambda: ostore(b - 1, n).wait())
+
+            @pl.when(b < blocks)
+            def _():
+                ob[n] = dot(xb[_odd(b)], gv[:, _cols(n, HALF)])
 
             ostore(b, n).start()
             return carry
 
-        return lax.fori_loop(0, 2, half, carry)
-
-    lax.fori_loop(1, rows, block, 0)
-    ostore(rows - 1, 0).wait()
-    ostore(rows - 1, 1).wait()
-
-
-def _dhead(xall, gall):
+        return lax.fori_loop(jnp.where(b == 0, 1, 0), 2, half, carry)
+
+    _loop(blocks, block)
+    for n in PAIR:
+        ostore(blocks - 1, n).wait()
+        tstore(n).wait()
+
+
+def _dhead(xall, gall, s_self, r1a):
     hbm = pl.BlockSpec(memory_space=ANY)
     dma = pltpu.SemaphoreType.DMA
     return pl.pallas_call(
         _dhead_kernel,
-        in_specs=[hbm, hbm],
-        out_specs=hbm,
-        out_shape=jax.ShapeDtypeStruct((HID, VOC), BF16),
+        in_specs=[hbm] * 4,
+        out_specs=(hbm, hbm),
+        out_shape=(jax.ShapeDtypeStruct((HID, VOC), BF16), jax.ShapeDtypeStruct((BLK, HID), F32)),
         scratch_shapes=[
             pltpu.VMEM((TOK, VOC), BF16),
             pltpu.VMEM((2, TOK, PIECE), BF16),
             pltpu.VMEM((2, PIECE, HALF), BF16),
+            pltpu.VMEM((2, BLK // 4, HID), F32),
+            pltpu.VMEM((2, BLK // 4, HID), F32),
             dma(TWO),
             dma((8,)),
+            dma(TWO),
+            dma(TWO),
+            dma(TWO),
             dma(TWO),
         ],
         compiler_params=pltpu.CompilerParams(vmem_limit_bytes=60 * MIB),
         cost_estimate=pl.CostEstimate(flops=2 * TOK * HID * VOC, bytes_accessed=200 * MIB, transcendentals=0),
         name="dhead",
-    )(xall, gall)
-
-
-def _final_kernel(s_hbm, a_hbm, b_hbm, r_hbm, l_ref, o_hbm, loss_ref, terms, ov, in_sem, o_sem):
+    )(xall, gall, s_self, r1a)
+
+
+def _final_kernel(t_hbm, s_hbm, b_hbm, r_hbm, l_ref, o_hbm, loss_ref, terms, ov, in_sem, o_sem):
     rows = PIECE // SUB
     ahead = 6
-
-    def chunk(ref, i):
-        return ref.at[pl.ds(pl.multiple_of(i * rows, rows), rows)]
-
-    def load(i):
-        row = _rem(i, SUB // 2)
-        _copy(chunk(s_hbm, i), chunk(terms.at[0], i), in_sem.at[0, i]).start()
-        pl.when(i < SUB // 2)(lambda: _copy(chunk(a_hbm, row), chunk(terms.at[1], i), in_sem.at[1, i]).start())
-        pl.when(i >= SUB // 2)(lambda: _copy(chunk(b_hbm, row), chunk(terms.at[1], i), in_sem.at[1, i]).start())
-        _copy(chunk(r_hbm, i), chunk(terms.at[2], i), in_sem.at[2, i]).start()
-
-    def first(i, carry):
-        load(i)
+    half = SUB // 2
+
+    def load(t, ref, i, dst):
+        return _copy(ref.at[_cols(i, rows)], terms.at[t, _cols(dst, rows)], in_sem.at[t, dst])
+
+    def start(i):
+        @pl.when(i < half)
+        def _():
+            load(0, t_hbm, i, i).start()
+
+        @pl.when(i >= half)
+        def _():
+            load(0, s_hbm, i, i).start()
+            load(1, b_hbm, i - half, i).start()
+
+        load(2, r_hbm, i, i).start()
+
+    def begin(i, carry):
+        start(i)
         return carry
 
-    _loop(ahead, first)
+    _loop(ahead, begin)
     loss_ref[0] = l_ref[0, 0]
 
     def add(i, carry):
-        for t in range(3):
-            _copy(chunk(s_hbm, i), chunk(terms.at[t], i), in_sem.at[t, i]).wait()
-        pl.when(i < SUB - ahead)(lambda: load(i + ahead))
-        rs = pl.ds(pl.multiple_of(i * rows, rows), rows)
-        ov[rs, :] = (terms[0, rs, :] + terms[1, rs, :] + terms[2, rs, :]).astype(BF16)
-        _copy(chunk(ov, i), chunk(o_hbm, i), o_sem).start()
+        rs = _cols(i, rows)
+        load(0, s_hbm, i, i).wait()
+        load(2, r_hbm, i, i).wait()
+        pl.when(i < SUB - ahead)(lambda: start(i + ahead))
+
+        @pl.when(i < half)
+        def _():
+            ov[rs, :] = (terms[0, rs, :] + terms[2, rs, :]).astype(BF16)
+
+        @pl.when(i >= half)
+        def _():
+            load(1, b_hbm, i - half, i).wait()
+            ov[rs, :] = (terms[0, rs, :] + terms[1, rs, :] + terms[2, rs, :]).astype(BF16)
+
+        _copy(ov.at[rs], o_hbm.at[rs], o_sem).start()
         return carry
 
     _loop(SUB, add)
     _copy(ov, o_hbm, o_sem).wait()
 
 
-def _final(s_self, r1a, r1b, r2, loss):
+def _final(t, s_self, r1b, r2, loss):
     hbm = pl.BlockSpec(memory_space=ANY)
     dma = pltpu.SemaphoreType.DMA
     return pl.pallas_call(
@@ -861,9 +915,9 @@
             dma(()),
         ],
         compiler_params=pltpu.CompilerParams(vmem_limit_bytes=62 * MIB),
-        cost_estimate=pl.CostEstimate(flops=3 * PIECE * HID, bytes_accessed=28 * MIB, transcendentals=0),
+        cost_estimate=pl.CostEstimate(flops=3 * PIECE * HID, bytes_accessed=24 * MIB, transcendentals=0),
         name="final",
-    )(s_self, r1a, r1b, r2, loss)
+    )(t, s_self, r1b, r2, loss)
 
 
 def solution(mesh):
@@ -882,8 +936,8 @@
         xall, gall, s_n1b, s_self, y2, r1a, loss = _head(hid, lab.reshape(4, LANE), w)[:7]
         r1b = lax.ppermute(s_n1b, "tp", first)
         r2 = lax.ppermute(y2, "tp", second)
-        d_head = _dhead(xall, gall)
-        d_hidden, mean_loss = _final(s_self, r1a, r1b, r2, loss)
+        d_head, t = _dhead(xall, gall, s_self, r1a)
+        d_hidden, mean_loss = _final(t, s_self, r1b, r2, loss)
         return mean_loss, d_hidden, d_head
 
     return jax.shard_map(

time: 481 us -> 480 us (level)
  no operation moved by 1% of the time
where the time goes in v9:
time: 480 us
  Pallas kernels  476 us (99%)
    pallas_call x1, Pallas kernels, _head(): pl.pallas_call(_head_kernel, out_shape=(sd((TOK, HID), BF16), sd((TOK, VO...  318 us
    pallas_call x1, Pallas kernels, _dhead(): pl.pallas_call(_dhead_kernel, in_specs=[hbm] * 4, out_specs=(hbm, hbm), o...  148 us
    pallas_call x1, Pallas kernels, _final(): pl.pallas_call(_final_kernel, in_specs=[hbm] * 4 + [pl.BlockSpec(memory_s...  10.8 us
  transfers between devices with their start and end apart: 2, of which 0 were waited for; matrix products, arithmetic and copies ran while one was open for 0% of the time, Pallas kernels for 31%

profile of v9, /device:TPU:0, one launch (start us, length us, event | category | flops | bytes accessed | tf_op | source)
XLA Modules:
  0.0 480.2 jit_solution(6697346395220986350)
XLA Ops:
  0.6 317.8 %head.1 = (bf16[4096,4096]{1,0:T(8,128)(2,1)}, bf16[4096,4096]{1,0:T(8,128)(2,1)}, f32[256,4096]{1,0:T(8,128)}, f32[512,4096]{1,0:T(8,128)}, f32[512,4096]{1,0:T...) custom-call(bf16[512,4096]{1,0:T(8,128)(2,1)} %x_hbm.1, ...), custom_call_target="tpu_custom_call" | custom-call | flops 274877906944 | bytes 419430400 | tf_op jit(solution)/shard_map/head/pallas_call | solution.py:656
  318.4 1.7 collective-permute-start
  320.2 1.3 collective-permute-start.1
  321.4 147.8 %dhead.1 = (bf16[4096,4096]{1,0:T(8,128)(2,1)}, f32[256,4096]{1,0:T(8,128)}) custom-call(bf16[4096,4096]{1,0:T(8,128)(2,1)} %get-tuple-element.14.x_hbm, bf16[4096,4096]{1,0:T(8,128)(2,1)} %get-tuple-element.15.g_hbm, f32[512,4096]{1,0:T(8,128)} %get-tuple-element.16.s_hbm, f32[256,4096]{1,0:T(8,128)} %get-tuple-element.17.a_hbm), custom_call_target="tpu_custom_call" | custom-call | flops 137438953472 | bytes 209715200 | tf_op jit(solution)/shard_map/dhead/pallas_call | solution.py:830
  469.2 0.0 collective-permute-done.b_hbm
  469.2 0.0 collective-permute-done.1.r_hbm
  469.2 10.8 %final.1 = (bf16[512,4096]{1,0:T(8,128)(2,1)}, f32[1]{0:T(128)}) custom-call(f32[256,4096]{1,0:T(8,128)} %get-tuple-element.18.t_hbm, f32[512,4096]{1,0:T(8,128)} %get-tuple-element.16.s_hbm, f32[256,4096]{1,0:T(8,128)} %collective-permute-done.b_hbm, f32[512,4096]{1,0:T(8,128)} %collective-permute-done.1.r_hbm, f32[8,128]{1,0:T(8,128)} %get-tuple-element.21.l_ref), custom_call_target="tpu_custom_call" | custom-call | flops 6291456 | bytes 25165824 | tf_op jit(solution)/shard_map/final/pallas_call | solution.py:906
Async XLA Ops:
  318.4 150.8 %collective-permute-start = (f32[256,4096]{1,0:T(8,128)}, f32[256,4096]{1,0:T(8,128)}, u32[]{:S(2)}, u32[]{:S(2)}) collective-permute-start(f32[256,4096]{1,0:T(8,128)} %get-tuple-element.19), channel_id=1, source_target_pairs={{0,2},{1,5},{2,0},{3,7},{4,6},{5,1},{6,4},{7,3}} | collective-permute-start | bytes 12582920 | tf_op jit(solution)/shard_map/ppermute | solution.py:937
  320.2 149.1 %collective-permute-start.1 = (f32[512,4096]{1,0:T(8,128)}, f32[512,4096]{1,0:T(8,128)}, u32[]{:S(2)}, u32[]{:S(2)}) collective-permute-start(f32[512,4096]{1,0:T(8,128)} %get-tuple-element.20), channel_id=1, source_target_pairs={{0,4},{1,3},{2,6},{3,1},{4,0},{5,7},{6,2},{7,5}} | collective-permute-start | bytes 25165832 | tf_op jit(solution)/shard_map/ppermute | solution.py:938

commit v10 on v9

--- a/solution.py
+++ b/solution.py
@@ -23,6 +23,7 @@
 PAIR = (0, 1)
 TILE = (8, LANE)
 SUB = 16
+FIRST_DIMS = (((0,), (0,)), ((), ()))
 FOUR = range(4)
 OTHERS = range(1, 8)
 SEVEN = pl.ds(0, 7)
@@ -730,7 +731,8 @@
 
 
 def _dhead_kernel(
-    x_hbm, g_hbm, s_hbm, a_hbm, o_hbm, t_hbm, gv, xb, ob, sv, av, x_sem, g_sem, o_sem, s_sem, a_sem, t_sem
+    x_hbm, g_hbm, s_hbm, a_hbm, o_hbm, t_hbm,
+    gv, xb, ob, acc, sv, av, x_sem, g_sem, o_sem, s_sem, a_sem, t_sem, f_sem,
 ):
     blocks = HID // PIECE
     rows = BLK // 4
@@ -745,7 +747,7 @@
         return _copy(ob.at[n], o_hbm.at[_cols(b), _cols(n, HALF)], o_sem.at[n])
 
     def dot(lhs, rhs):
-        return lax.dot_general(lhs, rhs, (((0,), (0,)), ((), ())), preferred_element_type=F32).astype(BF16)
+        return lax.dot_general(lhs, rhs, FIRST_DIMS, preferred_element_type=F32).astype(BF16)
 
     def terms(p):
         slot = _odd(p)
@@ -755,30 +757,50 @@
     def tstore(p):
         return _copy(sv.at[_odd(p)], t_hbm.at[_cols(p, rows)], t_sem.at[_odd(p)])
 
-    xload(0).start()
-    gload(0).start()
-    xload(0).wait()
+    def part(h):
+        tokens = pl.ds(h * HALF, HALF)
+        return (
+            _copy(x_hbm.at[tokens, _cols(0)], xb.at[0, tokens], f_sem.at[h, 0]),
+            _copy(g_hbm.at[tokens, _cols(0)], gv.at[tokens, _cols(0)], f_sem.at[h, 1]),
+        )
+
+    def part_dot(h):
+        tokens = slice(h * HALF, (h + 1) * HALF)
+        return lax.dot_general(
+            xb[0, tokens, :], gv[tokens, :PIECE], FIRST_DIMS, preferred_element_type=F32
+        )
+
+    for h in PAIR:
+        for copy in part(h):
+            copy.start()
+    for copy in part(0):
+        copy.wait()
     gload(1).start()
+
+    @pl.when(lax.axis_index("tp") < 8)
+    def _():
+        acc[...] = part_dot(0)
+
+    for copy in part(1):
+        copy.wait()
+    gload(2).start()
+
+    @pl.when(lax.axis_index("tp") < 8)
+    def _():
+        ob[0, :, :PIECE] = (acc[...] + part_dot(1)).astype(BF16)
 
     def first(j, carry):
         gload(j).wait()
-
-        @pl.when(j == 0)
-        def _():
-            gload(2).start()
-
-        @pl.when(j > 0)
-        def _():
-            gload(2 * j + 1).start()
-
-        @pl.when((j > 0) & (j < 3))
+        gload(2 * j + 1).start()
+
+        @pl.when(j < 3)
         def _():
             gload(2 * j + 2).start()
 
         ob[0, :, _cols(j)] = dot(xb[0], gv[:, _cols(j)])
         return carry
 
-    _loop(4, first)
+    lax.fori_loop(1, 4, first, 0)
     ostore(0, 0).start()
     xload(1).start()
     for j in range(4, 8):
@@ -836,6 +858,7 @@
             pltpu.VMEM((TOK, VOC), BF16),
             pltpu.VMEM((2, TOK, PIECE), BF16),
             pltpu.VMEM((2, PIECE, HALF), BF16),
+            pltpu.VMEM((PIECE, PIECE), F32),
             pltpu.VMEM((2, BLK // 4, HID), F32),
             pltpu.VMEM((2, BLK // 4, HID), F32),
             dma(TWO),
@@ -844,6 +867,7 @@
             dma(TWO),
             dma(TWO),
             dma(TWO),
+            dma(TWO + TWO),
         ],
         compiler_params=pltpu.CompilerParams(vmem_limit_bytes=60 * MIB),
         cost_estimate=pl.CostEstimate(flops=2 * TOK * HID * VOC, bytes_accessed=200 * MIB, transcendentals=0),
@@ -934,8 +958,8 @@
 
     def local_step(hid, w, lab):
         xall, gall, s_n1b, s_self, y2, r1a, loss = _head(hid, lab.reshape(4, LANE), w)[:7]
+        r2 = lax.ppermute(y2, "tp", second)
         r1b = lax.ppermute(s_n1b, "tp", first)
-        r2 = lax.ppermute(y2, "tp", second)
         d_head, t = _dhead(xall, gall, s_self, r1a)
         d_hidden, mean_loss = _final(t, s_self, r1b, r2, loss)
         return mean_loss, d_hidden, d_head

time: 480 us -> 480 us (level)
  no operation moved by 1% of the time
where the time goes in v10:
time: 480 us; the launch traced here: 479 us
  Pallas kernels  475 us (99%)
    pallas_call x1, Pallas kernels, _head(): pl.pallas_call(_head_kernel, out_shape=(sd((TOK, HID), BF16), sd((TOK, VO...  318 us
    pallas_call x1, Pallas kernels, _dhead(): pl.pallas_call(_dhead_kernel, in_specs=[hbm] * 4, out_specs=(hbm, hbm), o...  147 us
    pallas_call x1, Pallas kernels, _final(): pl.pallas_call(_final_kernel, in_specs=[hbm] * 4 + [pl.BlockSpec(memory_s...  10.8 us
  transfers between devices with their start and end apart: 2, of which 0 were waited for; matrix products, arithmetic and copies ran while one was open for 0% of the time, Pallas kernels for 31%

profile of v10, /device:TPU:0, one launch (start us, length us, event | category | flops | bytes accessed | tf_op | source)
XLA Modules:
  0.0 479.3 jit_solution(9178972598975719865)
XLA Ops:
  0.6 317.8 %head.1 = (bf16[4096,4096]{1,0:T(8,128)(2,1)}, bf16[4096,4096]{1,0:T(8,128)(2,1)}, f32[256,4096]{1,0:T(8,128)}, f32[512,4096]{1,0:T(8,128)}, f32[512,4096]{1,0:T...) custom-call(bf16[512,4096]{1,0:T(8,128)(2,1)} %x_hbm.1, ...), custom_call_target="tpu_custom_call" | custom-call | flops 274877906944 | bytes 419430400 | tf_op jit(solution)/shard_map/head/pallas_call | solution.py:657
  318.4 1.7 collective-permute-start
  320.2 1.3 collective-permute-start.1
  321.4 146.9 %dhead.1 = (bf16[4096,4096]{1,0:T(8,128)(2,1)}, f32[256,4096]{1,0:T(8,128)}) custom-call(bf16[4096,4096]{1,0:T(8,128)(2,1)} %get-tuple-element.14.x_hbm, bf16[4096,4096]{1,0:T(8,128)(2,1)} %get-tuple-element.15.g_hbm, f32[512,4096]{1,0:T(8,128)} %get-tuple-element.16.s_hbm, f32[256,4096]{1,0:T(8,128)} %get-tuple-element.17.a_hbm), custom_call_target="tpu_custom_call" | custom-call | flops 137438953472 | bytes 209715200 | tf_op jit(solution)/shard_map/dhead/pallas_call | solution.py:852
  468.3 0.0 collective-permute-done.b_hbm
  468.4 0.0 collective-permute-done.1.r_hbm
  468.4 10.8 %final.1 = (bf16[512,4096]{1,0:T(8,128)(2,1)}, f32[1]{0:T(128)}) custom-call(f32[256,4096]{1,0:T(8,128)} %get-tuple-element.18.t_hbm, f32[512,4096]{1,0:T(8,128)} %get-tuple-element.16.s_hbm, f32[256,4096]{1,0:T(8,128)} %collective-permute-done.b_hbm, f32[512,4096]{1,0:T(8,128)} %collective-permute-done.1.r_hbm, f32[8,128]{1,0:T(8,128)} %get-tuple-element.21.l_ref), custom_call_target="tpu_custom_call" | custom-call | flops 6291456 | bytes 25165824 | tf_op jit(solution)/shard_map/final/pallas_call | solution.py:930
Async XLA Ops:
  318.4 149.9 %collective-permute-start = (f32[256,4096]{1,0:T(8,128)}, f32[256,4096]{1,0:T(8,128)}, u32[]{:S(2)}, u32[]{:S(2)}) collective-permute-start(f32[256,4096]{1,0:T(8,128)} %get-tuple-element.19), channel_id=1, source_target_pairs={{0,2},{1,5},{2,0},{3,7},{4,6},{5,1},{6,4},{7,3}} | collective-permute-start | bytes 12582920 | tf_op jit(solution)/shard_map/ppermute | solution.py:962
  320.2 148.2 %collective-permute-start.1 = (f32[512,4096]{1,0:T(8,128)}, f32[512,4096]{1,0:T(8,128)}, u32[]{:S(2)}, u32[]{:S(2)}) collective-permute-start(f32[512,4096]{1,0:T(8,128)} %get-tuple-element.20), channel_id=1, source_target_pairs={{0,4},{1,3},{2,6},{3,1},{4,0},{5,7},{6,2},{7,5}} | collective-permute-start | bytes 25165832 | tf_op jit(solution)/shard_map/ppermute | solution.py:961

commit v11 on v10

--- a/solution.py
+++ b/solution.py
@@ -65,14 +65,15 @@
 def _pieces(lhs, rhs, put, jobs, transposed):
     dims = (((1,), (1,)), ((), ())) if transposed else (((1,), (0,)), ((), ()))
     pieces = HALF // PIECE
-    deep = 8
+    deep = HID // BLK
     for nt in range(pieces):
         acc = None
         for kt in range(deep):
             part = lax.dot_general(lhs(kt), rhs(nt, kt), dims, preferred_element_type=F32)
             acc = part if acc is None else acc + part
-            for job in jobs[nt * deep + kt]:
-                job()
+            if kt % 2:
+                for job in jobs[(nt * deep + kt) // 2]:
+                    job()
         put(nt, acc)
 
 
@@ -312,8 +313,8 @@
             ml[h] = m
 
         _product(
-            lambda kt: xg[slot, :, kt * PIECE : (kt + 1) * PIECE],
-            lambda nt, kt: wv[kt * PIECE : (kt + 1) * PIECE, h * HALF + nt * PIECE : h * HALF + (nt + 1) * PIECE],
+            lambda kt: xg[slot, :, kt * BLK : (kt + 1) * BLK],
+            lambda nt, kt: wv[kt * BLK : (kt + 1) * BLK, h * HALF + nt * PIECE : h * HALF + (nt + 1) * PIECE],
             put,
             jobs,
             False,
@@ -324,8 +325,8 @@
     _copy(lab_v, lab_v, lab_sem).wait()
     for j in FOUR:
         wcopy(j).wait()
-    for j in range(4, 8):
-        wcopy(j).start()
+    for j in FOUR:
+        wcopy(4 + j).start()
 
     def phase1(i, carry):
         slot = _odd(i)
@@ -391,8 +392,8 @@
 
         @pl.when(i == 0)
         def _():
-            for j in range(4, 8):
-                wcopy(j).wait()
+            for j in FOUR:
+                wcopy(4 + j).wait()
 
         @pl.when(i > 0)
         def _():
@@ -563,8 +564,8 @@
                 pbuf[n, :, nt * PIECE : (nt + 1) * PIECE] = acc
 
             _product(
-                lambda kt: gbufs[cur][:, kt * PIECE : (kt + 1) * PIECE],
-                lambda nt, kt: wv[pl.ds(pl.multiple_of(n * HALF + nt * PIECE, PIECE), PIECE), kt * PIECE : (kt + 1) * PIECE],
+                lambda kt: gbufs[cur][:, kt * BLK : (kt + 1) * BLK],
+                lambda nt, kt: wv[pl.ds(pl.multiple_of(n * HALF + nt * PIECE, PIECE), PIECE), kt * BLK : (kt + 1) * BLK],
                 put,
                 jobs,
                 True,
@@ -803,8 +804,8 @@
     lax.fori_loop(1, 4, first, 0)
     ostore(0, 0).start()
     xload(1).start()
-    for j in range(4, 8):
-        gload(j).wait()
+    for j in FOUR:
+        gload(4 + j).wait()
 
     def block(b, carry):
         @pl.when(b > 0)

time: 480 us -> 478 us (level)
  no operation moved by 1% of the time
where the time goes in v11:
time: 478 us; the launch traced here: 477 us
  Pallas kernels  474 us (99%)
    pallas_call x1, Pallas kernels, _head(): pl.pallas_call(_head_kernel, out_shape=(sd((TOK, HID), BF16), sd((TOK, VO...  317 us
    pallas_call x1, Pallas kernels, _dhead(): pl.pallas_call(_dhead_kernel, in_specs=[hbm] * 4, out_specs=(hbm, hbm), o...  147 us
    pallas_call x1, Pallas kernels, _final(): pl.pallas_call(_final_kernel, in_specs=[hbm] * 4 + [pl.BlockSpec(memory_s...  10.8 us
  transfers between devices with their start and end apart: 2, of which 0 were waited for; matrix products, arithmetic and copies ran while one was open for 0% of the time, Pallas kernels for 31%

profile of v11, /device:TPU:0, one launch (start us, length us, event | category | flops | bytes accessed | tf_op | source)
XLA Modules:
  0.0 477.5 jit_solution(12080416711905923544)
XLA Ops:
  0.6 316.8 %head.1 = (bf16[4096,4096]{1,0:T(8,128)(2,1)}, bf16[4096,4096]{1,0:T(8,128)(2,1)}, f32[256,4096]{1,0:T(8,128)}, f32[512,4096]{1,0:T(8,128)}, f32[512,4096]{1,0:T...) custom-call(bf16[512,4096]{1,0:T(8,128)(2,1)} %x_hbm.1, ...), custom_call_target="tpu_custom_call" | custom-call | flops 274877906944 | bytes 419430400 | tf_op jit(solution)/shard_map/head/pallas_call | solution.py:658
  317.4 0.9 collective-permute-start
  318.3 1.3 collective-permute-start.1
  319.6 146.9 %dhead.1 = (bf16[4096,4096]{1,0:T(8,128)(2,1)}, f32[256,4096]{1,0:T(8,128)}) custom-call(bf16[4096,4096]{1,0:T(8,128)(2,1)} %get-tuple-element.14.x_hbm, bf16[4096,4096]{1,0:T(8,128)(2,1)} %get-tuple-element.15.g_hbm, f32[512,4096]{1,0:T(8,128)} %get-tuple-element.16.s_hbm, f32[256,4096]{1,0:T(8,128)} %get-tuple-element.17.a_hbm), custom_call_target="tpu_custom_call" | custom-call | flops 137438953472 | bytes 209715200 | tf_op jit(solution)/shard_map/dhead/pallas_call | solution.py:853
  466.5 0.0 collective-permute-done.b_hbm
  466.5 0.0 collective-permute-done.1.r_hbm
  466.5 10.8 %final.1 = (bf16[512,4096]{1,0:T(8,128)(2,1)}, f32[1]{0:T(128)}) custom-call(f32[256,4096]{1,0:T(8,128)} %get-tuple-element.18.t_hbm, f32[512,4096]{1,0:T(8,128)} %get-tuple-element.16.s_hbm, f32[256,4096]{1,0:T(8,128)} %collective-permute-done.b_hbm, f32[512,4096]{1,0:T(8,128)} %collective-permute-done.1.r_hbm, f32[8,128]{1,0:T(8,128)} %get-tuple-element.21.l_ref), custom_call_target="tpu_custom_call" | custom-call | flops 6291456 | bytes 25165824 | tf_op jit(solution)/shard_map/final/pallas_call | solution.py:931
Async XLA Ops:
  317.4 149.1 %collective-permute-start = (f32[256,4096]{1,0:T(8,128)}, f32[256,4096]{1,0:T(8,128)}, u32[]{:S(2)}, u32[]{:S(2)}) collective-permute-start(f32[256,4096]{1,0:T(8,128)} %get-tuple-element.19), channel_id=1, source_target_pairs={{0,2},{1,5},{2,0},{3,7},{4,6},{5,1},{6,4},{7,3}} | collective-permute-start | bytes 12582920 | tf_op jit(solution)/shard_map/ppermute | solution.py:963
  318.3 148.2 %collective-permute-start.1 = (f32[512,4096]{1,0:T(8,128)}, f32[512,4096]{1,0:T(8,128)}, u32[]{:S(2)}, u32[]{:S(2)}) collective-permute-start(f32[512,4096]{1,0:T(8,128)} %get-tuple-element.20), channel_id=1, source_target_pairs={{0,4},{1,3},{2,6},{3,1},{4,0},{5,7},{6,2},{7,5}} | collective-permute-start | bytes 25165832 | tf_op jit(solution)/shard_map/ppermute | solution.py:962

commit v12 on v11

--- a/solution.py
+++ b/solution.py
@@ -431,25 +431,25 @@
     last = NBLK - 1
     klast, qlast = order1(jnp.int32(last))
     kprev, qprev = order1(jnp.int32(last - 1))
+    keep_stats(kprev, qprev)
     zcopy(last, 1).start()
     zcopy(last, 0).wait()
     zload(1, zb, 0).start()
-    keep_stats(kprev, qprev)
+    send_stats(kprev, qprev)
     for r in range(32):
         lane_stats(la, 1, r * 8)
-    send_stats(kprev, qprev)
     for part in PAIR:
         row_stats(part)
     keep_stats(klast, qlast)
-    zcopy(last, 1).wait()
-    zload(1, zb, 1).start()
-    send_stats(klast, qlast)
     second_kind, second_q = order2(jnp.int32(1))
     second_blk = block_id(second_kind, second_q)
     stats_arrived(1)
     loss_acc[...] += combine(entry(second_kind, second_q))
     for part in PAIR:
         columns(second_blk, 1, part)
+    send_stats(klast, qlast)
+    zcopy(last, 1).wait()
+    zload(1, zb, 1).start()
 
     def tile(ref, q, n):
         return ref.at[pl.ds(pl.multiple_of(q * LANE, LANE), LANE), pl.ds(pl.multiple_of(n * HALF, HALF), HALF)]

time: 478 us -> 478 us (level)
  no operation moved by 1% of the time
where the time goes in v12:
time: 478 us; the launch traced here: 477 us
  Pallas kernels  474 us (99%)
    pallas_call x1, Pallas kernels, _head(): pl.pallas_call(_head_kernel, out_shape=(sd((TOK, HID), BF16), sd((TOK, VO...  317 us
    pallas_call x1, Pallas kernels, _dhead(): pl.pallas_call(_dhead_kernel, in_specs=[hbm] * 4, out_specs=(hbm, hbm), o...  147 us
    pallas_call x1, Pallas kernels, _final(): pl.pallas_call(_final_kernel, in_specs=[hbm] * 4 + [pl.BlockSpec(memory_s...  10.8 us
  transfers between devices with their start and end apart: 2, of which 0 were waited for; matrix products, arithmetic and copies ran while one was open for 0% of the time, Pallas kernels for 31%

profile of v12, /device:TPU:0, one launch (start us, length us, event | category | flops | bytes accessed | tf_op | source)
XLA Modules:
  0.0 477.5 jit_solution(249529707676323002)
XLA Ops:
  0.6 316.8 %head.1 = (bf16[4096,4096]{1,0:T(8,128)(2,1)}, bf16[4096,4096]{1,0:T(8,128)(2,1)}, f32[256,4096]{1,0:T(8,128)}, f32[512,4096]{1,0:T(8,128)}, f32[512,4096]{1,0:T...) custom-call(bf16[512,4096]{1,0:T(8,128)(2,1)} %x_hbm.1, ...), custom_call_target="tpu_custom_call" | custom-call | flops 274877906944 | bytes 419430400 | tf_op jit(solution)/shard_map/head/pallas_call | solution.py:658
  317.4 0.9 collective-permute-start
  318.3 1.3 collective-permute-start.1
  319.6 146.9 %dhead.1 = (bf16[4096,4096]{1,0:T(8,128)(2,1)}, f32[256,4096]{1,0:T(8,128)}) custom-call(bf16[4096,4096]{1,0:T(8,128)(2,1)} %get-tuple-element.14.x_hbm, bf16[4096,4096]{1,0:T(8,128)(2,1)} %get-tuple-element.15.g_hbm, f32[512,4096]{1,0:T(8,128)} %get-tuple-element.16.s_hbm, f32[256,4096]{1,0:T(8,128)} %get-tuple-element.17.a_hbm), custom_call_target="tpu_custom_call" | custom-call | flops 137438953472 | bytes 209715200 | tf_op jit(solution)/shard_map/dhead/pallas_call | solution.py:853
  466.5 0.0 collective-permute-done.b_hbm
  466.5 0.0 collective-permute-done.1.r_hbm
  466.5 10.8 %final.1 = (bf16[512,4096]{1,0:T(8,128)(2,1)}, f32[1]{0:T(128)}) custom-call(f32[256,4096]{1,0:T(8,128)} %get-tuple-element.18.t_hbm, f32[512,4096]{1,0:T(8,128)} %get-tuple-element.16.s_hbm, f32[256,4096]{1,0:T(8,128)} %collective-permute-done.b_hbm, f32[512,4096]{1,0:T(8,128)} %collective-permute-done.1.r_hbm, f32[8,128]{1,0:T(8,128)} %get-tuple-element.21.l_ref), custom_call_target="tpu_custom_call" | custom-call | flops 6291456 | bytes 25165824 | tf_op jit(solution)/shard_map/final/pallas_call | solution.py:931
Async XLA Ops:
  317.4 149.1 %collective-permute-start = (f32[256,4096]{1,0:T(8,128)}, f32[256,4096]{1,0:T(8,128)}, u32[]{:S(2)}, u32[]{:S(2)}) collective-permute-start(f32[256,4096]{1,0:T(8,128)} %get-tuple-element.19), channel_id=1, source_target_pairs={{0,2},{1,5},{2,0},{3,7},{4,6},{5,1},{6,4},{7,3}} | collective-permute-start | bytes 12582920 | tf_op jit(solution)/shard_map/ppermute | solution.py:963
  318.3 148.2 %collective-permute-start.1 = (f32[512,4096]{1,0:T(8,128)}, f32[512,4096]{1,0:T(8,128)}, u32[]{:S(2)}, u32[]{:S(2)}) collective-permute-start(f32[512,4096]{1,0:T(8,128)} %get-tuple-element.20), channel_id=1, source_target_pairs={{0,4},{1,3},{2,6},{3,1},{4,0},{5,7},{6,2},{7,5}} | collective-permute-start | bytes 25165832 | tf_op jit(solution)/shard_map/ppermute | solution.py:962

commit v13 on v12

--- a/solution.py
+++ b/solution.py
@@ -144,12 +144,11 @@
         return rx.at[kind * 8 + q * 2 + part]
 
     def wcopy(j):
-        cols = pl.ds(j * PIECE, PIECE)
+        cols = pl.ds(j * HALF, HALF)
         return _copy(w_hbm.at[:, cols], wv.at[:, cols], w_sem.at[j])
 
     _copy(own(0), xg.at[0, pl.ds(pl.multiple_of(c * LANE, LANE), LANE)], xl_sem.at[0]).start()
-    for j in FOUR:
-        wcopy(j).start()
+    wcopy(0).start()
 
     barrier = pltpu.get_barrier_semaphore()
     for d in OTHERS:
@@ -323,10 +322,8 @@
     wait_rows(0, 0, oc)
     _copy(xrows(0, 0, oc), xg.at[0, pl.ds(pl.multiple_of(oc * LANE, LANE), LANE)], xl_sem.at[0]).start()
     _copy(lab_v, lab_v, lab_sem).wait()
-    for j in FOUR:
-        wcopy(j).wait()
-    for j in FOUR:
-        wcopy(4 + j).start()
+    wcopy(0).wait()
+    wcopy(1).start()
 
     def phase1(i, carry):
         slot = _odd(i)
@@ -392,8 +389,7 @@
 
         @pl.when(i == 0)
         def _():
-            for j in FOUR:
-                wcopy(4 + j).wait()
+            wcopy(1).wait()
 
         @pl.when(i > 0)
         def _():
@@ -700,7 +696,7 @@
             vmem((2, BLK, LANE), F32),
             vmem((2, BLK, LANE), F32),
             vmem((2, LANE), F32),
-            dma((8,)),
+            dma(TWO),
             dma(()),
             dma(()),
             dma((32,)),

time: 478 us -> 477 us (level)
  no operation moved by 1% of the time
where the time goes in v13:
time: 477 us
  Pallas kernels  474 us (99%)
    pallas_call x1, Pallas kernels, _head(): pl.pallas_call(_head_kernel, out_shape=(sd((TOK, HID), BF16), sd((TOK, VO...  317 us
    pallas_call x1, Pallas kernels, _dhead(): pl.pallas_call(_dhead_kernel, in_specs=[hbm] * 4, out_specs=(hbm, hbm), o...  147 us
    pallas_call x1, Pallas kernels, _final(): pl.pallas_call(_final_kernel, in_specs=[hbm] * 4 + [pl.BlockSpec(memory_s...  10.8 us
  transfers between devices with their start and end apart: 2, of which 0 were waited for; matrix products, arithmetic and copies ran while one was open for 0% of the time, Pallas kernels for 31%

profile of v13, /device:TPU:0, one launch (start us, length us, event | category | flops | bytes accessed | tf_op | source)
XLA Modules:
  0.0 477.2 jit_solution(4535377193959686760)
XLA Ops:
  0.6 316.6 %head.1 = (bf16[4096,4096]{1,0:T(8,128)(2,1)}, bf16[4096,4096]{1,0:T(8,128)(2,1)}, f32[256,4096]{1,0:T(8,128)}, f32[512,4096]{1,0:T(8,128)}, f32[512,4096]{1,0:T...) custom-call(bf16[512,4096]{1,0:T(8,128)(2,1)} %x_hbm.1, ...), custom_call_target="tpu_custom_call" | custom-call | flops 274877906944 | bytes 419430400 | tf_op jit(solution)/shard_map/head/pallas_call | solution.py:654
  317.2 0.9 collective-permute-start
  318.1 1.2 collective-permute-start.1
  319.3 146.9 %dhead.1 = (bf16[4096,4096]{1,0:T(8,128)(2,1)}, f32[256,4096]{1,0:T(8,128)}) custom-call(bf16[4096,4096]{1,0:T(8,128)(2,1)} %get-tuple-element.14.x_hbm, bf16[4096,4096]{1,0:T(8,128)(2,1)} %get-tuple-element.15.g_hbm, f32[512,4096]{1,0:T(8,128)} %get-tuple-element.16.s_hbm, f32[256,4096]{1,0:T(8,128)} %get-tuple-element.17.a_hbm), custom_call_target="tpu_custom_call" | custom-call | flops 137438953472 | bytes 209715200 | tf_op jit(solution)/shard_map/dhead/pallas_call | solution.py:849
  466.2 0.0 collective-permute-done.b_hbm
  466.2 0.0 collective-permute-done.1.r_hbm
  466.2 10.8 %final.1 = (bf16[512,4096]{1,0:T(8,128)(2,1)}, f32[1]{0:T(128)}) custom-call(f32[256,4096]{1,0:T(8,128)} %get-tuple-element.18.t_hbm, f32[512,4096]{1,0:T(8,128)} %get-tuple-element.16.s_hbm, f32[256,4096]{1,0:T(8,128)} %collective-permute-done.b_hbm, f32[512,4096]{1,0:T(8,128)} %collective-permute-done.1.r_hbm, f32[8,128]{1,0:T(8,128)} %get-tuple-element.21.l_ref), custom_call_target="tpu_custom_call" | custom-call | flops 6291456 | bytes 25165824 | tf_op jit(solution)/shard_map/final/pallas_call | solution.py:927
Async XLA Ops:
  317.2 149.0 %collective-permute-start = (f32[256,4096]{1,0:T(8,128)}, f32[256,4096]{1,0:T(8,128)}, u32[]{:S(2)}, u32[]{:S(2)}) collective-permute-start(f32[256,4096]{1,0:T(8,128)} %get-tuple-element.19), channel_id=1, source_target_pairs={{0,2},{1,5},{2,0},{3,7},{4,6},{5,1},{6,4},{7,3}} | collective-permute-start | bytes 12582920 | tf_op jit(solution)/shard_map/ppermute | solution.py:959
  318.1 148.1 %collective-permute-start.1 = (f32[512,4096]{1,0:T(8,128)}, f32[512,4096]{1,0:T(8,128)}, u32[]{:S(2)}, u32[]{:S(2)}) collective-permute-start(f32[512,4096]{1,0:T(8,128)} %get-tuple-element.20), channel_id=1, source_target_pairs={{0,4},{1,3},{2,6},{3,1},{4,0},{5,7},{6,2},{7,5}} | collective-permute-start | bytes 25165832 | tf_op jit(solution)/shard_map/ppermute | solution.py:958

commit v14 on v13

--- a/solution.py
+++ b/solution.py
@@ -874,7 +874,7 @@
 
 def _final_kernel(t_hbm, s_hbm, b_hbm, r_hbm, l_ref, o_hbm, loss_ref, terms, ov, in_sem, o_sem):
     rows = PIECE // SUB
-    ahead = 6
+    ahead = 10
     half = SUB // 2
 
     def load(t, ref, i, dst):

time: 477 us -> 477 us (level)
  no operation moved by 1% of the time
where the time goes in v14:
time: 477 us
  Pallas kernels  474 us (99%)
    pallas_call x1, Pallas kernels, _head(): pl.pallas_call(_head_kernel, out_shape=(sd((TOK, HID), BF16), sd((TOK, VO...  317 us
    pallas_call x1, Pallas kernels, _dhead(): pl.pallas_call(_dhead_kernel, in_specs=[hbm] * 4, out_specs=(hbm, hbm), o...  147 us
    pallas_call x1, Pallas kernels, _final(): pl.pallas_call(_final_kernel, in_specs=[hbm] * 4 + [pl.BlockSpec(memory_s...  10.8 us
  transfers between devices with their start and end apart: 2, of which 0 were waited for; matrix products, arithmetic and copies ran while one was open for 0% of the time, Pallas kernels for 31%

profile of v14, /device:TPU:0, one launch (start us, length us, event | category | flops | bytes accessed | tf_op | source)
XLA Modules:
  0.0 477.1 jit_solution(516654007657697339)
XLA Ops:
  0.6 316.6 %head.1 = (bf16[4096,4096]{1,0:T(8,128)(2,1)}, bf16[4096,4096]{1,0:T(8,128)(2,1)}, f32[256,4096]{1,0:T(8,128)}, f32[512,4096]{1,0:T(8,128)}, f32[512,4096]{1,0:T...) custom-call(bf16[512,4096]{1,0:T(8,128)(2,1)} %x_hbm.1, ...), custom_call_target="tpu_custom_call" | custom-call | flops 274877906944 | bytes 419430400 | tf_op jit(solution)/shard_map/head/pallas_call | solution.py:654
  317.2 0.9 collective-permute-start
  318.1 1.2 collective-permute-start.1
  319.3 146.9 %dhead.1 = (bf16[4096,4096]{1,0:T(8,128)(2,1)}, f32[256,4096]{1,0:T(8,128)}) custom-call(bf16[4096,4096]{1,0:T(8,128)(2,1)} %get-tuple-element.14.x_hbm, bf16[4096,4096]{1,0:T(8,128)(2,1)} %get-tuple-element.15.g_hbm, f32[512,4096]{1,0:T(8,128)} %get-tuple-element.16.s_hbm, f32[256,4096]{1,0:T(8,128)} %get-tuple-element.17.a_hbm), custom_call_target="tpu_custom_call" | custom-call | flops 137438953472 | bytes 209715200 | tf_op jit(solution)/shard_map/dhead/pallas_call | solution.py:849
  466.2 0.0 collective-permute-done.b_hbm
  466.2 0.0 collective-permute-done.1.r_hbm
  466.2 10.8 %final.1 = (bf16[512,4096]{1,0:T(8,128)(2,1)}, f32[1]{0:T(128)}) custom-call(f32[256,4096]{1,0:T(8,128)} %get-tuple-element.18.t_hbm, f32[512,4096]{1,0:T(8,128)} %get-tuple-element.16.s_hbm, f32[256,4096]{1,0:T(8,128)} %collective-permute-done.b_hbm, f32[512,4096]{1,0:T(8,128)} %collective-permute-done.1.r_hbm, f32[8,128]{1,0:T(8,128)} %get-tuple-element.21.l_ref), custom_call_target="tpu_custom_call" | custom-call | flops 6291456 | bytes 25165824 | tf_op jit(solution)/shard_map/final/pallas_call | solution.py:927
Async XLA Ops:
  317.2 149.0 %collective-permute-start = (f32[256,4096]{1,0:T(8,128)}, f32[256,4096]{1,0:T(8,128)}, u32[]{:S(2)}, u32[]{:S(2)}) collective-permute-start(f32[256,4096]{1,0:T(8,128)} %get-tuple-element.19), channel_id=1, source_target_pairs={{0,2},{1,5},{2,0},{3,7},{4,6},{5,1},{6,4},{7,3}} | collective-permute-start | bytes 12582920 | tf_op jit(solution)/shard_map/ppermute | solution.py:959
  318.1 148.1 %collective-permute-start.1 = (f32[512,4096]{1,0:T(8,128)}, f32[512,4096]{1,0:T(8,128)}, u32[]{:S(2)}, u32[]{:S(2)}) collective-permute-start(f32[512,4096]{1,0:T(8,128)} %get-tuple-element.20), channel_id=1, source_target_pairs={{0,4},{1,3},{2,6},{3,1},{4,0},{5,7},{6,2},{7,5}} | collective-permute-start | bytes 25165832 | tf_op jit(solution)/shard_map/ppermute | solution.py:958
